TPU v7x, 32 devices: a whole 2x2x4 slice. The times are simulated.
32 devices in a mesh: seq: 8 (over z, core), batch: 4 (over y, x).
Axes of the slice: x: 2, y: 2, z: 4, core: 2. Of those that a mesh axis runs over, the one named last changes fastest.
Arguments:
- hidden_in: bfloat16 [4, 1024, 1024], P('batch', 'seq'), may hold values from -6 to 6
- cotangent: bfloat16 [4, 1024, 1024], P('batch', 'seq'), may hold values from -6 to 6
- lengths: int32 [4], P('batch'), may hold values from 1 to 1024, as said below
- mixer_gain: bfloat16 [1024], P(('seq', 'batch')), may hold values from 0.099609375 to 1.8984375
- query_weight: bfloat16 [1024, 1024], P(('seq', 'batch')), may hold values from -0.1875 to 0.1875
- key_weight: bfloat16 [1024, 2048], P(('seq', 'batch')), may hold values from -0.1875 to 0.1875
- value_weight: bfloat16 [1024, 2048], P(('seq', 'batch')), may hold values from -0.1875 to 0.1875
- beta_weight: bfloat16 [1024, 16], P(('seq', 'batch')), may hold values from -0.1875 to 0.1875
- alpha_weight: bfloat16 [1024, 8], P(('seq', 'batch')), may hold values from -0.1875 to 0.1875
- gate_weight: bfloat16 [1024, 1024], P(('seq', 'batch')), may hold values from -0.1875 to 0.1875
- out_weight: bfloat16 [1024, 1024], P(None, ('seq', 'batch')), may hold values from -0.375 to 0.375
- feed_gain: bfloat16 [1024], P(('seq', 'batch')), may hold values from 0.099609375 to 1.8984375
- feed_gate: bfloat16 [1024, 2816], P(('seq', 'batch')), may hold values from -0.1875 to 0.1875
- feed_up: bfloat16 [1024, 2816], P(('seq', 'batch')), may hold values from -0.1875 to 0.1875
- feed_down: bfloat16 [2816, 1024], P(None, ('seq', 'batch')), may hold values from -0.15625 to 0.15625
- conv_taps: bfloat16 [4, 5120], replicated, may hold values from -3 to 3
- decay_log: float32 [8], replicated, may hold values from -1 to 0.5
- decay_bias: float32 [8], replicated, may hold values from -8 to -2.25
- head_gain: bfloat16 [128], replicated, may hold values from 0.099609375 to 1.8984375
Outputs:
- block_out: bfloat16 [4, 1024, 1024], P('batch', 'seq')
- grad_in: bfloat16 [4, 1024, 1024], P('batch', 'seq')
- grad_mixer_gain: float32 [1024], replicated
- grad_query_weight: float32 [1024, 1024], P('seq', 'batch')
- grad_key_weight: float32 [1024, 2048], P('seq', 'batch')
- grad_value_weight: float32 [1024, 2048], P('seq', 'batch')
- grad_beta_weight: float32 [1024, 16], replicated
- grad_alpha_weight: float32 [1024, 8], replicated
- grad_gate_weight: float32 [1024, 1024], P('seq', 'batch')
- grad_out_weight: float32 [1024, 1024], P('seq', 'batch')
- grad_feed_gain: float32 [1024], replicated
- grad_feed_gate: float32 [1024, 2816], P('seq', 'batch')
- grad_feed_up: float32 [1024, 2816], P('seq', 'batch')
- grad_feed_down: float32 [2816, 1024], P('seq', 'batch')
- grad_conv_taps: float32 [4, 5120], replicated
- grad_decay_log: float32 [8], replicated
- grad_decay_bias: float32 [8], replicated
- grad_head_gain: float32 [128], replicated
Inputs may be any that keep to these rules, and one draw needn't show every extreme that they name: `lengths`: A row's positions below its length are real, the rest padding; in every draw some row has all 1024 positions real.
All inputs are finite; a program needn't handle non-finite values.
Results may differ from a plain program's by a relative error of at most 0.024.
Values may be sent and summed in bfloat16 or wider, within the bound.
A program may use at most 192 MiB of HBM per device.

v0:
```python
import jax
import jax.numpy as jnp
from jax import lax
from jax.sharding import PartitionSpec as P

H = 8
DK = 128
SPAN = 64
KEY = 1024


EPSILON = 1e-05
PRECISE = lax.Precision.HIGHEST


def shifted(x, axis, by):
    count = lax.axis_size(axis)
    pairs = [(i, i + by) for i in range(count) if 0 <= i + by < count]
    return lax.ppermute(x, axis, pairs)


def entering(x, axis, combine, identity):
    count, mine = (lax.axis_size(axis), lax.axis_index(axis))
    everything = jax.tree.map(
        lambda part, kind: lax.all_gather(part.astype(kind), axis), x, (jnp.bfloat16, jnp.bfloat16)
    )
    start = jax.tree.map(
        lambda part, zero: jnp.broadcast_to(jnp.asarray(zero, part.dtype), part.shape), x, identity
    )

    def entering_step(k, before):
        reached = k < mine
        new = combine(
            before, jax.tree.map(lambda part, own: part[k].astype(own.dtype), everything, x)
        )
        return jax.tree.map(lambda a, b: jnp.where(reached, a, b), new, before)

    return lax.fori_loop(0, count, entering_step, start)


def prefix(x, axis, combine, identity):
    count, mine = (lax.axis_size(axis), lax.axis_index(axis))
    everything = jax.tree.map(
        lambda part, kind: lax.all_gather(part.astype(kind), axis),
        x,
        jax.tree.map(lambda a: jnp.bfloat16 if a.dtype == jnp.float32 else a.dtype, x),
    )
    start = jax.tree.map(
        lambda part, zero: jnp.broadcast_to(jnp.asarray(zero, part.dtype), part.shape), x, identity
    )

    def prefix_step(k, before):
        at = count - 1 - k
        reached = at > mine
        new = combine(
            before, jax.tree.map(lambda part, own: part[at].astype(own.dtype), everything, x)
        )
        return jax.tree.map(lambda a, b: jnp.where(reached, a, b), new, before)

    return lax.fori_loop(0, count, prefix_step, start)


def shortened(x):
    return jax.tree.map(lambda a: a.astype(jnp.bfloat16) if a.dtype == jnp.float32 else a, x)


def root_norm(values, norm_gain):
    return (
        values * lax.rsqrt(jnp.mean(values * values, axis=-1, keepdims=True) + EPSILON) * norm_gain
    )


def unit_norm(values):
    return values * lax.rsqrt(jnp.sum(values * values, axis=-1, keepdims=True) + EPSILON)


def project(activation, weight):
    return jnp.dot(activation, weight, preferred_element_type=jnp.float32)


def project_back(gradient, weight):
    return lax.dot_general(
        gradient,
        weight,
        (((gradient.ndim - 1,), (1,)), ((), ())),
        preferred_element_type=jnp.float32,
    )


def weight_grad(activation, gradient):
    return jnp.einsum("rtd,rtx->dx", activation, gradient, preferred_element_type=jnp.float32)


def gated_norm(raw_out, gate_lin, norm_gain):
    normed = root_norm(raw_out, norm_gain) * jax.nn.silu(gate_lin.reshape(raw_out.shape))
    return normed.reshape(gate_lin.shape)


def identity_for(row_count):
    return (
        jnp.broadcast_to(jnp.eye(DK, dtype=jnp.float32), (row_count, H, DK, DK)),
        jnp.zeros((row_count, H, DK, DK), jnp.float32),
    )


def compose(former, latter):
    return (
        jnp.einsum("...ij,...jk->...ik", latter[0], former[0], precision=PRECISE),
        jnp.einsum("...ij,...jk->...ik", latter[0], former[1], precision=PRECISE) + latter[1],
    )


def features(extended, conv_taps, beta_lin, alpha_lin, decay_log, decay_bias, keep_mask):
    row_count, tok_count = (beta_lin.shape[0], beta_lin.shape[1])
    mixed_sum = conv_taps[0] * extended[:, 0:tok_count]
    for tap_index in range(1, 4):
        mixed_sum = (
            mixed_sum + conv_taps[tap_index] * extended[:, tap_index : tap_index + tok_count]
        )
    activated = jax.nn.silu(mixed_sum)
    queries = unit_norm(activated[..., :KEY].reshape(row_count, tok_count, H, DK)) * DK ** (-0.5)
    key_vecs = unit_norm(activated[..., KEY : 3 * KEY].reshape(row_count, tok_count, 2, H, DK))
    value_vecs = activated[..., 3 * KEY :].reshape(row_count, tok_count, 2, H, DK)
    strength = (
        jax.nn.sigmoid(beta_lin).reshape(row_count, tok_count, 2, H) * keep_mask[:, :, None, None]
    )
    gate_log = -jnp.exp(decay_log) * jax.nn.softplus(alpha_lin + decay_bias) * keep_mask[:, :, None]
    return (queries, key_vecs, value_vecs, strength, gate_log)


def span_terms(queries, key_vecs, value_vecs, strength, gate_log):
    row_count, tok_count = (gate_log.shape[0], gate_log.shape[1])
    blocks = tok_count // SPAN
    sub_steps = 2 * SPAN
    sub_gates = jnp.stack([gate_log, jnp.zeros_like(gate_log)], axis=2).reshape(
        row_count, blocks, sub_steps, H
    )
    cumulative = jnp.swapaxes(jnp.cumsum(sub_gates, axis=2), 2, 3)
    key_heads = jnp.swapaxes(key_vecs.reshape(row_count, blocks, sub_steps, H, DK), 2, 3)
    value_heads = jnp.swapaxes(value_vecs.reshape(row_count, blocks, sub_steps, H, DK), 2, 3)
    beta_heads = jnp.swapaxes(strength.reshape(row_count, blocks, sub_steps, H), 2, 3)
    query_heads = jnp.swapaxes(queries.reshape(row_count, blocks, SPAN, H, DK), 2, 3)
    places = jnp.arange(sub_steps)
    lower_mask = places[:, None] >= places[None, :]
    strict_mask = places[:, None] > places[None, :]
    spread = cumulative[..., :, None] - cumulative[..., None, :]
    decays = jnp.where(lower_mask, jnp.exp(jnp.where(lower_mask, spread, 0.0)), 0.0)
    key_gram = jnp.einsum("rchid,rchjd->rchij", key_heads, key_heads, precision=PRECISE)
    system = jnp.where(strict_mask, key_gram * decays, 0.0) * beta_heads[..., :, None] + jnp.eye(
        sub_steps, dtype=jnp.float32
    )
    right_side = jnp.concatenate(
        [
            (beta_heads * jnp.exp(cumulative))[..., None] * key_heads,
            beta_heads[..., None] * value_heads,
        ],
        axis=-1,
    )
    solved = lax.linalg.triangular_solve(
        system, right_side, left_side=True, lower=True, unit_diagonal=True
    )
    weighted = solved[..., :DK]
    base_vals = solved[..., DK:]
    final_log = cumulative[..., -1:]
    carried_keys = jnp.exp(final_log - cumulative)[..., None] * key_heads
    transit = jnp.exp(final_log)[..., None] * jnp.eye(DK, dtype=jnp.float32)
    transit = transit - jnp.einsum("rchjd,rchje->rchde", carried_keys, weighted, precision=PRECISE)
    offset = jnp.einsum("rchjd,rchje->rchde", carried_keys, base_vals, precision=PRECISE)
    query_log = cumulative[..., 1::2]
    scores = (
        jnp.einsum("rchtd,rchjd->rchtj", query_heads, key_heads, precision=PRECISE)
        * decays[..., 1::2, :]
    )
    return (query_heads, weighted, base_vals, scores, query_log, transit, offset)


def span_outputs(pieces, initial):
    query_heads, weighted, base_vals, scores, query_log, transit, offset = pieces

    def advance(carried, step_maps):
        return (
            jnp.einsum("rhde,rhef->rhdf", step_maps[0], carried, precision=PRECISE) + step_maps[1],
            carried,
        )

    final_state, starts = lax.scan(
        advance, initial, (jnp.moveaxis(transit, 1, 0), jnp.moveaxis(offset, 1, 0))
    )
    starts = jnp.moveaxis(starts, 0, 1)
    new_vals = base_vals - jnp.einsum("rchnd,rchde->rchne", weighted, starts, precision=PRECISE)
    output = jnp.exp(query_log)[..., None] * jnp.einsum(
        "rchtd,rchde->rchte", query_heads, starts, precision=PRECISE
    )
    output = output + jnp.einsum("rchtj,rchje->rchte", scores, new_vals, precision=PRECISE)
    row_count, blocks = (output.shape[0], output.shape[1])
    output = jnp.swapaxes(output, 2, 3).reshape(row_count, blocks * SPAN, H, DK)
    return (output, final_state)


def device_map(transit, offset):

    def absorb(carried, step_maps):
        return (compose(carried, step_maps), None)

    result, _ = lax.scan(
        absorb,
        identity_for(transit.shape[0]),
        (jnp.moveaxis(transit, 1, 0), jnp.moveaxis(offset, 1, 0)),
    )
    return result


def on_device(
    hidden_in,
    cotangent,
    lengths,
    mixer_gain,
    query_weight,
    key_weight,
    value_weight,
    beta_weight,
    alpha_weight,
    gate_weight,
    out_weight,
    feed_gain,
    feed_gate,
    feed_up,
    feed_down,
    conv_taps,
    decay_log,
    decay_bias,
    head_gain,
):
    (
        mixer_full,
        query_full,
        key_full,
        value_full,
        beta_full,
        alpha_full,
        gate_full,
        out_full,
        feed_gain_full,
        feed_gate_full,
        feed_up_full,
        feed_down_full,
    ) = (
        lax.all_gather(mixer_gain, ("seq", "batch"), axis=0, tiled=True),
        lax.all_gather(query_weight, ("seq", "batch"), axis=0, tiled=True),
        lax.all_gather(key_weight, ("seq", "batch"), axis=0, tiled=True),
        lax.all_gather(value_weight, ("seq", "batch"), axis=0, tiled=True),
        lax.all_gather(beta_weight, ("seq", "batch"), axis=0, tiled=True),
        lax.all_gather(alpha_weight, ("seq", "batch"), axis=0, tiled=True),
        lax.all_gather(gate_weight, ("seq", "batch"), axis=0, tiled=True),
        lax.all_gather(out_weight, ("seq", "batch"), axis=1, tiled=True),
        lax.all_gather(feed_gain, ("seq", "batch"), axis=0, tiled=True),
        lax.all_gather(feed_gate, ("seq", "batch"), axis=0, tiled=True),
        lax.all_gather(feed_up, ("seq", "batch"), axis=0, tiled=True),
        lax.all_gather(feed_down, ("seq", "batch"), axis=1, tiled=True),
    )
    row_count, tok_count = (hidden_in.shape[0], hidden_in.shape[1])
    positions = lax.axis_index("seq") * tok_count + jnp.arange(tok_count, dtype=jnp.int32)
    keep_mask = (positions[None, :] < lengths[:, None]).astype(jnp.float32)
    stream_in = hidden_in.astype(jnp.float32)
    mixer_scale = mixer_full.astype(jnp.float32)
    normed_in = root_norm(stream_in, mixer_scale).astype(jnp.bfloat16)
    projected = jnp.concatenate(
        [
            project(normed_in, query_full).astype(jnp.bfloat16),
            project(normed_in, key_full).astype(jnp.bfloat16),
            project(normed_in, value_full).astype(jnp.bfloat16),
        ],
        axis=-1,
    )
    left_rim = shifted(projected[:, tok_count - 3 :], "seq", 1)
    extended = jnp.concatenate([left_rim, projected], axis=1).astype(jnp.float32)
    beta_lin = project(normed_in, beta_full)
    alpha_lin = project(normed_in, alpha_full)
    gate_lin = project(normed_in, gate_full)
    taps_wide = conv_taps.astype(jnp.float32)
    head_scale = head_gain.astype(jnp.float32)
    pieces = span_terms(
        *features(extended, taps_wide, beta_lin, alpha_lin, decay_log, decay_bias, keep_mask)
    )
    device_maps = device_map(pieces[5], pieces[6])
    identity_maps = identity_for(row_count)
    incoming = entering((device_maps[0], device_maps[1]), "seq", compose, identity_maps)
    initial = incoming[1]
    raw_out, _ = span_outputs(pieces, initial)
    gated = gated_norm(raw_out, gate_lin, head_scale).astype(jnp.bfloat16)
    after_mixer = stream_in + project(gated, out_full)
    feed_scale = feed_gain_full.astype(jnp.float32)
    normed_mid = root_norm(after_mixer, feed_scale).astype(jnp.bfloat16)
    gate_act = project(normed_mid, feed_gate_full)
    up_act = project(normed_mid, feed_up_full)
    hidden = (jax.nn.silu(gate_act) * up_act).astype(jnp.bfloat16)
    block_out = (after_mixer + project(hidden, feed_down_full)).astype(jnp.bfloat16)
    d_hidden = project_back(cotangent, feed_down_full)
    sigmoid_gate = jax.nn.sigmoid(gate_act)
    d_gate = (d_hidden * up_act * sigmoid_gate * (1.0 + gate_act * (1.0 - sigmoid_gate))).astype(
        jnp.bfloat16
    )
    d_up = (d_hidden * gate_act * sigmoid_gate).astype(jnp.bfloat16)
    d_mid = project_back(d_gate, feed_gate_full) + project_back(d_up, feed_up_full)
    _, mid_back = jax.vjp(root_norm, after_mixer, feed_scale)
    d_stream, grad_feed_gain = mid_back(d_mid)
    d_stream = cotangent.astype(jnp.float32) + d_stream
    d_branch = d_stream.astype(jnp.bfloat16)
    d_gated = project_back(d_branch, out_full)

    def mixer_core(extended_in, taps_in, beta_in, alpha_in, decay_in, bias_in, state_in):
        core_pieces = span_terms(
            *features(extended_in, taps_in, beta_in, alpha_in, decay_in, bias_in, keep_mask)
        )
        return (span_outputs(core_pieces, state_in), core_pieces)

    _, core_back, pieces_again = jax.vjp(
        mixer_core,
        extended,
        taps_wide,
        beta_lin,
        alpha_lin,
        decay_log,
        decay_bias,
        initial,
        has_aux=True,
    )
    _, norm_back = jax.vjp(gated_norm, raw_out, gate_lin, head_scale)
    d_raw, d_gate_lin, grad_head_gain = norm_back(d_gated)

    def outputs_only(state_in):
        return span_outputs(pieces_again, state_in)[0]

    _, state_back = jax.vjp(outputs_only, initial)
    own_grad = state_back(d_raw)[0]
    suffix_maps = prefix(
        (jnp.swapaxes(device_maps[0], -1, -2), own_grad), "seq", compose, identity_maps
    )
    d_extended, grad_conv_taps, d_beta, d_alpha, grad_decay_log, grad_decay_bias, _ = core_back(
        (d_raw, suffix_maps[1])
    )
    from_right = shifted(shortened(d_extended[:, :3]), "seq", -1)
    d_proj = d_extended[:, 3:].at[:, tok_count - 3 :].add(from_right).astype(jnp.bfloat16)
    d_query = d_proj[..., :KEY]
    d_key = d_proj[..., KEY : 3 * KEY]
    d_value = d_proj[..., 3 * KEY :]
    d_beta_low = d_beta.astype(jnp.bfloat16)
    d_alpha_low = d_alpha.astype(jnp.bfloat16)
    d_gate_low = d_gate_lin.astype(jnp.bfloat16)
    grad_beta_weight = weight_grad(normed_in, d_beta_low)
    grad_alpha_weight = weight_grad(normed_in, d_alpha_low)
    d_normed = (
        project_back(d_query, query_full)
        + project_back(d_key, key_full)
        + project_back(d_value, value_full)
    )
    d_normed = (
        d_normed
        + project_back(d_beta_low, beta_full)
        + project_back(d_alpha_low, alpha_full)
        + project_back(d_gate_low, gate_full)
    )
    _, in_back = jax.vjp(root_norm, stream_in, mixer_scale)
    d_input, grad_mixer_gain = in_back(d_normed)
    grad_in = (d_stream + d_input).astype(jnp.bfloat16)
    small_sums = lax.psum(
        (
            grad_mixer_gain,
            grad_beta_weight,
            grad_alpha_weight,
            grad_feed_gain,
            grad_conv_taps,
            grad_decay_log,
            grad_decay_bias,
            grad_head_gain,
        ),
        ("seq", "batch"),
    )
    all_acts = (
        lax.all_gather(normed_in, "batch", axis=0, tiled=True),
        lax.all_gather(gated, "batch", axis=0, tiled=True),
        lax.all_gather(normed_mid, "batch", axis=0, tiled=True),
        lax.all_gather(hidden, "batch", axis=0, tiled=True),
    )
    all_cols = (
        lax.all_to_all(d_query, "batch", split_axis=2, concat_axis=0, tiled=True),
        lax.all_to_all(d_key, "batch", split_axis=2, concat_axis=0, tiled=True),
        lax.all_to_all(d_value, "batch", split_axis=2, concat_axis=0, tiled=True),
        lax.all_to_all(d_gate_low, "batch", split_axis=2, concat_axis=0, tiled=True),
        lax.all_to_all(d_branch, "batch", split_axis=2, concat_axis=0, tiled=True),
        lax.all_to_all(d_gate, "batch", split_axis=2, concat_axis=0, tiled=True),
        lax.all_to_all(d_up, "batch", split_axis=2, concat_axis=0, tiled=True),
        lax.all_to_all(cotangent, "batch", split_axis=2, concat_axis=0, tiled=True),
    )
    summed = (
        lax.psum_scatter(
            weight_grad(all_acts[0], all_cols[0]).astype(jnp.bfloat16),
            "seq",
            scatter_dimension=0,
            tiled=True,
        ).astype(jnp.float32),
        lax.psum_scatter(
            weight_grad(all_acts[0], all_cols[1]).astype(jnp.bfloat16),
            "seq",
            scatter_dimension=0,
            tiled=True,
        ).astype(jnp.float32),
        lax.psum_scatter(
            weight_grad(all_acts[0], all_cols[2]).astype(jnp.bfloat16),
            "seq",
            scatter_dimension=0,
            tiled=True,
        ).astype(jnp.float32),
        lax.psum_scatter(
            weight_grad(all_acts[0], all_cols[3]).astype(jnp.bfloat16),
            "seq",
            scatter_dimension=0,
            tiled=True,
        ).astype(jnp.float32),
        lax.psum_scatter(
            weight_grad(all_acts[1], all_cols[4]).astype(jnp.bfloat16),
            "seq",
            scatter_dimension=0,
            tiled=True,
        ).astype(jnp.float32),
        lax.psum_scatter(
            weight_grad(all_acts[2], all_cols[5]).astype(jnp.bfloat16),
            "seq",
            scatter_dimension=0,
            tiled=True,
        ).astype(jnp.float32),
        lax.psum_scatter(
            weight_grad(all_acts[2], all_cols[6]).astype(jnp.bfloat16),
            "seq",
            scatter_dimension=0,
            tiled=True,
        ).astype(jnp.float32),
        lax.psum_scatter(
            weight_grad(all_acts[3], all_cols[7]).astype(jnp.bfloat16),
            "seq",
            scatter_dimension=0,
            tiled=True,
        ).astype(jnp.float32),
    )
    return (
        block_out,
        grad_in,
        small_sums[0],
        summed[0],
        summed[1],
        summed[2],
        small_sums[1],
        small_sums[2],
        summed[3],
        summed[4],
        small_sums[3],
        summed[5],
        summed[6],
        summed[7],
        small_sums[4],
        small_sums[5],
        small_sums[6],
        small_sums[7],
    )


def solution(mesh):
    placed = (
        P("batch", "seq", None),
        P("batch", "seq", None),
        P("batch"),
        P(("seq", "batch")),
        P(("seq", "batch"), None),
        P(("seq", "batch"), None),
        P(("seq", "batch"), None),
        P(("seq", "batch"), None),
        P(("seq", "batch"), None),
        P(("seq", "batch"), None),
        P(None, ("seq", "batch")),
        P(("seq", "batch")),
        P(("seq", "batch"), None),
        P(("seq", "batch"), None),
        P(None, ("seq", "batch")),
        P(),
        P(),
        P(),
        P(),
    )
    return jax.shard_map(
        on_device,
        mesh=mesh,
        in_specs=placed,
        out_specs=(
            P("batch", "seq", None),
            P("batch", "seq", None),
            P(),
            P("seq", "batch"),
            P("seq", "batch"),
            P("seq", "batch"),
            P(),
            P(),
            P("seq", "batch"),
            P("seq", "batch"),
            P(),
            P("seq", "batch"),
            P("seq", "batch"),
            P("seq", "batch"),
            P(),
            P(),
            P(),
            P(),
        ),
        check_vma=False,
    )
```

profile of v0, /device:TPU:7, one launch (start us, length us, event | category | flops | bytes accessed | tf_op | source)
XLA Modules:
  0.0 1527.5 jit_solution(13250606000975931500)
XLA Ops:
  11.2 39.9 %all-reduce.21 = (bf16[1024]{0:T(1024)(128)(2,1)S(1)}, bf16[1024]{0:T(1024)(128)(2,1)}) all-reduce(bf16[1024]{0:T(1024)(128)(2,1)S(1)} %dynamic-update-slice.3, bf16[1024]{0:T(1024)(128)(2,1)S(1)} %dynamic-update-slice.4), channel_id=1, replica_groups=mesh['seq'=8,'batch'=4] {'seq','batch'}, use_global_device_ids=true, to_apply=%add.17 | all-reduce | flops 2048 | bytes 8192
  51.1 57.3 %all-gather.6 = bf16[32,32,8]{1,2,0:T(8,128)(2,1)S(1)} all-gather(bf16[1,32,8]{1,2,0:T(8,128)(2,1)} %bitcast.914), channel_id=1, replica_groups=mesh['seq'=8,'batch'=4] {'seq','batch'}, dimensions={0}, use_global_device_ids=true | all-gather | bytes 16896 | tf_op jit(solution)/shard_map/all_gather | solution.py:253
  113.6 66.5 %all-gather.7 = bf16[32,32,16]{1,2,0:T(8,128)(2,1)S(1)} all-gather(bf16[1,32,16]{1,2,0:T(8,128)(2,1)} %bitcast.913), channel_id=1, replica_groups=mesh['seq'=8,'batch'=4] {'seq','batch'}, dimensions={0}, use_global_device_ids=true | all-gather | bytes 33792 | tf_op jit(solution)/shard_map/all_gather | solution.py:252
  224.9 158.7 %custom-call.12 = f32[1,2,8,1,128,128]{4,5,3,2,1,0:T(8,128)} custom-call(f32[1,2,8,1,128,128]{5,4,3,2,1,0:T(8,128)} %get-tuple-element.870), custom_call_target="InvertDiagBlocksLowerTriangular" | custom-call | tf_op jit(solution)/shard_map/triangular_solve/custom-call.1 | solution.py:159
  395.4 9.5 while.93
  434.8 30.6 %all-gather.47.cloned.1.call-done = bf16[8,8,128,128]{3,2,1,0:T(8,128)(2,1)} async-done(((bf16[1,8,128,128]{3,2,1,0:T(8,128)(2,1)}), bf16[8,8,128,128]{3,2,1,0:T(8,128)(2,1)}) %all-gather.47.cloned.1.call-update) | async-done | bytes 2097168 | tf_op jit(solution)/shard_map/all_gather | solution.py:25
  465.4 12.6 while.96
  494.1 28.7 %all-gather.31.cloned.1.call-done = bf16[1024,1024]{1,0:T(8,128)(2,1)} async-done(((bf16[32,1024]{1,0:T(8,128)(2,1)}), bf16[1024,1024]{1,0:T(8,128)(2,1)}) %all-gather.31.cloned.1.call-update) | async-done | bytes 2097168 | tf_op jit(solution)/shard_map/all_gather | solution.py:254
  527.0 53.8 %all-gather.33.cloned.1.call-done = bf16[1024,1024]{0,1:T(8,128)(2,1)} async-done(((bf16[1024,32]{0,1:T(8,128)(2,1)}), bf16[1024,1024]{0,1:T(8,128)(2,1)}) %all-gather.33.cloned.1.call-update) | async-done | bytes 2097168 | tf_op jit(solution)/shard_map/all_gather | solution.py:255
  590.7 59.2 %all-gather.37.cloned.1.call-done = bf16[1024,2816]{1,0:T(8,128)(2,1)} async-done(((bf16[32,2816]{1,0:T(8,128)(2,1)}), bf16[1024,2816]{1,0:T(8,128)(2,1)}) %all-gather.37.cloned.1.call-update) | async-done | bytes 5767184 | tf_op jit(solution)/shard_map/all_gather | solution.py:258
  654.7 64.1 %all-gather.35.cloned.1.call-done = bf16[1024,2816]{1,0:T(8,128)(2,1)} async-done(((bf16[32,2816]{1,0:T(8,128)(2,1)}), bf16[1024,2816]{1,0:T(8,128)(2,1)}) %all-gather.35.cloned.1.call-update) | async-done | bytes 5767184 | tf_op jit(solution)/shard_map/all_gather | solution.py:257
  723.5 64.0 %all-gather.39.cloned.1.call-done = bf16[2816,1024]{0,1:T(8,128)(2,1)} async-done(((bf16[2816,32]{0,1:T(8,128)(2,1)}), bf16[2816,1024]{0,1:T(8,128)(2,1)}) %all-gather.39.cloned.1.call-update) | async-done | bytes 5767184 | tf_op jit(solution)/shard_map/all_gather | solution.py:259
  861.9 17.4 %reduce.41 = bf16[2816,128]{1,0:T(8,128)(2,1)} reduce(bf16[2816,1,128]{2,1,0:T(2,128)(2,1)} %bitcast.845, bf16[]{:T(256)} %broadcast.740), dimensions={1}, to_apply=%bitcast.691.reduce_sub_computation | reduce | bytes 1441794
  881.3 12.7 all_to_all.146
  908.7 158.6 %custom-call.8 = f32[1,2,8,1,128,128]{4,5,3,2,1,0:T(8,128)} custom-call(f32[1,2,8,1,128,128]{5,4,3,2,1,0:T(8,128)} %add_bitcast_fusion), custom_call_target="InvertDiagBlocksLowerTriangular" | custom-call | tf_op jit(solution)/shard_map/transpose(jvp())/triangular_solve | solution.py:159
  1103.6 17.6 %reduce.42 = bf16[2816,128]{1,0:T(8,128)(2,1)} reduce(bf16[2816,1,128]{2,1,0:T(2,128)(2,1)} %bitcast.847, bf16[]{:T(256)} %broadcast.740), dimensions={1}, to_apply=%bitcast.693.reduce_sub_computation | reduce | bytes 1441794
  1153.9 12.7 while.98
  1168.8 9.8 while.95
  1259.3 11.4 reduce.37
  1270.9 11.7 all_to_all.148
  1287.2 11.4 reduce.38
  1298.8 10.4 all_to_all.149
  1378.2 41.9 %all-reduce.19 = (f32[1024]{0:T(1024)}, f32[1024,8]{0,1:T(8,128)}, f32[1024]{0:T(1024)}, f32[8]{0:T(128)}, f32[8]{0:T(128)}, /*index=5*/f32[128]{0:T(128)}) all-reduce(f32[1024]{0:T(1024)S(1)} %get-tuple-element.765, f32[1024,8]{0,1:T(8,128)S(1)} %fusion.210, ...), channel_id=1, replica_groups=mesh['seq'=8,'batch'=4] {'seq','batch'}, use_global_device_ids=true, to_apply=%region_34.36 | all-reduce | flops 10384 | bytes 83072 | tf_op jit(solution)/shard_map/psum | solution.py:366
  1430.3 87.2 %all-reduce.24.cloned.1.call-done = (f32[1024,16]{0,1:T(8,128)}, f32[4,5120]{1,0:T(4,128)}) async-done(((f32[1024,16]{0,1:T(8,128)}, f32[4,5120]{1,0:T(4,128)}), (f32[1024,16]{0,1:T(8,128)}, f32[4,5120]{1,0:T(4,128)})) %all-reduce.24.cloned.1.call-update) | async-done | bytes 147472 | tf_op jit(solution)/shard_map/psum | solution.py:366
  (715 shorter events, 514.6 us)
Async XLA Ops:
  7.2 176.4 %all-gather.25.cloned.1.call-start = ((), (), s32[]{:S(2)}) async-start(), calls=%async_computation.16 | async-start | bytes 2162688 | tf_op jit(solution)/shard_map/all_gather | solution.py:249
  7.9 177.8 %all-gather.27.cloned.1.call-start = ((), (), s32[]{:S(2)}) async-start(), calls=%async_computation.17 | async-start | bytes 4325376 | tf_op jit(solution)/shard_map/all_gather | solution.py:250
  8.7 186.6 %all-gather.29.cloned.1.call-start = ((), (), s32[]{:S(2)}) async-start(), calls=%async_computation.18 | async-start | bytes 4325376 | tf_op jit(solution)/shard_map/all_gather | solution.py:251
  9.4 425.4 %all-gather.45.cloned.1.call-start = ((), (), s32[]{:S(2)}) async-start(), calls=%async_computation.32 | async-start | bytes 2359296 | tf_op jit(solution)/shard_map/all_gather | solution.py:25
  407.6 115.3 %all-gather.31.cloned.1.call-start = ((), (), s32[]{:S(2)}) async-start(), calls=%async_computation.19 | async-start | bytes 2162688 | tf_op jit(solution)/shard_map/all_gather | solution.py:254
  408.2 172.7 %all-gather.33.cloned.1.call-start = ((), (), s32[]{:S(2)}) async-start(), calls=%async_computation.20 | async-start | bytes 2162688 | tf_op jit(solution)/shard_map/all_gather | solution.py:255
  408.9 241.0 %all-gather.37.cloned.1.call-start = ((), (), s32[]{:S(2)}) async-start(), calls=%async_computation.22 | async-start | bytes 5947392 | tf_op jit(solution)/shard_map/all_gather | solution.py:258
  409.7 309.2 %all-gather.35.cloned.1.call-start = ((), (), s32[]{:S(2)}) async-start(), calls=%async_computation.21 | async-start | bytes 5947392 | tf_op jit(solution)/shard_map/all_gather | solution.py:257
  410.4 377.1 %all-gather.39.cloned.1.call-start = ((), (), s32[]{:S(2)}) async-start(), calls=%async_computation.23 | async-start | bytes 5947392 | tf_op jit(solution)/shard_map/all_gather | solution.py:259
  411.0 426.0 %all-gather.41.cloned.1.call-start = ((), (), s32[]{:S(2)}) async-start(), calls=%async_computation.24 | async-start | bytes 1310720 | tf_op jit(solution)/shard_map/all_gather | solution.py:380
  411.7 443.3 %all-gather.53.cloned.1.call-start = ((), (), s32[]{:S(2)}) async-start(), calls=%async_computation.36 | async-start | bytes 1310720 | tf_op jit(solution)/shard_map/all_gather | solution.py:381
  526.4 373.5 %all-gather.43.cloned.1.call-start = ((), (), s32[]{:S(2)}) async-start(), calls=%async_computation.30 | async-start | bytes 1310720 | tf_op jit(solution)/shard_map/all_gather | solution.py:382
  585.3 568.6 %all-gather.49.cloned.1.call-start = ((), (), s32[]{:S(2)}) async-start(), calls=%async_computation.34 | async-start | bytes 2359296 | tf_op jit(solution)/shard_map/all_gather | solution.py:44
  590.5 563.4 %all-gather.51.cloned.1.call-start = ((), (), s32[]{:S(2)}) async-start(), calls=%async_computation.35 | async-start | bytes 2359296 | tf_op jit(solution)/shard_map/all_gather | solution.py:44
  819.8 518.2 %all-gather.55.cloned.1.call-start = ((), (), s32[]{:S(2)}) async-start(), calls=%async_computation.37 | async-start | bytes 3604480 | tf_op jit(solution)/shard_map/all_gather | solution.py:383
  820.4 525.2 %reduce-scatter.19.cloned.1.call-start = ((), (), s32[]{:S(2)}) async-start(), calls=%async_computation.28 | async-start | bytes 589824 | tf_op jit(solution)/shard_map/reduce_scatter | solution.py:414
  839.6 507.6 %reduce-scatter.21.cloned.1.call-start = ((), (), s32[]{:S(2)}) async-start(), calls=%async_computation.29 | async-start | bytes 589824 | tf_op jit(solution)/shard_map/reduce_scatter | solution.py:420
  857.7 562.5 %reduce-scatter.25.cloned.1.call-start = ((), (), s32[]{:S(2)}) async-start(), calls=%async_computation.38 | async-start | bytes 1769472
  1129.0 293.1 %reduce-scatter.27.cloned.1.call-start = ((), (), s32[]{:S(2)}) async-start(), calls=%async_computation.39 | async-start | bytes 1769472
  1153.8 270.1 %reduce-scatter.13.cloned.1.call-start = ((), (), s32[]{:S(2)}) async-start(), calls=%async_computation.25 | async-start | bytes 589824 | tf_op jit(solution)/shard_map/reduce_scatter | solution.py:396
  1257.6 167.8 %reduce-scatter.15.cloned.1.call-start = ((), (), s32[]{:S(2)}) async-start(), calls=%async_computation.26 | async-start | bytes 1179648 | tf_op jit(solution)/shard_map/reduce_scatter | solution.py:402
  1286.4 140.6 %reduce-scatter.17.cloned.1.call-start = ((), (), s32[]{:S(2)}) async-start(), calls=%async_computation.27 | async-start | bytes 1179648 | tf_op jit(solution)/shard_map/reduce_scatter | solution.py:408
  1325.2 103.5 %reduce-scatter.23.cloned.1.call-start = ((), (), s32[]{:S(2)}) async-start(), calls=%async_computation.31 | async-start | bytes 1622016 | tf_op jit(solution)/shard_map/reduce_scatter | solution.py:438
  1342.0 175.6 %all-reduce.24.cloned.1.call-start = ((), (), s32[]{:S(2)}) async-start(), calls=%async_computation.40 | async-start | bytes 294912 | tf_op jit(solution)/shard_map/psum | solution.py:366
  (161 other events, 1684.3 us)
Sparse Core Ops, SparseCore 0:
  10.9 57.0 all-gather.24
  70.9 61.0 all-gather.26
  134.8 60.3 all-gather.28
  405.8 28.9 all-gather.44
  436.8 28.5 all-gather.46
  468.1 54.7 all-gather.30
  525.7 55.0 all-gather.32
  583.7 66.1 all-gather.36
  652.8 65.9 all-gather.34
  721.6 65.9 all-gather.38
  816.8 26.4 all-gather.52
  845.8 26.4 all-gather.42
  874.3 30.6 all-gather.48
  907.0 28.7 all-gather.50
  937.6 40.5 all-gather.54
  980.2 29.1 reduce-scatter.18
  1011.5 29.6 reduce-scatter.20
  1043.5 32.4 reduce-scatter.24
  1153.9 34.1 reduce-scatter.26
  1257.7 28.0 reduce-scatter.12
  1288.1 30.7 reduce-scatter.14
  1321.2 30.8 reduce-scatter.16
  1354.2 31.9 reduce-scatter.22
  1393.0 124.4 all-reduce.23
  (1 shorter events, 24.5 us)
where the time goes:
time: 1540 us; the launch traced here: 1530 us
  other arithmetic  457 us (30%)
  waiting for transfers between devices  407 us (26%)
  blocking collectives  262 us (17%)
  matrix products  197 us (13%)
  local copies, waits for them, and re-layouts  163 us (11%)
  starting transfers between devices  21.7 us (1%)
  between operations  17.6 us (1%)
    another operation x6, other arithmetic, span_terms(): lax.linalg.triangular_solve(system, right_side, left_side=True, lower=Tru...  321 us
    psum x1, waiting for transfers between devices, on_device(): lax.psum((grad_mixer_gain, grad_beta_weight, grad_alpha_weight, grad_feed...  87.2 us
    unnamed x11, other arithmetic  68.7 us
    all_gather x1, blocking collectives, on_device(): lax.all_gather(beta_weight, ('seq', 'batch'), axis=0, tiled=True)  66.5 us
    all_gather x1, waiting for transfers between devices, on_device(): lax.all_gather(feed_gate, ('seq', 'batch'), axis=0, tiled=True)  64.1 us
    all_gather x1, waiting for transfers between devices, on_device(): lax.all_gather(feed_down, ('seq', 'batch'), axis=1, tiled=True)  64 us
    all_gather x1, waiting for transfers between devices, on_device(): lax.all_gather(feed_up, ('seq', 'batch'), axis=0, tiled=True)  59.2 us
    all_gather x1, blocking collectives, on_device(): lax.all_gather(alpha_weight, ('seq', 'batch'), axis=0, tiled=True)  57.3 us
  transfers between devices with their start and end apart: 29, of which 11 were waited for; matrix products, arithmetic and copies ran while one was open for 40% of the time, Pallas kernels for 0%

commit v1 on v0

v1 whole, which is shorter than its diff:
```python
import functools
import jax
import jax.numpy as jnp
from jax import lax
from jax.experimental import pallas as pl
from jax.experimental.pallas import tpu as pltpu
from jax.sharding import PartitionSpec as P

F32, BF16 = jnp.float32, jnp.bfloat16
EPS = 1e-05
DK = 128
HALF = 64
GS = 4
GB = GS * HALF
NN = (((1,), (0,)), ((), ()))
NT = (((1,), (1,)), ((), ()))
TN = (((0,), (0,)), ((), ()))


def mm(a, b, dims=NN):
    return lax.dot_general(a.astype(BF16), b.astype(BF16), dims, preferred_element_type=F32)


def split(a):
    hi = a.astype(BF16)
    return hi, (a - hi.astype(F32)).astype(BF16)


def mm3(a, b, dims=NN):
    (ah, al), (bh, bl) = (x if isinstance(x, tuple) else split(x) for x in (a, b))
    return (
        lax.dot_general(ah, bl, dims, preferred_element_type=F32)
        + lax.dot_general(al, bh, dims, preferred_element_type=F32)
    ) + lax.dot_general(ah, bh, dims, preferred_element_type=F32)


def iota(shape, axis):
    return lax.broadcasted_iota(jnp.int32, shape, axis)


def sub_masks():
    rows, cols = iota((128, 128), 0), iota((128, 128), 1)
    tr, tc = 2 * (rows & 63) + (rows >> 6), 2 * (cols & 63) + (cols >> 6)
    strict = tr > tc
    levels = []
    for bits in range(3, 7):
        same_up = (tr >> (bits + 1)) == (tc >> (bits + 1))
        levels.append(strict & same_up & ((tr >> bits) != (tc >> bits)))
    base = strict & ((tr >> 3) == (tc >> 3))
    return strict, base, levels


def unit(a):
    r = lax.rsqrt(jnp.sum(a * a, axis=-1, keepdims=True) + EPS)
    return a * r, r


def softplus(x):
    return jnp.maximum(x, 0.0) + jnp.log1p(jnp.exp(-jnp.abs(x)))


def lane(x, width=128):
    return jnp.broadcast_to(x, (x.shape[0], width))


def gates(sm, dec_log, dec_bias, keep):
    sig0, sig1 = jax.nn.sigmoid(sm[:, 0:1]), jax.nn.sigmoid(sm[:, 1:2])
    al = sm[:, 2:3] + dec_bias
    return sig0, sig1, al


def span_decay(gb, tri, masks):
    c = mm3(tri, gb)
    ct = jnp.transpose(jnp.concatenate([c, c], axis=0))[:64]
    e = jnp.exp(jnp.minimum(c - ct, 0.0))
    return c, e


def conv_mix(buf, taps):
    mix = taps[0:1] * buf[5 : 5 + GB]
    for j in range(1, 4):
        mix = mix + taps[j : j + 1] * buf[5 + j : 5 + j + GB]
    return mix


def head_taps(taps_ref, head, heads):
    parts = []
    for col in (head, heads + head, 2 * heads + head, 3 * heads + head, 4 * heads + head):
        parts.append(taps_ref[:, pl.ds(pl.multiple_of(col * 128, 128), 128)].astype(F32))
    return jnp.concatenate(parts, axis=1)


def fwd_kernel(
    rep, heads,
    len_ref, dlog_ref, dbias_ref,
    hid_ref, gain_ref, w_ref, taps_ref, hg_ref,
    part_ref, normed_ref, pre_ref, gl_ref, sm_ref, gated_ref, raw_ref,
    t_ref, wt_ref, vn_ref, n_ref, p_ref, s_ref,
    buf, state,
):
    step = pl.program_id(0)
    place = lax.axis_index("seq")
    head = place // rep

    @pl.when(step == 0)
    def _():
        state[...] = jnp.zeros_like(state)
        buf[0:8] = jnp.zeros((8, 640), F32)

    x = hid_ref[...].astype(F32)
    r = lax.rsqrt(jnp.mean(x * x, axis=-1, keepdims=True) + EPS)
    normed = (x * r * gain_ref[...]).astype(BF16)
    normed_ref[...] = normed
    proj = mm(normed, w_ref[:, 0:896])
    pre = proj[:, 0:640].astype(BF16).astype(F32)
    pre_ref[...] = pre
    gl = proj[:, 640:768]
    sm = proj[:, 768:896]
    gl_ref[...] = gl
    sm_ref[...] = sm
    buf[8 : 8 + GB] = pre
    taps = head_taps(taps_ref, head, heads)
    mix = conv_mix(buf, taps)
    buf[0:8] = pre[GB - 8 : GB]
    act = mix * jax.nn.sigmoid(mix)
    q = unit(act[:, 0:128])[0] * DK ** (-0.5)
    k0, k1 = unit(act[:, 128:256])[0], unit(act[:, 256:384])[0]
    v0, v1 = act[:, 384:512], act[:, 512:640]
    pos = step * GB + iota((GB, 1), 0)
    keep = (pos < len_ref[0]).astype(F32)
    sig0, sig1, al = gates(sm, None, dbias_ref[head], keep)
    b0, b1 = sig0 * keep, sig1 * keep
    eg = jnp.exp(jnp.full((1, 1), dlog_ref[head], F32))
    g = lane(-eg * softplus(al) * keep)
    b0, b1 = lane(b0), lane(b1)

    strict, base, levels = sub_masks()
    eye = (iota((128, 128), 0) == iota((128, 128), 1)).astype(F32)
    tri = (iota((64, 64), 0) >= iota((64, 64), 1)).astype(F32)
    causal = iota((64, 128), 0) >= (iota((64, 128), 1) & 63)

    K, Q, V, B, C, N, P, Kc = [], [], [], [], [], [], [], []
    for s in range(GS):
        sl = slice(64 * s, 64 * s + 64)
        K.append(jnp.concatenate([k0[sl], k1[sl]], axis=0))
        V.append(jnp.concatenate([v0[sl], v1[sl]], axis=0))
        B.append(jnp.concatenate([b0[sl], b1[sl]], axis=0))
        Q.append(q[sl])
        c, e = span_decay(g[sl], tri, None)
        C.append(c)
        ee = jnp.concatenate([e, e], axis=0)
        gram = mm3(jnp.concatenate([K[s], Q[s]], axis=0), K[s], NT)
        N.append(jnp.where(strict, gram[:128] * ee, 0.0) * B[s])
        P.append(jnp.where(causal, gram[128:] * e, 0.0))
        cc = jnp.concatenate([c, c], axis=0)
        Kc.append(jnp.exp(cc[63:64] - cc) * K[s])
    X = []
    n1 = [jnp.where(base, n, 0.0) for n in N]
    n1s = [split(n) for n in n1]
    n2 = [mm3(a, a) for a in n1s]
    n2s = [split(n) for n in n2]
    n3 = [mm3(a, b) for a, b in zip(n1s, n2s)]
    n4 = [mm3(a, a) for a in n2s]
    y = [eye - a + b - c for a, b, c in zip(n1, n2, n3)]
    X = [a + mm3(a, b) for a, b in zip(y, n4)]
    for lv in levels:
        xs = [split(x_) for x_ in X]
        bl = [jnp.where(lv, n, 0.0) for n in N]
        xb = [mm3(a, b) for a, b in zip(xs, bl)]
        X = [x_ - mm3(a, b) for x_, a, b in zip(X, xb, xs)]
    W, U = [], []
    for s in range(GS):
        cc = jnp.concatenate([C[s], C[s]], axis=0)
        rhs = jnp.concatenate([B[s] * jnp.exp(cc) * K[s], B[s] * V[s]], axis=1)
        wu = mm3(X[s], rhs)
        W.append(wu[:, :128])
        U.append(wu[:, 128:])
        t_ref[s] = X[s]
        wt_ref[s] = W[s]
        n_ref[s] = N[s]
        p_ref[s] = P[s]
    S = state[...]
    raw = []
    Ws = [split(a) for a in W]
    Kcs = [split(a) for a in Kc]
    for s in range(GS):
        s_ref[s] = S
        ss = split(S)
        vn = U[s] - mm3(Ws[s], ss)
        vn_ref[s] = vn
        vs = split(vn)
        o = jnp.exp(C[s]) * mm3(Q[s], ss) + mm3(P[s], vs)
        raw.append(o)
        S = jnp.exp(C[s][63:64]) * S + mm3(Kcs[s], vs, TN)
    state[...] = S
    o = jnp.concatenate(raw, axis=0)
    raw_ref[...] = o
    rr = lax.rsqrt(jnp.mean(o * o, axis=-1, keepdims=True) + EPS)
    gated = (o * rr * hg_ref[...] * (gl * jax.nn.sigmoid(gl))).astype(BF16)
    gated_ref[...] = gated
    if rep > 1:
        gated = jnp.where(lax.rem(place, rep) == 0, gated, jnp.zeros_like(gated))
    part_ref[...] = mm(gated, w_ref[:, 896:1024], NT).astype(BF16)


def bwd_kernel(
    rep, heads, steps,
    len_ref, dlog_ref, dbias_ref,
    dbr_ref, w_ref, taps_ref, hg_ref, pre_ref, prev_ref, gl_ref, sm_ref, raw_ref,
    t_ref, wt_ref, vn_ref, n_ref, p_ref, s_ref,
    dall_ref, part_ref, small_ref,
    buf, dbuf, dstate,
):
    step = pl.program_id(0)
    blk = steps - 1 - step
    place = lax.axis_index("seq")
    head = place // rep

    @pl.when(step == 0)
    def _():
        dstate[...] = jnp.zeros_like(dstate)
        dbuf[GB : GB + 8] = jnp.zeros((8, 640), F32)
        small_ref[...] = jnp.zeros_like(small_ref)

    d_gated = mm(dbr_ref[...], w_ref[:, 896:1024])
    gl, sm, o, hg = gl_ref[...], sm_ref[...], raw_ref[...], hg_ref[...]
    sg = jax.nn.sigmoid(gl)
    rr = lax.rsqrt(jnp.mean(o * o, axis=-1, keepdims=True) + EPS)
    yn = o * rr
    dn = d_gated * (gl * sg)
    d_gl = d_gated * (yn * hg) * (sg * (1.0 + gl * (1.0 - sg)))
    g_hg = jnp.sum(dn * yn, axis=0, keepdims=True)
    dy = dn * hg
    d_raw = rr * (dy - yn * jnp.mean(yn * dy, axis=-1, keepdims=True))

    pre = pre_ref[...]
    buf[8 : 8 + GB] = pre
    buf[0:8] = jnp.where(blk > 0, prev_ref[...], 0.0)
    taps = head_taps(taps_ref, head, heads)
    mix = conv_mix(buf, taps)
    sig = jax.nn.sigmoid(mix)
    act = mix * sig
    qn, rq = unit(act[:, 0:128])
    k0, r0 = unit(act[:, 128:256])
    k1, r1 = unit(act[:, 256:384])
    v0, v1 = act[:, 384:512], act[:, 512:640]
    q = qn * DK ** (-0.5)
    pos = blk * GB + iota((GB, 1), 0)
    keep = (pos < len_ref[0]).astype(F32)
    sig0, sig1, al = gates(sm, None, dbias_ref[head], keep)
    eg = jnp.exp(jnp.full((1, 1), dlog_ref[head], F32))
    g1 = -eg * softplus(al) * keep
    g = lane(g1)
    b0, b1 = lane(sig0 * keep), lane(sig1 * keep)

    strict, _, _ = sub_masks()
    tri = (iota((64, 64), 0) >= iota((64, 64), 1)).astype(F32)
    trit = (iota((64, 64), 0) <= iota((64, 64), 1)).astype(F32)
    causal = iota((64, 128), 0) >= (iota((64, 128), 1) & 63)

    K, Q, V, B, C, E, Kc, A1, A2, DO = [], [], [], [], [], [], [], [], [], []
    for s in range(GS):
        sl = slice(64 * s, 64 * s + 64)
        K.append(jnp.concatenate([k0[sl], k1[sl]], axis=0))
        V.append(jnp.concatenate([v0[sl], v1[sl]], axis=0))
        B.append(jnp.concatenate([b0[sl], b1[sl]], axis=0))
        Q.append(q[sl])
        c, e = span_decay(g[sl], tri, None)
        C.append(c)
        E.append(e)
        cc = jnp.concatenate([c, c], axis=0)
        Kc.append(jnp.exp(cc[63:64] - cc) * K[s])
        do = d_raw[sl]
        DO.append(do)
        A1.append(mm3(p_ref[s], do, TN))
        A2.append(mm3(jnp.exp(c) * Q[s], do, TN))
    dS = dstate[...]
    DV, DS = [None] * GS, [None] * GS
    for s in reversed(range(GS)):
        DS[s] = dS
        dss = split(dS)
        dvn = A1[s] + mm3(Kc[s], dss)
        DV[s] = dvn
        dS = jnp.exp(C[s][63:64]) * dS + A2[s] - mm3(wt_ref[s], dvn, TN)
    dstate[...] = dS
    dq_l, dk0_l, dk1_l, dv0_l, dv1_l, db0_l, db1_l, dg_l = [], [], [], [], [], [], [], []
    for s in range(GS):
        vn, sst, n, p = vn_ref[s], s_ref[s], n_ref[s], p_ref[s]
        vns = split(vn)
        cc = jnp.concatenate([C[s], C[s]], axis=0)
        ec = jnp.exp(cc)
        ee = jnp.concatenate([E[s], E[s]], axis=0)
        dr = mm3(t_ref[s], DV[s], TN)
        dd = mm3(jnp.concatenate([dr, DO[s]], axis=0), vns, NT)
        dN = jnp.where(strict, -dd[:128], 0.0)
        dP = jnp.where(causal, dd[128:], 0.0)
        h = mm3(jnp.concatenate([dr, DO[s]], axis=0), sst, NT)
        hk, hq = h[:128], h[128:]
        fh = dP * E[s]
        dq = ec[:64] * hq + mm3(fh, K[s])
        dgm = dN * ee * B[s]
        dkc = mm3(vns, DS[s], NT)
        ekc = jnp.exp(cc[63:64] - cc)
        dk = (
            ekc * dkc - B[s] * ec * hk + mm3(fh, Q[s], TN) + mm3(dgm + jnp.transpose(dgm), K[s])
        )
        khk = jnp.sum(K[s] * hk, axis=-1, keepdims=True)
        ecl = ec[:, 0:1]
        nb = jnp.where(strict, ee, 0.0)
        graml = mm3(K[s], K[s], NT)
        db = (
            jnp.sum(dr * V[s], axis=-1, keepdims=True)
            - ecl * khk
            + jnp.sum(dN * (graml * nb), axis=-1, keepdims=True)
        )
        e1 = dN * n
        f1 = dP * p
        z = e1[:64, :64] + e1[:64, 64:] + e1[64:, :64] + e1[64:, 64:] + f1[:, :64] + f1[:, 64:]
        dc = jnp.sum(z - jnp.transpose(z), axis=-1, keepdims=True)
        dks = -B[s][:, 0:1] * ecl * khk
        hj = jnp.sum(Kc[s] * dkc, axis=-1, keepdims=True)
        dc = dc + dks[:64] + dks[64:] - hj[:64] - hj[64:]
        dc = dc + ec[:64, 0:1] * jnp.sum(Q[s] * hq, axis=-1, keepdims=True)
        dcl = jnp.sum(hj, keepdims=True).reshape(1, 1) + ec[63:64, 0:1] * jnp.sum(
            jnp.sum(sst * DS[s], axis=-1, keepdims=True), axis=0, keepdims=True
        )
        dg = mm3(trit, lane(dc)) + dcl
        dg_l.append(dg[:, 0:1])
        dq_l.append(dq)
        dk0_l.append(dk[:64])
        dk1_l.append(dk[64:])
        dv = B[s] * dr
        dv0_l.append(dv[:64])
        dv1_l.append(dv[64:])
        db0_l.append(db[:64])
        db1_l.append(db[64:])
    cat = lambda parts: jnp.concatenate(parts, axis=0)
    dq, dk0, dk1, dv0, dv1 = cat(dq_l), cat(dk0_l), cat(dk1_l), cat(dv0_l), cat(dv1_l)
    db0, db1, dg = cat(db0_l), cat(db1_l), cat(dg_l)

    def unit_back(d, n, rn):
        return rn * (d - n * jnp.sum(d * n, axis=-1, keepdims=True))

    d_act = jnp.concatenate(
        [unit_back(dq * DK ** (-0.5), qn, rq), unit_back(dk0, k0, r0), unit_back(dk1, k1, r1), dv0, dv1],
        axis=1,
    )
    d_mix = d_act * (sig * (1.0 + mix * (1.0 - sig)))
    for j in range(4):
        small_ref[j : j + 1, 0:640] += jnp.sum(d_mix * buf[5 + j : 5 + j + GB], axis=0, keepdims=True)
    dbuf[0:GB] = d_mix
    d_pre = taps[3:4] * d_mix
    for j in range(3):
        d_pre = d_pre + taps[j : j + 1] * dbuf[3 - j : 3 - j + GB]
    dbuf[GB : GB + 8] = d_mix[0:8]

    d_al = -dg * eg * jax.nn.sigmoid(al) * keep
    d_b0 = db0 * keep * sig0 * (1.0 - sig0)
    d_b1 = db1 * keep * sig1 * (1.0 - sig1)
    lanes = iota((GB, 128), 1)
    d_sm = jnp.where(lanes == 0, d_b0, jnp.where(lanes == 1, d_b1, jnp.where(lanes == 2, d_al, 0.0)))
    small_ref[0:1, 640:768] += g_hg
    small_ref[1:2, 640:768] += jnp.broadcast_to(jnp.sum(dg * g1, axis=0, keepdims=True), (1, 128))
    small_ref[2:3, 640:768] += jnp.broadcast_to(jnp.sum(d_al, axis=0, keepdims=True), (1, 128))
    dall = jnp.concatenate([d_pre.astype(BF16), d_gl.astype(BF16), d_sm.astype(BF16)], axis=1)
    dall_ref[...] = dall
    if rep > 1:
        dall = jnp.where(lax.rem(place, rep) == 0, dall, jnp.zeros_like(dall))
    part_ref[...] = mm(dall, w_ref[:, 0:896], NT).astype(BF16)


def mixer_fwd(lengths, dlog, dbias, hid, gain, w, taps, hg, rep, heads):
    n = hid.shape[0]
    steps = n // GB
    spans = n // HALF
    sds = jax.ShapeDtypeStruct
    smem = pl.BlockSpec(memory_space=pltpu.SMEM)
    whole = lambda a: pl.BlockSpec(a.shape, lambda i: (0,) * a.ndim)
    rows = lambda width: pl.BlockSpec((GB, width), lambda i: (i, 0))
    sq = lambda r: pl.BlockSpec((GS, r, 128), lambda i: (i, 0, 0))
    outs = [
        (sds((n, 1024), BF16), rows(1024)),
        (sds((n, 1024), BF16), rows(1024)),
        (sds((n, 640), F32), rows(640)),
        (sds((n, 128), F32), rows(128)),
        (sds((n, 128), F32), rows(128)),
        (sds((n, 128), BF16), rows(128)),
        (sds((n, 128), F32), rows(128)),
        (sds((spans, 128, 128), F32), sq(128)),
        (sds((spans, 128, 128), F32), sq(128)),
        (sds((spans, 128, 128), F32), sq(128)),
        (sds((spans, 128, 128), F32), sq(128)),
        (sds((spans, 64, 128), F32), sq(64)),
        (sds((spans, 128, 128), F32), sq(128)),
    ]
    return pl.pallas_call(
        functools.partial(fwd_kernel, rep, heads),
        grid=(steps,),
        in_specs=[smem, smem, smem, rows(1024), whole(gain), whole(w), whole(taps), whole(hg)],
        out_specs=[o[1] for o in outs],
        out_shape=[o[0] for o in outs],
        scratch_shapes=[pltpu.VMEM((8 + GB, 640), F32), pltpu.VMEM((128, 128), F32)],
        compiler_params=pltpu.CompilerParams(vmem_limit_bytes=48 * 1024 * 1024),
        cost_estimate=pl.CostEstimate(flops=4 * n * 1024 * 1024, bytes_accessed=16 * n * 1024, transcendentals=n * 2000),
        name="mixer_fwd",
    )(lengths, dlog, dbias, hid, gain, w, taps, hg)


def mixer_bwd(lengths, dlog, dbias, dbr, w, taps, hg, saved, rep, heads):
    pre, gl, sm, raw, t, wt, vn, nm, p, st = saved
    n = dbr.shape[0]
    steps = n // GB
    sds = jax.ShapeDtypeStruct
    smem = pl.BlockSpec(memory_space=pltpu.SMEM)
    whole = lambda a: pl.BlockSpec(a.shape, lambda i: (0,) * a.ndim)
    rows = lambda width: pl.BlockSpec((GB, width), lambda i: (steps - 1 - i, 0))
    sq = lambda r: pl.BlockSpec((GS, r, 128), lambda i: (steps - 1 - i, 0, 0))
    prev = pl.BlockSpec((8, 640), lambda i: (jnp.maximum((steps - 1 - i) * (GB // 8) - 1, 0), 0))
    return pl.pallas_call(
        functools.partial(bwd_kernel, rep, heads, steps),
        grid=(steps,),
        in_specs=[smem, smem, smem, rows(1024), whole(w), whole(taps), whole(hg), rows(640), prev, rows(128),
                  rows(128), rows(128), sq(128), sq(128), sq(128), sq(128), sq(64), sq(128)],
        out_specs=[rows(896), rows(1024), pl.BlockSpec((8, 768), lambda i: (0, 0))],
        out_shape=[sds((n, 896), BF16), sds((n, 1024), BF16), sds((8, 768), F32)],
        scratch_shapes=[pltpu.VMEM((8 + GB, 640), F32), pltpu.VMEM((GB + 8, 640), F32), pltpu.VMEM((128, 128), F32)],
        compiler_params=pltpu.CompilerParams(vmem_limit_bytes=48 * 1024 * 1024),
        cost_estimate=pl.CostEstimate(flops=4 * n * 1024 * 1024, bytes_accessed=16 * n * 1024, transcendentals=n * 2000),
        name="mixer_bwd",
    )(lengths, dlog, dbias, dbr, w, taps, hg, pre, pre, gl, sm, raw, t, wt, vn, nm, p, st)


MESH = pl.DeviceIdType.MESH


class Place:
    def __init__(self, ns, nb):
        self.ns, self.nb, self.nz = ns, nb, ns // 2
        self.s, self.b = lax.axis_index("seq"), lax.axis_index("batch")
        self.z, self.c = self.s // 2, lax.rem(self.s, 2)
        self.sib = self.s + 1 - 2 * self.c

    def chip(self, dz):
        return lax.rem(self.z + dz, self.nz)

    def chip_before(self, dz):
        return lax.rem(self.z + self.nz - dz, self.nz)

    def seq_at(self, ds):
        return lax.rem(self.s + ds, self.ns)

    def seq_before(self, ds):
        return lax.rem(self.s + self.ns - ds, self.ns)

    def batch_at(self, db):
        return lax.rem(self.b + db, self.nb)

    def batch_before(self, db):
        return lax.rem(self.b + self.nb - db, self.nb)


def enter(at):
    barrier = pltpu.get_barrier_semaphore()
    for ds in range(1, at.ns):
        pl.semaphore_signal(barrier, inc=1, device_id={"seq": at.seq_at(ds)}, device_id_type=MESH)
    for db in range(1, at.nb):
        pl.semaphore_signal(barrier, inc=1, device_id={"batch": at.batch_at(db)}, device_id_type=MESH)
    pl.semaphore_wait(barrier, at.ns + at.nb - 2)


def send(src, dst, send_sem, recv_sem, where):
    return pltpu.make_async_remote_copy(
        src_ref=src, dst_ref=dst, send_sem=send_sem, recv_sem=recv_sem, device_id=where, device_id_type=MESH
    )


class SeqGather:
    def __init__(self, at, src, out, ssem, rsem):
        self.at, self.out, self.ssem, self.rsem = at, out, ssem, rsem
        nz = at.nz
        self.far = [
            send(src, out.at[at.s], ssem.at[dz], rsem.at[dz], {"seq": 2 * at.chip(dz) + at.c}) for dz in range(1, nz)
        ]
        self.near = send(src, out.at[at.s], ssem.at[0], rsem.at[0], {"seq": at.sib})

    def start(self):
        for copy in self.far:
            copy.start()
        self.near.start()

    def finish(self):
        at, out, nz = self.at, self.out, self.at.nz
        onward = []
        for dz in range(1, nz):
            self.far[dz - 1].wait_recv()
            block = out.at[2 * at.chip_before(dz) + at.c]
            copy = send(block, block, self.ssem.at[nz - 1 + dz], self.rsem.at[nz - 1 + dz], {"seq": at.sib})
            copy.start()
            onward.append(copy)
        self.near.wait_recv()
        for copy in onward:
            copy.wait_recv()
        for copy in self.far + [self.near] + onward:
            copy.wait_send()


class SeqSum:
    def __init__(self, at, part, got, out, far, ssem, rsem):
        self.at, self.part, self.got, self.out, self.far = at, part, got, out, far
        self.pair = []
        self.hop = []
        for i, dz in enumerate(list(range(1, at.nz)) + [0]):
            z = at.chip(dz)
            self.pair.append(
                send(part.at[2 * z + 1 - at.c], got.at[dz], ssem.at[i], rsem.at[i], {"seq": at.sib})
            )
            if dz:
                self.hop.append(
                    send(out.at[dz], far.at[dz], ssem.at[at.nz + i], rsem.at[at.nz + i], {"seq": 2 * z + at.c})
                )

    def start(self):
        for copy in self.pair:
            copy.start()

    def forward(self):
        at = self.at
        for i in range(at.nz - 1):
            dz = i + 1
            self.pair[i].wait_recv()
            mine = self.part[2 * at.chip(dz) + at.c].astype(F32)
            self.out[dz] = (mine + self.got[dz].astype(F32)).astype(BF16)
            self.hop[i].start()
        self.pair[at.nz - 1].wait_recv()

    def finish(self):
        at = self.at
        total = self.part[2 * at.z + at.c].astype(F32) + self.got[0].astype(F32)
        for copy in self.hop:
            copy.wait_recv()
        for dz in range(1, at.nz):
            total = total + self.far[dz].astype(F32)
        for copy in self.pair + self.hop:
            copy.wait_send()
        return total


def gather_kernel(ns, nb, hid, wmix, wff, hid_out, wm_out, ff_out, lsem, hs, hr, ws, wr, fs, fr):
    at = Place(ns, nb)
    enter(at)
    local = [
        pltpu.make_async_copy(hid, hid_out.at[at.s], lsem.at[0]),
        pltpu.make_async_copy(wmix.at[at.s], wm_out.at[at.s, at.b], lsem.at[1]),
        pltpu.make_async_copy(wff.at[at.b], ff_out.at[:, at.b], lsem.at[2]),
    ]
    for copy in local:
        copy.start()
    spread = [
        send(wmix.at[at.seq_at(ds)], wm_out.at[at.s, at.b], ws.at[ds], wr.at[ds], {"seq": at.seq_at(ds)})
        for ds in range(1, ns)
    ]
    for copy in spread:
        copy.start()
    rows = SeqGather(at, hid, hid_out, hs, hr)
    rows.start()
    onward = []
    for ds in range(ns):
        if ds:
            spread[ds - 1].wait_recv()
        origin = at.seq_before(ds)
        block = wm_out.at[origin, at.b]
        for db in range(1, nb):
            k = ns + ds * (nb - 1) + db - 1
            copy = send(wmix.at[at.s] if ds == 0 else block, block, ws.at[k], wr.at[k], {"batch": at.batch_at(db)})
            copy.start()
            onward.append(copy)
    cols = [
        send(wff.at[at.batch_at(db)], ff_out.at[:, at.b], fs.at[db], fr.at[db], {"batch": at.batch_at(db)})
        for db in range(1, nb)
    ]
    for copy in cols:
        copy.start()
    rows.finish()
    for copy in onward + cols:
        copy.wait_recv()
    for copy in spread + onward + cols:
        copy.wait_send()
    for copy in local:
        copy.wait()


def mid_kernel(ns, nb, part, hid, cot, gain, after, nm_out, cot_out, got, out, far, nm, lsem, qs, qr, ns_, nr, cs, cr):
    at = Place(ns, nb)
    enter(at)
    rows = SeqSum(at, part, got, out, far, qs, qr)
    rows.start()
    mine = pltpu.make_async_copy(cot, cot_out.at[at.b], lsem.at[0])
    mine.start()
    cots = [
        send(cot, cot_out.at[at.b], cs.at[db], cr.at[db], {"batch": at.batch_at(db)}) for db in range(1, nb)
    ]
    for copy in cots:
        copy.start()
    rows.forward()
    total = rows.finish() + hid[...].astype(F32)
    after[...] = total
    r = lax.rsqrt(jnp.mean(total * total, axis=-1, keepdims=True) + EPS)
    nm[...] = (total * r * gain[...]).astype(BF16)
    own = pltpu.make_async_copy(nm, nm_out.at[at.b], lsem.at[1])
    own.start()
    mids = [send(nm, nm_out.at[at.b], ns_.at[db], nr.at[db], {"batch": at.batch_at(db)}) for db in range(1, nb)]
    for copy in mids:
        copy.start()
    for copy in mids + cots:
        copy.wait_recv()
    for copy in mids + cots:
        copy.wait_send()
    mine.wait()
    own.wait()


def turn_kernel(
    ns, nb, pmid, pout, after, cot, gain,
    block_out, d_stream, dbr_out, gfeed,
    got_m, got_o, dbr, lsem, ms, mr, os_, or_, gs, gr,
):
    at = Place(ns, nb)
    enter(at)
    mids = [
        send(pmid.at[at.batch_at(db)], got_m.at[db], ms.at[db], mr.at[db], {"batch": at.batch_at(db)})
        for db in range(1, nb)
    ]
    outs = [
        send(pout.at[at.batch_at(db)], got_o.at[db], os_.at[db], or_.at[db], {"batch": at.batch_at(db)})
        for db in range(1, nb)
    ]
    for copy in mids + outs:
        copy.start()
    x = after[...]
    d_mid = pmid[at.b].astype(F32)
    for copy in mids:
        copy.wait_recv()
    for db in range(1, nb):
        d_mid = d_mid + got_m[db].astype(F32)
    r = lax.rsqrt(jnp.mean(x * x, axis=-1, keepdims=True) + EPS)
    y = x * r
    gfeed[...] = jnp.sum(d_mid * y, axis=0, keepdims=True)
    dy = d_mid * gain[...]
    ds_ = cot[...].astype(F32) + r * (dy - y * jnp.mean(dy * y, axis=-1, keepdims=True))
    d_stream[...] = ds_
    dbr[...] = ds_.astype(BF16)
    own = pltpu.make_async_copy(dbr, dbr_out.at[at.s], lsem.at[0])
    own.start()
    rows = SeqGather(at, dbr, dbr_out, gs, gr)
    rows.start()
    for copy in outs:
        copy.wait_recv()
    total = after[...] + pout[at.b].astype(F32)
    for db in range(1, nb):
        total = total + got_o[db].astype(F32)
    block_out[...] = total.astype(BF16)
    rows.finish()
    for copy in mids + outs:
        copy.wait_send()
    own.wait()


def last_kernel(
    ns, nb, rep,
    part, grads, gout, smalls, hid, gain, d_stream, gfeed,
    grad_in, slots, gout_sum, small_all, vec_sum,
    got, out, far, got_g, piece, got_o, got_s, small_sum, got_v, vec, got_w,
    ready, lsem, qs, qr, gs, gr, ps, pr, os_, or_, ss, sr, us, ur, vs, vr, xs, xr,
):
    at = Place(ns, nb)
    nk, nq = ns // nb, slots.shape[0] // 6
    enter(at)
    for ds in range(1, ns):
        pl.semaphore_signal(ready, inc=1, device_id={"seq": at.seq_at(ds)}, device_id_type=MESH)
    rows = SeqSum(at, part, got, out, far, qs, qr)
    rows.start()
    over = []
    for k in range(nk):
        for db in range(1, nb):
            to = at.batch_at(db)
            i = k * nb + db
            over.append(send(grads.at[to + nb * k], got_g.at[i], gs.at[i], gr.at[i], {"batch": to}))
    outs = [
        send(gout.at[at.batch_at(db)], got_o.at[db], os_.at[db], or_.at[db], {"batch": at.batch_at(db)})
        for db in range(1, nb)
    ]
    small = [
        send(smalls, got_s.at[db], ss.at[db], sr.at[db], {"batch": at.batch_at(db)}) for db in range(1, nb)
    ]
    for copy in small + over + outs:
        copy.start()
    rows.forward()
    total = smalls[...]
    for copy in small:
        copy.wait_recv()
    for db in range(1, nb):
        total = total + got_s[db]
    small_sum[...] = total
    own = pltpu.make_async_copy(small_sum, small_all.at[at.s], lsem.at[0])
    own.start()
    heads = [
        send(small_sum, small_all.at[at.s], us.at[ds], ur.at[ds], {"seq": at.seq_at(ds)}) for ds in range(1, ns)
    ]
    for copy in heads:
        copy.start()
    for copy in over:
        copy.wait_recv()
    pl.semaphore_wait(ready, ns - 1)
    width = slots.shape[2]
    units = (at.s // nq, at.s, ns + at.s, at.s, ns + at.s, at.s // nq)
    placed = []
    for k in range(nk):
        row = at.b + nb * k
        acc = grads[row].astype(F32)
        for db in range(1, nb):
            acc = acc + got_g[k * nb + db].astype(F32)
        for m in range(6):
            block = acc[:, 128 * m : 128 * m + 128]
            if rep > 1:
                block = jnp.where(lax.rem(at.s, rep) == 0, block[:, :width], block[:, width:])
            piece[k * 6 + m] = block.astype(BF16)
            if m in (0, 5):
                owner, slot = at.s // nq, (0 if m == 0 else 5 * nq) + lax.rem(at.s, nq)
            else:
                unit_at = ((m - 1) % 2) * ns + at.s
                owner, slot = unit_at // (2 * nq), (nq if m < 3 else 3 * nq) + lax.rem(unit_at, 2 * nq)
            placed.append((piece.at[k * 6 + m], row, owner, slot, k * 6 + m))
    for src, row, owner, slot, i in placed:
        here = jnp.logical_and(row == at.s, owner == at.b)

        @pl.when(here)
        def _():
            pltpu.make_async_copy(src, slots.at[slot], pr.at[slot]).start()

        @pl.when(jnp.logical_not(here))
        def _():
            send(src, slots.at[slot], ps.at[i], pr.at[slot], {"seq": row, "batch": owner}).start()

    d_normed = rows.finish()
    x = hid[...].astype(F32)
    r = lax.rsqrt(jnp.mean(x * x, axis=-1, keepdims=True) + EPS)
    y = x * r
    vec[0:1] = jnp.sum(d_normed * y, axis=0, keepdims=True)
    vec[1:2] = gfeed[...]
    pair = [send(vec, got_v.at[db], vs.at[db], vr.at[db], {"batch": at.batch_at(db)}) for db in range(1, nb)]
    for copy in pair:
        copy.start()
    dy = d_normed * gain[...]
    grad_in[...] = (d_stream[...] + r * (dy - y * jnp.mean(dy * y, axis=-1, keepdims=True))).astype(BF16)
    for copy in outs:
        copy.wait_recv()
    acc = gout[at.b].astype(F32)
    for db in range(1, nb):
        acc = acc + got_o[db].astype(F32)
    gout_sum[...] = acc
    for copy in pair:
        copy.wait_recv()
    row_sum = vec[...]
    for db in range(1, nb):
        row_sum = row_sum + got_v[db]
    got_w[0] = row_sum
    wide = [
        send(got_w.at[0], got_w.at[ds], xs.at[ds], xr.at[ds], {"seq": at.seq_at(ds)}) for ds in range(1, ns)
    ]
    for copy in wide:
        copy.start()
    for copy in wide + heads:
        copy.wait_recv()
    row_sum = got_w[0]
    for ds in range(1, ns):
        row_sum = row_sum + got_w[ds]
    vec_sum[...] = row_sum
    for src, row, owner, slot, i in placed:
        here = jnp.logical_and(row == at.s, owner == at.b)

        @pl.when(jnp.logical_not(here))
        def _():
            send(src, slots.at[slot], ps.at[i], pr.at[slot], {"seq": row, "batch": owner}).wait_send()

    for slot in range(slots.shape[0]):
        pltpu.make_async_copy(piece.at[0], slots.at[slot], pr.at[slot]).wait()
    for copy in small + over + outs + heads + pair + wide:
        copy.wait_send()
    own.wait()


def comm_call(kernel, outs, scratch, ident, name, args, specs, flops=0):
    sds = jax.ShapeDtypeStruct
    return pl.pallas_call(
        kernel,
        in_specs=specs,
        out_specs=[o[1] for o in outs],
        out_shape=[o[0] for o in outs],
        scratch_shapes=scratch,
        compiler_params=pltpu.CompilerParams(
            collective_id=ident, has_side_effects=True, vmem_limit_bytes=48 * 1024 * 1024
        ),
        name=name,
    )(*args)


def dma(n):
    return pltpu.SemaphoreType.DMA((n,))


def on_device(
    hidden_in, cotangent, lengths, mixer_gain, query_weight, key_weight, value_weight, beta_weight, alpha_weight,
    gate_weight, out_weight, feed_gain, feed_gate, feed_up, feed_down, conv_taps, decay_log, decay_bias, head_gain,
):
    ns, nb = lax.axis_size("seq"), lax.axis_size("batch")
    heads = decay_log.shape[0]
    rep = ns // heads
    assert hidden_in.shape[0] == 1 and ns == rep * heads and ns % nb == 0
    tok, width = hidden_in.shape[1:]
    rows = query_weight.shape[0]
    share = feed_gate.shape[1] // nb
    halves = ns // nb
    sds = jax.ShapeDtypeStruct
    vmem, hbm = pl.BlockSpec(memory_space=pltpu.VMEM), pl.BlockSpec(memory_space=pl.ANY)
    hidden, cot = hidden_in[0], cotangent[0]

    small = jnp.concatenate(
        [
            jnp.swapaxes(beta_weight.reshape(rows, 2, heads), 1, 2),
            alpha_weight[:, :, None],
            jnp.broadcast_to(mixer_gain[:, None, None], (rows, heads, 1)),
            jnp.broadcast_to(feed_gain[:, None, None], (rows, heads, 1)),
            jnp.zeros((rows, heads, DK - 5), BF16),
        ],
        axis=-1,
    )
    mix = jnp.concatenate(
        [
            query_weight.reshape(rows, heads, 1, DK),
            jnp.swapaxes(key_weight.reshape(rows, 2, heads, DK), 1, 2),
            jnp.swapaxes(value_weight.reshape(rows, 2, heads, DK), 1, 2),
            gate_weight.reshape(rows, heads, 1, DK),
            small[:, :, None],
            out_weight.T.reshape(rows, heads, 1, DK),
        ],
        axis=2,
    )
    mix = jnp.repeat(jnp.swapaxes(mix, 0, 1).reshape(heads, rows, 8 * DK), rep, axis=0)
    feed = jnp.stack(
        [jnp.swapaxes(w.reshape(rows, nb, share), 0, 1) for w in (feed_gate, feed_up, feed_down.T)], axis=1
    )
    nz = ns // 2
    hid_all, wm, ff = comm_call(
        functools.partial(gather_kernel, ns, nb),
        [
            (sds((ns, tok, width), BF16), hbm),
            (sds((ns, nb, rows, 8 * DK), BF16), hbm),
            (sds((3, nb, rows, share), BF16), hbm),
        ],
        [dma(3), dma(2 * nz - 1), dma(2 * nz - 1), dma(ns * nb), dma(ns * nb), dma(nb), dma(nb)],
        0, "gather", (hidden, mix, feed), [vmem] * 3,
    )
    wm = wm.reshape(width, 8 * DK)
    ff = lax.all_gather(ff.reshape(3, nb * rows, share), "seq", axis=1, tiled=True)
    gains = wm[:, 6 * DK + 3 : 6 * DK + 5].astype(F32).T
    gain_in, gain_mid = gains[0:1], gains[1:2]
    gain_head = head_gain.astype(F32)[None]

    part, normed, pre, gl, sm, gated, raw, *maps = mixer_fwd(
        lengths, decay_log, decay_bias, hid_all.reshape(ns * tok, width), gain_in, wm, conv_taps, gain_head, rep, heads
    )
    block = lambda n, kind=BF16: pltpu.VMEM((n, tok, width), kind)
    after, nm_all, cot_all = comm_call(
        functools.partial(mid_kernel, ns, nb),
        [
            (sds((tok, width), F32), vmem),
            (sds((nb, tok, width), BF16), hbm),
            (sds((nb, tok, width), BF16), hbm),
        ],
        [block(nz), block(nz), block(nz), pltpu.VMEM((tok, width), BF16), dma(2), dma(2 * nz), dma(2 * nz)]
        + [dma(nb)] * 4,
        1, "mid", (part.reshape(ns, tok, width), hidden, cot, gain_mid), [vmem] * 4,
    )
    nm_all, cot_all = nm_all.reshape(nb * tok, width), cot_all.reshape(nb * tok, width)
    w_gate, w_up, w_down = ff[0], ff[1], ff[2]
    dot = lambda a, b, dims: lax.dot_general(a, b, dims, preferred_element_type=F32)
    gate_act = dot(nm_all, w_gate, NN)
    up_act = dot(nm_all, w_up, NN)
    sig = jax.nn.sigmoid(gate_act)
    act = (gate_act * sig * up_act).astype(BF16)
    d_act = dot(cot_all, w_down, NN)
    d_gate = (d_act * up_act * sig * (1.0 + gate_act * (1.0 - sig))).astype(BF16)
    d_up = (d_act * gate_act * sig).astype(BF16)
    pout = dot(act, w_down, NT).astype(BF16).reshape(nb, tok, width)
    pmid = (dot(d_gate, w_gate, NT) + dot(d_up, w_up, NT)).astype(BF16).reshape(nb, tok, width)
    block_out, d_stream, dbr_all, gfeed = comm_call(
        functools.partial(turn_kernel, ns, nb),
        [
            (sds((tok, width), BF16), vmem),
            (sds((tok, width), F32), vmem),
            (sds((ns, tok, width), BF16), hbm),
            (sds((1, width), F32), vmem),
        ],
        [block(nb), block(nb), pltpu.VMEM((tok, width), BF16), dma(1)] + [dma(nb)] * 4 + [dma(2 * nz - 1)] * 2,
        2, "turn", (pmid, pout, after, cot, gain_mid), [vmem] * 5,
    )
    dbr_all = dbr_all.reshape(ns * tok, width)
    g_gate, g_up = dot(nm_all, d_gate, TN), dot(nm_all, d_up, TN)
    g_down = dot(act, cot_all, TN)
    g_down = jnp.swapaxes(g_down.astype(BF16).reshape(halves, share // halves, nb, width // nb), 1, 2)
    over_seq = lambda g: lax.psum_scatter(g, "seq", scatter_dimension=0, tiled=True)
    g_gate = over_seq(g_gate.astype(BF16)).astype(F32)
    g_up = over_seq(g_up.astype(BF16)).astype(F32)
    g_down = over_seq(g_down.reshape(ns, share // halves, width // nb))[0]
    moves = [
        (s * nb + b, (b * halves + s // nb) * nb + s % nb) for s in range(ns) for b in range(nb)
    ]
    g_down = lax.ppermute(g_down, ("seq", "batch"), moves).astype(F32)

    dall, dnp, tap_sums = mixer_bwd(
        lengths, decay_log, decay_bias, dbr_all, wm, conv_taps, gain_head, (pre, gl, sm, raw, *maps), rep, heads
    )
    g_mix = dot(normed, dall, TN)
    g_out = dot(gated, dbr_all, TN)
    s_at = lax.axis_index("seq")
    if rep > 1:
        g_out = lax.dynamic_slice_in_dim(g_out, (s_at % rep) * (DK // rep), DK // rep, 0)
    g_out = jnp.swapaxes(g_out.astype(BF16).reshape(DK // rep, nb, width // nb), 0, 1)
    grads = g_mix[:, : 6 * DK].astype(BF16).reshape(ns, width // ns, 6 * DK)
    smalls = jnp.concatenate([tap_sums[:4], g_mix[:, 6 * DK : 6 * DK + 3].T.reshape(4, 6 * DK)], axis=0)
    nq = heads * rep // nb
    nk = ns // nb
    cw = DK // rep
    wrows = width // ns
    grad_in, slots, gout_sum, small_all, vec_sum = comm_call(
        functools.partial(last_kernel, ns, nb, rep),
        [
            (sds((tok, width), BF16), vmem),
            (sds((6 * nq, wrows, cw), BF16), vmem),
            (sds((DK // rep, width // nb), F32), vmem),
            (sds((ns, 8, 6 * DK), F32), vmem),
            (sds((2, width), F32), vmem),
        ],
        [
            block(nz), block(nz), block(nz),
            pltpu.VMEM((nk * nb, wrows, 6 * DK), BF16),
            pltpu.VMEM((nk * 6, wrows, cw), BF16),
            pltpu.VMEM((nb, DK // rep, width // nb), BF16),
            pltpu.VMEM((nb, 8, 6 * DK), F32),
            pltpu.VMEM((8, 6 * DK), F32),
            pltpu.VMEM((nb, 2, width), F32),
            pltpu.VMEM((2, width), F32),
            pltpu.VMEM((ns, 2, width), F32),
            pltpu.SemaphoreType.REGULAR,
            dma(1), dma(2 * nz), dma(2 * nz), dma(nk * nb), dma(nk * nb), dma(nk * 6), dma(6 * nq),
            dma(nb), dma(nb), dma(nb), dma(nb), dma(ns), dma(ns), dma(nb), dma(nb), dma(ns), dma(ns),
        ],
        3, "last",
        (dnp.reshape(ns, tok, width), grads, g_out, smalls, hidden, gain_in, d_stream, gfeed), [vmem] * 8,
    )
    def owned(first, count):
        return jnp.swapaxes(slots[first : first + count], 0, 1).reshape(wrows, count * cw).astype(F32)

    small_all = small_all[::rep]
    head_weight = small_all[:, 4:8].reshape(heads, 3, width)
    return (
        block_out[None],
        grad_in[None],
        vec_sum[0],
        owned(0, nq),
        owned(nq, 2 * nq),
        owned(3 * nq, 2 * nq),
        jnp.transpose(head_weight[:, :2], (2, 1, 0)).reshape(width, 2 * heads),
        head_weight[:, 2].T,
        owned(5 * nq, nq),
        gout_sum,
        vec_sum[1],
        g_gate,
        g_up,
        g_down,
        jnp.transpose(small_all[:, :4, : 5 * DK].reshape(heads, 4, 5, DK), (1, 2, 0, 3)).reshape(4, -1),
        small_all[:, 1, 5 * DK],
        small_all[:, 2, 5 * DK],
        jnp.sum(small_all[:, 0, 5 * DK :], axis=0),
    )


def solution(mesh):
    both = ("seq", "batch")
    tokens, split_rows, grid = P("batch", "seq", None), P(both, None), P("seq", "batch")
    return jax.shard_map(
        on_device,
        mesh=mesh,
        in_specs=(
            tokens, tokens, P("batch"), P(both), split_rows, split_rows, split_rows, split_rows, split_rows,
            split_rows, P(None, both), P(both), split_rows, split_rows, P(None, both), P(), P(), P(), P(),
        ),
        out_specs=(
            tokens, tokens, P(), grid, grid, grid, P(), P(), grid, grid, P(), grid, grid, grid, P(), P(), P(), P(),
        ),
        check_vma=False,
    )
```

time: 1540 us -> 364 us (0.24)
  other arithmetic: 457 us -> 3.1 us
  waiting for transfers between devices: 407 us -> 2.84 us
  blocking collectives: 262 us -> 0 us
  Pallas kernels: 0 us -> 247 us
  matrix products: 197 us -> 25.1 us
  local copies, waits for them, and re-layouts: 163 us -> 58 us
  starting transfers between devices: 21.7 us -> 5.41 us
    another operation x9 -> x1, other arithmetic: 324 us -> 0.07 us  [on_device(): jnp.stack([jnp.swapaxes(w.reshape(rows, nb, share), 0, 1) for w in (feed_...]
    all_gather x16 -> x1, waiting for transfers between devices: 309 us -> 0.01 us  [on_device(): lax.all_gather(ff.reshape(3, nb * rows, share), 'seq', axis=1, tiled=True)]
    pallas_call x0 -> x6, Pallas kernels: none -> 247 us  [the longest x4 188 us: comm_call(): pl.pallas_call(kernel, in_specs=specs, out_specs=[o[1] for o in outs], ou...]
    dot_general x80 -> x11, matrix products: 189 us -> 25.1 us  [on_device(): lax.dot_general(a, b, dims, preferred_element_type=F32)]
    all_gather x2 -> x0, blocking collectives: 124 us -> none  [the longest x1 66.5 us: on_device(): lax.all_gather(beta_weight, ('seq', 'batch'), axis=0, tiled=True)]
    psum x1 -> x0, waiting for transfers between devices: 87.2 us -> none  [on_device(): lax.psum((grad_mixer_gain, grad_beta_weight, grad_alpha_weight, grad_feed...]
    unnamed x11 -> x0, other arithmetic: 68.7 us -> none
    all_to_all x6 -> x0, blocking collectives: 56.5 us -> none  [the longest x1 12.7 us: on_device(): lax.all_to_all(d_gate, 'batch', split_axis=2, concat_axis=0, tiled=True)]
  transfers between devices with their start and end apart: 29 -> 5, of which waited for: 11 -> 1; matrix products, arithmetic and copies ran while one was open for 40% -> 10% of each run, Pallas kernels for 0% -> 59%
where the time goes in v1:
time: 364 us; the launch traced here: 357 us
  Pallas kernels  247 us (68%)
  local copies, waits for them, and re-layouts  58 us (16%)
  matrix products  25.1 us (7%)
  between operations  15.1 us (4%)
  starting transfers between devices  5.41 us (1%)
    pallas_call x4, Pallas kernels, comm_call(): pl.pallas_call(kernel, in_specs=specs, out_specs=[o[1] for o in outs], ou...  188 us
    unnamed x111, local copies, waits for them, and re-layouts  39.1 us
    pallas_call x1, Pallas kernels, mixer_bwd(): pl.pallas_call(functools.partial(bwd_kernel, rep, heads, steps), grid=(st...  34.1 us
    dot_general x11, matrix products, on_device(): lax.dot_general(a, b, dims, preferred_element_type=F32)  25.1 us
    pallas_call x1, Pallas kernels, mixer_fwd(): pl.pallas_call(functools.partial(fwd_kernel, rep, heads), grid=(steps,),...  24.6 us
  transfers between devices with their start and end apart: 5, of which 1 were waited for; matrix products, arithmetic and copies ran while one was open for 10% of the time, Pallas kernels for 59%

profile of v1, /device:TPU:7, one launch (start us, length us, event | category | flops | bytes accessed | tf_op | source)
XLA Modules:
  0.0 356.7 jit_solution(13659995868902118104)
XLA Ops:
  16.8 36.4 %gather.1 = (bf16[8,128,1024]{2,1,0:T(8,128)(2,1)S(1)}, bf16[8,4,32,1024]{3,2,1,0:T(8,128)(2,1)S(1)}, bf16[3,4,32,704]{3,2,1,0:T(8,128)(2,1)}) custom-call(bf16[128,1024]{1,0:T(8,128)(2,1)S(1)} %bitcast.143, bf16[8,32,1024]{2,1,0:T(8,128)(2,1)S(1)} %reshape_broadcast_in_dim_reshape.3.wmix, bf16[4,3,32,704]{3,2,1,0:T(8,128)(2,1)S(1)} %pad_maximum_fusion.wff), custom_call_target="tpu_custom_call" | custom-call | tf_op jit(solution)/shard_map/gather/pallas_call | solution.py:794
  55.8 24.6 %mixer_fwd.1 = (bf16[1024,1024]{1,0:T(8,128)(2,1)}, bf16[1024,1024]{1,0:T(8,128)(2,1)}, f32[1024,640]{1,0:T(8,128)}, f32[1024,128]{1,0:T(8,128)S(1)}, f32[1024,1...) custom-call(s32[1]{0:T(128)S(6)} %copy.160.len_ref, ...), custom_call_target="tpu_custom_call" | custom-call | flops 4294967296 | bytes 16777216 | tf_op jit(solution)/shard_map/mixer_fwd/pallas_call | solution.py:396
  86.4 1.6 copy-done.4
  88.0 51.3 %mid.1 = (f32[128,1024]{1,0:T(8,128)S(1)}, bf16[4,128,1024]{2,1,0:T(8,128)(2,1)S(1)}, bf16[4,128,1024]{2,1,0:T(8,128)(2,1)S(1)}) custom-call(bf16[8,128,1024]{2,1,0:T(8,128)(2,1)S(1)} %bitcast.147, bf16[128,1024]{1,0:T(8,128)(2,1)S(1)} %bitcast.144, bf16[128,1024]{1,0:T(8,128)(2,1)S(1)} %bitcast.151, f32[1,1024]{1,0:T(1,128)S(1)} %get-tuple-element.145.gain), custom_call_target="tpu_custom_call" | custom-call | tf_op jit(solution)/shard_map/mid/pallas_call | solution.py:794
  140.1 2.5 fusion
  143.8 2.7 multiply_convert_fusion
  147.4 2.1 convolution_convert_fusion.2
  149.5 4.0 %reshape.162 = bf16[2,352,4,256]{3,2,1,0:T(4,128)(2,1)} reshape(bf16[704,1024]{1,0:T(8,128)(2,1)} %convolution_convert_fusion.2) | data formatting | bytes 2883584 | tf_op jit(solution)/shard_map/reshape | solution.py:910
  153.5 2.8 copy.123
  156.4 2.0 convolution_convert_fusion.1
  158.4 2.6 copy.130
  161.3 2.0 convolution_convert_fusion
  163.4 2.7 copy.132
  166.0 2.4 fusion.2
  168.5 2.5 add_convert_fusion
  171.1 2.5 convolution_convert_fusion.3
  173.7 48.4 %turn.1 = (bf16[128,1024]{1,0:T(8,128)(2,1)S(1)}, f32[128,1024]{1,0:T(8,128)S(1)}, bf16[8,128,1024]{2,1,0:T(8,128)(2,1)S(1)}, f32[1,1024]{1,0:T(1,128)S(1)}) custom-call(bf16[4,128,1024]{2,1,0:T(8,128)(2,1)S(1)} %bitcast.149, bf16[4,128,1024]{2,1,0:T(8,128)(2,1)S(1)} %bitcast.150, f32[128,1024]{1,0:T(8,128)S(1)} %copy-done.22, ...), custom_call_target="tpu_custom_call" | custom-call | tf_op jit(solution)/shard_map/turn/pallas_call | solution.py:794
  224.9 1.8 copy.115
  234.4 34.1 %mixer_bwd.1 = (bf16[1024,896]{1,0:T(8,128)(2,1)}, bf16[1024,1024]{1,0:T(8,128)(2,1)}, f32[8,768]{1,0:T(8,128)S(1)}) custom-call(s32[1]{0:T(128)S(6)} %copy.160.len_ref, f32[8]{0:T(128)S(1)} %copy-done.30, f32[8]{0:T(128)S(1)} %copy-done.31, bf16[1024,1024]{1,0:T(8,128)(2,1)} %bitcast.138, bf16[1024,1024]{1,0:T(8,128)(2,1)} %bitcast.142, ...), custom_call_target="tpu_custom_call" | custom-call | flops 4294967296 | bytes 16777216 | tf_op jit(solution)/shard_map/mixer_bwd/pallas_call | solution.py:419
  268.6 4.0 %fusion.6 = f32[1024,896]{1,0:T(8,128)S(1)} fusion(bf16[1024,1024]{1,0:T(8,128)(2,1)S(1)} %copy-done.45, bf16[1024,896]{1,0:T(8,128)(2,1)} %get-tuple-element.70), kind=kOutput, calls=%fused_computation.42 | convolution fusion | flops 1879048192 | bytes 7602176 | tf_op jit(solution)/shard_map/dot_general | solution.py:886
  273.8 1.6 copy-done.3
  275.4 52.2 %last.1 = (bf16[128,1024]{1,0:T(8,128)(2,1)S(1)}, bf16[12,128,128]{2,1,0:T(8,128)(2,1)S(1)}, f32[128,256]{1,0:T(8,128)S(1)}, f32[8,8,768]{2,1,0:T(8,128)S(1)}, f32[2,1024]{1,0:T(2,128)S(1)}) custom-call(bf16[8,128,1024]{2,1,0:T(8,128)(2,1)S(1)} %bitcast.146, bf16[8,128,768]{2,1,0:T(8,128)(2,1)S(1)} %bitcast.139, bf16[4,128,256]{2,1,0:T(8,128)(2,1)S(1)} %bitcast.148, ...), custom_call_target="tpu_custom_call" | custom-call | tf_op jit(solution)/shard_map/last/pallas_call | solution.py:794
  335.4 4.8 %collective-permute-start = (bf16[352,256]{1,0:T(8,128)(2,1)}, bf16[352,256]{1,0:T(8,128)(2,1)S(1)}, u32[]{:S(2)}, u32[]{:S(2)}) collective-permute-start(bf16[352,256]{1,0:T(8,128)(2,1)} %bitcast.193), channel_id=1, source_target_pairs={{0,0},{1,8},{2,16},{3,24},{4,1},{5,9},{6,17},{7,25},{8,2},{9,10},{... | collective-permute-start | bytes 540680 | tf_op jit(solution)/shard_map/ppermute | solution.py:918
  344.6 2.8 collective-permute-done
  (171 shorter events, 47.1 us)
Async XLA Ops:
  7.2 6.5 %copy-start.36 = (bf16[32,2048]{1,0:T(8,128)(2,1)S(1)}, bf16[32,2048]{1,0:T(8,128)(2,1)}, u32[]{:S(2)}) copy-start(bf16[32,2048]{1,0:T(8,128)(2,1)} %param.24) | copy-start | bytes 393220
  7.2 6.5 %copy-start.37 = (bf16[32,2048]{1,0:T(8,128)(2,1)S(1)}, bf16[32,2048]{1,0:T(8,128)(2,1)}, u32[]{:S(2)}) copy-start(bf16[32,2048]{1,0:T(8,128)(2,1)} %param.25) | copy-start | bytes 393220
  7.2 132.8 %all-gather.2.cloned.1.call-start = ((), (), s32[]{:S(2)}) async-start(), calls=%async_computation.3 | async-start | bytes 5308416 | tf_op jit(solution)/shard_map/all_gather | solution.py:864
  16.8 39.0 %copy-start.39 = (bf16[128]{0:T(256)(128)(2,1)S(1)}, bf16[128]{0:T(256)(128)(2,1)}, u32[]{:S(2)}) copy-start(bf16[128]{0:T(256)(128)(2,1)} %param.37) | copy-start | bytes 772
  16.8 39.0 %copy-start.29 = (bf16[4,5120]{1,0:T(4,128)(2,1)S(1)}, bf16[4,5120]{1,0:T(4,128)(2,1)}, u32[]{:S(2)}) copy-start(bf16[4,5120]{1,0:T(4,128)(2,1)} %taps_ref.3) | copy-start | bytes 122884
  16.8 39.0 %copy-start.30 = (f32[8]{0:T(128)S(1)}, f32[8]{0:T(128)}, u32[]{:S(2)}) copy-start(f32[8]{0:T(128)} %dlog_ref.3) | copy-start | bytes 100
  16.8 39.0 %copy-start.31 = (f32[8]{0:T(128)S(1)}, f32[8]{0:T(128)}, u32[]{:S(2)}) copy-start(f32[8]{0:T(128)} %dbias_ref.3) | copy-start | bytes 100
  54.5 280.9 %reduce-scatter.8.cloned.1.call-start = ((), (), s32[]{:S(2)}) async-start(), calls=%async_computation.4 | async-start | bytes 1622016 | tf_op jit(solution)/shard_map/reduce_scatter | solution.py:911
  55.8 30.5 %copy-start.9 = (bf16[1,128,1024]{2,1,0:T(8,128)(2,1)S(1)}, bf16[1,128,1024]{2,1,0:T(8,128)(2,1)}, u32[]{:S(2)}) copy-start(bf16[1,128,1024]{2,1,0:T(8,128)(2,1)} %param.20) | copy-start | bytes 786436
  140.1 2.8 copy-start.38
  153.5 2.8 copy-start.43
  156.3 184.5 %reduce-scatter.10.cloned.1.call-start = ((), (), s32[]{:S(2)}) async-start(), calls=%async_computation.5 | async-start | bytes 1769472
  158.4 2.9 copy-start.40
  161.1 181.7 %reduce-scatter.12.cloned.1.call-start = ((), (), s32[]{:S(2)}) async-start(), calls=%async_computation.6 | async-start | bytes 1769472
  163.4 2.7 copy-start.44
  168.5 2.6 copy-start.42
  171.1 2.6 copy-start.10
  171.1 2.6 copy-start.22
  173.6 49.9 %copy-start.24 = (bf16[1024,128]{1,0:T(8,128)(2,1)S(1)}, bf16[1024,128]{1,0:T(8,128)(2,1)}, u32[]{:S(2)}) copy-start(bf16[1024,128]{1,0:T(8,128)(2,1)} %copy-done.23) | copy-start | bytes 786436
  223.5 3.2 copy-start
  234.4 34.1 %copy-start.45 = (bf16[1024,1024]{1,0:T(8,128)(2,1)S(1)}, bf16[1024,1024]{1,0:T(8,128)(2,1)}, u32[]{:S(2)}) copy-start(bf16[1024,1024]{1,0:T(8,128)(2,1)} %get-tuple-element.69) | copy-start | bytes 6291460
  333.3 14.8 %copy-start.26 = (bf16[128,1024]{1,0:T(8,128)(2,1)S(1)}, bf16[128,1024]{1,0:T(8,128)(2,1)}, u32[]{:S(2)}) copy-start(bf16[128,1024]{1,0:T(8,128)(2,1)} %copy-done.25) | copy-start | bytes 786436
  335.4 12.0 %collective-permute-start = (bf16[352,256]{1,0:T(8,128)(2,1)}, bf16[352,256]{1,0:T(8,128)(2,1)S(1)}, u32[]{:S(2)}, u32[]{:S(2)}) collective-permute-start(bf16[352,256]{1,0:T(8,128)(2,1)} %bitcast.193), channel_id=1, source_target_pairs={{0,0},{1,8},{2,16},{3,24},{4,1},{5,9},{6,17},{7,25},{8,2},{9,10},{... | collective-permute-start | bytes 540680 | tf_op jit(solution)/shard_map/ppermute | solution.py:918
  341.9 7.6 %copy-start.28 = (f32[128,256]{1,0:T(8,128)S(1)}, f32[128,256]{1,0:T(8,128)}, u32[]{:S(2)}) copy-start(f32[128,256]{1,0:T(8,128)} %copy-done.27) | copy-start | bytes 393220
  (27 other events, 29.9 us)
Sparse Core Ops, SparseCore 0:
  54.6 73.7 all-gather.1
  156.4 35.7 reduce-scatter.7
  194.5 42.8 reduce-scatter.9
  239.6 31.2 reduce-scatter.11

commit v2 on v0

v2 whole, which is shorter than its diff:
```python
import functools
import jax
import jax.numpy as jnp
from jax import lax
from jax.experimental import pallas as pl
from jax.experimental.pallas import tpu as pltpu
from jax.sharding import PartitionSpec as P

F32, BF16 = jnp.float32, jnp.bfloat16
EPS = 1e-05
DK = 128
HALF = 64
GS = 4
GB = GS * HALF
NN = (((1,), (0,)), ((), ()))
NT = (((1,), (1,)), ((), ()))
TN = (((0,), (0,)), ((), ()))


def mm(a, b, dims=NN):
    return lax.dot_general(a.astype(BF16), b.astype(BF16), dims, preferred_element_type=F32)


def split(a):
    hi = a.astype(BF16)
    return hi, (a - hi.astype(F32)).astype(BF16)


def mm3(a, b, dims=NN):
    (ah, al), (bh, bl) = (x if isinstance(x, tuple) else split(x) for x in (a, b))
    return (
        lax.dot_general(ah, bl, dims, preferred_element_type=F32)
        + lax.dot_general(al, bh, dims, preferred_element_type=F32)
    ) + lax.dot_general(ah, bh, dims, preferred_element_type=F32)


def iota(shape, axis):
    return lax.broadcasted_iota(jnp.int32, shape, axis)


def sub_masks():
    rows, cols = iota((128, 128), 0), iota((128, 128), 1)
    tr, tc = 2 * (rows & 63) + (rows >> 6), 2 * (cols & 63) + (cols >> 6)
    strict = tr > tc
    levels = []
    for bits in range(3, 7):
        same_up = (tr >> (bits + 1)) == (tc >> (bits + 1))
        levels.append(strict & same_up & ((tr >> bits) != (tc >> bits)))
    base = strict & ((tr >> 3) == (tc >> 3))
    return strict, base, levels


def unit(a):
    r = lax.rsqrt(jnp.sum(a * a, axis=-1, keepdims=True) + EPS)
    return a * r, r


def softplus(x):
    return jnp.maximum(x, 0.0) + jnp.log1p(jnp.exp(-jnp.abs(x)))


def lane(x, width=128):
    return jnp.broadcast_to(x, (x.shape[0], width))


def gates(sm, dec_bias):
    return jax.nn.sigmoid(sm[:, 0:1]), jax.nn.sigmoid(sm[:, 1:2]), sm[:, 2:3] + dec_bias


def span_decay(gb, tri):
    c = mm3(tri, gb)
    ct = jnp.transpose(jnp.concatenate([c, c], axis=0))[:64]
    e = jnp.exp(jnp.minimum(c - ct, 0.0))
    return c, e


def conv_mix(buf, taps):
    mix = taps[0:1] * buf[5 : 5 + GB]
    for j in range(1, 4):
        mix = mix + taps[j : j + 1] * buf[5 + j : 5 + j + GB]
    return mix


def head_taps(taps_ref, head, heads):
    parts = []
    for col in (head, heads + head, 2 * heads + head, 3 * heads + head, 4 * heads + head):
        parts.append(taps_ref[:, pl.ds(pl.multiple_of(col * 128, 128), 128)].astype(F32))
    return jnp.concatenate(parts, axis=1)


MESH = pl.DeviceIdType.MESH
SPAN_ROWS = 5 * 128 + HALF
SAVE_ROWS = GS * SPAN_ROWS + 3 * GB


class Place:
    def __init__(self, ns, nb):
        self.ns, self.nb, self.nz = ns, nb, ns // 2
        self.s, self.b = lax.axis_index("seq"), lax.axis_index("batch")
        self.z, self.c = self.s // 2, lax.rem(self.s, 2)
        self.sib = self.s + 1 - 2 * self.c

    def seq_at(self, ds):
        return lax.rem(self.s + ds, self.ns)

    def seq_before(self, ds):
        return lax.rem(self.s + self.ns - ds, self.ns)

    def peer(self, mask):
        out, bit = 0, 1
        while bit < self.nb:
            mine, other = lax.rem(self.b // bit, 2), lax.rem(mask // bit, 2) if not isinstance(mask, int) else mask // bit % 2
            out = out + bit * (mine + other - 2 * mine * other)
            bit *= 2
        return out

    def peers(self):
        return range(self.nb - 1, 0, -1)


def greet(at):
    barrier = pltpu.get_barrier_semaphore()
    for ds in range(1, at.ns):
        pl.semaphore_signal(barrier, inc=1, device_id={"seq": at.seq_at(ds)}, device_id_type=MESH)
    for m in at.peers():
        pl.semaphore_signal(barrier, inc=1, device_id={"batch": at.peer(m)}, device_id_type=MESH)


def enter(at):
    pl.semaphore_wait(pltpu.get_barrier_semaphore(), at.ns + at.nb - 2)


def send(src, dst, send_sem, recv_sem, where):
    return pltpu.make_async_remote_copy(
        src_ref=src, dst_ref=dst, send_sem=send_sem, recv_sem=recv_sem, device_id=where, device_id_type=MESH
    )


def fetch(pairs, sem):
    copies = [pltpu.make_async_copy(src, dst, sem.at[k]) for k, (src, dst) in enumerate(pairs)]
    for copy in copies:
        copy.start()
    return copies


class BatchGather:
    def __init__(self, at, src, out_at, ssem, rsem):
        self.copies = [
            send(src, out_at, ssem.at[m], rsem.at[m], {"batch": at.peer(m)}) for m in at.peers()
        ]

    def start(self):
        for copy in self.copies:
            copy.start()

    def finish(self):
        for copy in self.copies:
            copy.wait_recv()
        for copy in self.copies:
            copy.wait_send()


class SeqGather:
    def __init__(self, at, src, out, ssem, rsem):
        self.at, self.src, self.out, self.ssem, self.rsem = at, src, out, ssem, rsem

    def hop(self, t, up):
        at = self.at
        origin = at.z - (t - 1) if up else at.z + (t - 1)
        slot = 2 * origin + at.c
        src = self.src if t == 1 else self.out.at[slot]
        to = at.s + 2 if up else at.s - 2
        k = t if up else at.nz + t
        return send(src, self.out.at[slot], self.ssem.at[k], self.rsem.at[k], {"seq": to})

    def can_send(self, t, up):
        at = self.at
        if up:
            return jnp.logical_and(at.z - (t - 1) >= 0, at.z + 1 < at.nz)
        return jnp.logical_and(at.z + (t - 1) < at.nz, at.z >= 1)

    def can_recv(self, t, up):
        return self.at.z - t >= 0 if up else self.at.z + t < self.at.nz

    def across(self, t, up):
        at, nz = self.at, self.at.nz
        k = 2 * nz + (t if up else nz + t)
        origin = 0 if t == 0 else (-t if up else t)
        slot = 2 * (at.z + origin) + at.c
        src = self.src if t == 0 else self.out.at[slot]
        return send(src, self.out.at[slot], self.ssem.at[k], self.rsem.at[k], {"seq": at.sib})

    def start(self):
        for up in (True, False):
            pl.when(self.can_send(1, up))(lambda: self.hop(1, up).start())
        self.across(0, True).start()

    def forward(self, t):
        for up in (True, False):

            @pl.when(self.can_recv(t, up))
            def _():
                self.hop(t, up).wait_recv()
                if t + 1 < self.at.nz:
                    pl.when(self.can_send(t + 1, up))(lambda: self.hop(t + 1, up).start())
                self.across(t, up).start()

    def finish(self):
        self.across(0, True).wait()
        for t in range(1, self.at.nz):
            for up in (True, False):
                pl.when(self.can_recv(t, up))(lambda: self.across(t, up).wait())
                pl.when(self.can_send(t, up))(lambda: self.hop(t, up).wait_send())


class SeqSum:
    def __init__(self, at, part, got, out, far, sems):
        self.at, self.part, self.got, self.out, self.far = at, part, got, out, far
        self.pair_s, self.pair_r, self.hop_s, self.hop_r = sems

    def pair(self, i):
        at = self.at
        return send(self.part.at[i, 1 - at.c], self.got.at[i], self.pair_s.at[i], self.pair_r.at[i], {"seq": at.sib})

    def hop(self, i):
        at = self.at
        dz = lax.rem(i - at.z + at.nz, at.nz)
        return send(self.out.at[i], self.far.at[dz], self.hop_s.at[i], self.hop_r.at[dz], {"seq": 2 * i + at.c})

    def start(self, i):
        self.pair(i).start()

    def flush(self, i):
        self.pair(i).wait_recv()

        @pl.when(i != self.at.z)
        def _():
            mine = self.part[i, self.at.c].astype(F32)
            self.out[i] = (mine + self.got[i].astype(F32)).astype(BF16)
            self.hop(i).start()

    def finish(self):
        at = self.at
        total = self.part[at.z, at.c].astype(F32) + self.got[at.z].astype(F32)
        for dz in range(1, at.nz):
            send(self.out.at[0], self.far.at[dz], self.hop_s.at[0], self.hop_r.at[dz], {"seq": at.sib}).wait_recv()
            total = total + self.far[dz].astype(F32)
        return total

    def drain(self):
        for i in range(self.at.nz):
            self.pair(i).wait_send()
            pl.when(i != self.at.z)(lambda: self.hop(i).wait_send())


def norm_rows(x):
    return lax.rsqrt(jnp.mean(x * x, axis=-1, keepdims=True) + EPS)


def gather_kernel(
    ns, nb, rep, heads,
    hid, wq, wk, wv, wg, wo, beta, alpha, gain_in, gain_mid, fg, fu, fd,
    hid_out, wm_out, ff_out,
    hv, qv, kv, vv, gv, ov, fgv, fuv, fdv, wbuf, fbuf, isem, lsem, hs, hr, ws, wr, os_, or_, fs, fr,
):
    at = Place(ns, nb)
    greet(at)
    loads = fetch(
        [(hid, hv), (wq, qv), (wk, kv), (wv, vv), (wg, gv), (wo, ov), (fg, fgv), (fu, fuv), (fd, fdv)], isem
    )
    rows = beta.shape[0]
    lanes = iota((rows, 128), 1)
    eye = iota((rows, rows), 0) == iota((rows, rows), 1)
    column = lambda ref: jnp.sum(jnp.where(eye, ref[...].astype(F32), 0.0), axis=1, keepdims=True)
    be, al = beta[...].astype(F32), alpha[...].astype(F32)
    tail = jnp.where(lanes == 3, column(gain_in), jnp.where(lanes == 4, column(gain_mid), 0.0))
    share = fbuf.shape[3]
    for copy in loads[1:6]:
        copy.wait()
    for h in range(heads):
        col = lambda j: slice(128 * (j * heads + h), 128 * (j * heads + h) + 128)
        small = jnp.where(lanes == 0, be[:, h : h + 1], tail)
        small = jnp.where(lanes == 1, be[:, heads + h : heads + h + 1], small)
        small = jnp.where(lanes == 2, al[:, h : h + 1], small)
        parts = (
            qv[:, col(0)], kv[:, col(0)], kv[:, col(1)], vv[:, col(0)], vv[:, col(1)], gv[:, col(0)],
            small.astype(BF16), ov[:, col(0)],
        )
        for j, p in enumerate(parts):
            wbuf[h, :, 128 * j : 128 * j + 128] = p
    loads[0].wait()
    enter(at)

    def piece(to, where):
        return send(wbuf.at[to // rep], wm_out.at[at.s, at.b], ws.at[to], wr.at[at.s], where)

    def arrives(origin):
        send(wbuf.at[0], wm_out.at[origin, at.b], ws.at[0], wr.at[origin], {"seq": at.sib}).wait_recv()

    def pass_on(zo):
        for m in at.peers():
            both = wm_out.at[pl.ds(2 * zo, 2), at.b]
            send(both, both, os_.at[zo, m], or_.at[zo, m], {"batch": at.peer(m)}).start()

    def around(fn):
        for t in range(1, at.nz):
            pl.when(at.z + t < at.nz)(lambda: fn(at.z + t))
            pl.when(at.z - t >= 0)(lambda: fn(at.z - t))

    def scatter(zo):
        for core in range(2):
            piece(2 * zo + core, {"seq": 2 * zo + core}).start()

    own = pltpu.make_async_copy(wbuf.at[at.s // rep], wm_out.at[at.s, at.b], lsem.at[0])
    own.start()
    piece(at.sib, {"seq": at.sib}).start()
    around(scatter)
    line = SeqGather(at, hv, hid_out, hs, hr)
    line.start()
    place = pltpu.make_async_copy(hv, hid_out.at[at.s], lsem.at[1])
    place.start()
    arrives(at.sib)
    own.wait()
    pass_on(at.z)
    for copy in loads[6:]:
        copy.wait()
    for b in range(nb):
        for j, w in enumerate((fgv, fuv, fdv)):
            fbuf[b, j] = w[:, share * b : share * (b + 1)]
    kept = pltpu.make_async_copy(fbuf.at[at.b], ff_out.at[:, at.b], lsem.at[2])
    kept.start()
    cols = [
        send(fbuf.at[at.peer(m)], ff_out.at[:, at.b], fs.at[m], fr.at[m], {"batch": at.peer(m)}) for m in at.peers()
    ]

    def relay(zo):
        for core in range(2):
            arrives(2 * zo + core)
        pass_on(zo)

    for t in range(1, at.nz):
        pl.when(at.z + t < at.nz)(lambda: relay(at.z + t))
        pl.when(at.z - t >= 0)(lambda: relay(at.z - t))
        line.forward(t)
    for copy in cols:
        copy.start()
    line.finish()

    def settle(zo):
        for m in at.peers():
            both = wm_out.at[pl.ds(2 * zo, 2), at.b]
            send(both, both, os_.at[zo, m], or_.at[zo, m], {"batch": at.peer(m)}).wait()

    for zo in range(at.nz):
        settle(zo)
    piece(at.sib, {"seq": at.sib}).wait_send()

    def sent(zo):
        for core in range(2):
            piece(2 * zo + core, {"seq": 2 * zo + core}).wait_send()

    around(sent)
    for copy in cols:
        copy.wait()
    place.wait()
    kept.wait()


def front_kernel(
    ns, nb, rep, heads,
    len_ref, dlog_ref, dbias_ref, hid_hbm, w_hbm, taps_hbm, hg_ref, cot_hbm,
    normed_hbm, pre_hbm, gated_hbm, save_hbm, gains, after, nm_out, cot_out,
    hid_ref, w_ref, taps_ref, cot, nm, zero, save, preb, normedb, gatedb,
    buf, state, part, got, out, far, isem, bsem, lsem, osem, ps, pr, qs, qr, ms, mr, cs, cr,
):
    at = Place(ns, nb)
    greet(at)
    steps = at.nz
    loads = fetch([(w_hbm, w_ref), (taps_hbm, taps_ref), (cot_hbm, cot)], isem)

    def block_in(i):
        return pltpu.make_async_copy(hid_hbm.at[pl.ds(2 * i, 2)], hid_ref.at[pl.ds(2 * i, 2)], bsem.at[i])

    for i in range(steps):
        block_in(i).start()
    zero[...] = jnp.zeros_like(zero)
    for copy in loads:
        copy.wait()

    def saves(i):
        slot = lax.rem(i, 2)
        first = pl.multiple_of(i * GB, GB)
        here = pl.ds(first, GB)
        return [
            pltpu.make_async_copy(save.at[slot], save_hbm.at[i], osem.at[slot, 0]),
            pltpu.make_async_copy(preb.at[slot], pre_hbm.at[pl.ds(pl.multiple_of(first + 8, 8), GB)], osem.at[slot, 1]),
            pltpu.make_async_copy(normedb.at[slot], normed_hbm.at[here], osem.at[slot, 2]),
            pltpu.make_async_copy(gatedb.at[slot], gated_hbm.at[here], osem.at[slot, 3]),
        ]

    head = at.s // rep
    state[...] = jnp.zeros_like(state)
    buf[0:8] = jnp.zeros((8, 640), F32)
    gains[...] = jnp.transpose(w_ref[:, 768:896].astype(F32))[0:8]
    taps = head_taps(taps_ref, head, heads)
    hg = hg_ref[...].astype(F32)
    rows = SeqSum(at, part, got, out, far, (ps, pr, qs, qr))
    enter(at)
    mine = pltpu.make_async_copy(cot, cot_out.at[at.b], lsem.at[0])
    mine.start()
    edge = pltpu.make_async_copy(zero, pre_hbm.at[0:8], lsem.at[1])
    edge.start()
    cots = BatchGather(at, cot, cot_out.at[at.b], cs, cr)
    cots.start()

    def step(i, _):
        first = i * GB
        slot = lax.rem(i, 2)

        @pl.when(i >= 2)
        def _():
            for copy in saves(i - 2):
                copy.wait()

        def keep_map(kind, s, value):
            row = SPAN_ROWS * s + 128 * kind
            save[slot, row : row + value.shape[0]] = value

        def keep_rows(kind, value):
            row = SPAN_ROWS * GS + GB * kind
            save[slot, row : row + GB] = value

        block_in(i).wait()
        x = hid_ref[pl.ds(2 * i, 2)].reshape(GB, -1).astype(F32)
        normed = (x * norm_rows(x) * gains[3:4]).astype(BF16)
        normedb[slot] = normed
        proj = mm(normed, w_ref[:, 0:896])
        pre = proj[:, 0:640].astype(BF16).astype(F32)
        preb[slot] = pre
        gl, sm = proj[:, 640:768], proj[:, 768:896]
        keep_rows(0, gl)
        keep_rows(1, sm)
        buf[8 : 8 + GB] = pre
        mix = conv_mix(buf, taps)
        buf[0:8] = pre[GB - 8 : GB]
        act = mix * jax.nn.sigmoid(mix)
        q = unit(act[:, 0:128])[0] * DK ** (-0.5)
        k0, k1 = unit(act[:, 128:256])[0], unit(act[:, 256:384])[0]
        v0, v1 = act[:, 384:512], act[:, 512:640]
        keep = (first + iota((GB, 1), 0) < len_ref[0]).astype(F32)
        sig0, sig1, al = gates(sm, dbias_ref[head])
        b0, b1 = lane(sig0 * keep), lane(sig1 * keep)
        eg = jnp.exp(jnp.full((1, 1), dlog_ref[head], F32))
        g = lane(-eg * softplus(al) * keep)
        strict, base, levels = sub_masks()
        eye = (iota((128, 128), 0) == iota((128, 128), 1)).astype(F32)
        tri = (iota((64, 64), 0) >= iota((64, 64), 1)).astype(F32)
        causal = iota((64, 128), 0) >= (iota((64, 128), 1) & 63)
        K, Q, V, B, C, N, PM, Kc = [], [], [], [], [], [], [], []
        for s in range(GS):
            sl = slice(64 * s, 64 * s + 64)
            K.append(jnp.concatenate([k0[sl], k1[sl]], axis=0))
            V.append(jnp.concatenate([v0[sl], v1[sl]], axis=0))
            B.append(jnp.concatenate([b0[sl], b1[sl]], axis=0))
            Q.append(q[sl])
            c, e = span_decay(g[sl], tri)
            C.append(c)
            ee = jnp.concatenate([e, e], axis=0)
            gram = mm3(jnp.concatenate([K[s], Q[s]], axis=0), K[s], NT)
            N.append(jnp.where(strict, gram[:128] * ee, 0.0) * B[s])
            PM.append(jnp.where(causal, gram[128:] * e, 0.0))
            cc = jnp.concatenate([c, c], axis=0)
            Kc.append(jnp.exp(cc[63:64] - cc) * K[s])
            keep_map(3, s, N[s])
            keep_map(5, s, PM[s])
        n1 = [jnp.where(base, n, 0.0) for n in N]
        n1s = [split(n) for n in n1]
        n2 = [mm3(a, a) for a in n1s]
        n2s = [split(n) for n in n2]
        n3 = [mm3(a, b) for a, b in zip(n1s, n2s)]
        n4 = [mm3(a, a) for a in n2s]
        y = [eye - a + b - c for a, b, c in zip(n1, n2, n3)]
        X = [a + mm3(a, b) for a, b in zip(y, n4)]
        for lv in levels:
            xs = [split(x_) for x_ in X]
            bl = [jnp.where(lv, n, 0.0) for n in N]
            xb = [mm3(a, b) for a, b in zip(xs, bl)]
            X = [x_ - mm3(a, b) for x_, a, b in zip(X, xb, xs)]
        pl.when(i > 0)(lambda: rows.flush(i - 1))
        W, U = [], []
        for s in range(GS):
            cc = jnp.concatenate([C[s], C[s]], axis=0)
            rhs = jnp.concatenate([B[s] * jnp.exp(cc) * K[s], B[s] * V[s]], axis=1)
            wu = mm3(X[s], rhs)
            W.append(wu[:, :128])
            U.append(wu[:, 128:])
            keep_map(0, s, X[s])
            keep_map(1, s, W[s])
        S = state[...]
        raw = []
        Ws = [split(a) for a in W]
        Kcs = [split(a) for a in Kc]
        for s in range(GS):
            keep_map(4, s, S)
            ss = split(S)
            vn = U[s] - mm3(Ws[s], ss)
            keep_map(2, s, vn)
            vs = split(vn)
            raw.append(jnp.exp(C[s]) * mm3(Q[s], ss) + mm3(PM[s], vs))
            S = jnp.exp(C[s][63:64]) * S + mm3(Kcs[s], vs, TN)
        state[...] = S
        o = jnp.concatenate(raw, axis=0)
        keep_rows(2, o)
        gated = (o * norm_rows(o) * hg * (gl * jax.nn.sigmoid(gl))).astype(BF16)
        gatedb[slot] = gated
        for copy in saves(i):
            copy.start()
        if rep > 1:
            gated = jnp.where(lax.rem(at.s, rep) == 0, gated, jnp.zeros_like(gated))
        part[i] = mm(gated, w_ref[:, 896:1024], NT).astype(BF16).reshape(2, GB // 2, -1)
        rows.start(i)
        return 0

    lax.fori_loop(0, steps, step, 0)
    rows.flush(steps - 1)
    total = rows.finish() + hid_ref[at.s].astype(F32)
    after[...] = total
    nm[...] = (total * norm_rows(total) * gains[4:5]).astype(BF16)
    mids = BatchGather(at, nm, nm_out.at[at.b], ms, mr)
    mids.start()
    own = pltpu.make_async_copy(nm, nm_out.at[at.b], lsem.at[2])
    own.start()
    rows.drain()
    for i in (steps - 2, steps - 1):
        for copy in saves(i):
            copy.wait()
    cots.finish()
    mids.finish()
    mine.wait()
    edge.wait()
    own.wait()


def feed_kernel(
    ns, nb,
    nm_hbm, cot_hbm, ff_hbm, after, gains,
    block_out, d_stream, dbr_out, gfeed, sums,
    nm_all, cot_all, ff, acts, dgs, dus, pmid, pout, got_m, got_o, dbr, gbuf, gdown,
    isem, lsem, ms, mr, os_, or_, gs, gr, ds_s, dr_s,
):
    at = Place(ns, nb)
    greet(at)
    loads = fetch([(nm_hbm, nm_all), (cot_hbm, cot_all), (ff_hbm, ff)], isem)
    for copy in loads:
        copy.wait()
    tok = after.shape[0]
    share = ff.shape[2]
    enter(at)

    def mid_copy(m):
        to = at.peer(m)
        return send(pmid.at[to], got_m.at[m], ms.at[m], mr.at[m], {"batch": to})

    def out_copy(m):
        to = at.peer(m)
        return send(pout.at[to], got_o.at[m], os_.at[m], or_.at[m], {"batch": to})

    def both(ref, one, two):
        return jnp.concatenate([ref[one], ref[two]], axis=0)

    def pair(j, _):
        m = nb - 1 - 2 * j
        one, two = at.peer(m), at.peer(m - 1)
        x, d = both(nm_all, one, two), both(cot_all, one, two)
        ga, ua, da = mm(x, ff[0]), mm(x, ff[1]), mm(d, ff[2])
        sig = jax.nn.sigmoid(ga)
        act = (ga * sig * ua).astype(BF16)
        dg = (da * ua * sig * (1.0 + ga * (1.0 - sig))).astype(BF16)
        du = (da * ga * sig).astype(BF16)
        for ref, value in ((acts, act), (dgs, dg), (dus, du)):
            ref[one] = value[:tok]
            ref[two] = value[tok:]
        p = (mm(dg, ff[0], NT) + mm(du, ff[1], NT)).astype(BF16)
        pmid[one] = p[:tok]
        pmid[two] = p[tok:]
        mid_copy(m).start()
        pl.when(m > 1)(lambda: mid_copy(m - 1).start())
        return 0

    lax.fori_loop(0, nb // 2, pair, 0)

    def outs(j, _):
        m = nb - 1 - 2 * j
        one, two = at.peer(m), at.peer(m - 1)
        p = mm(both(acts, one, two), ff[2], NT).astype(BF16)
        pout[one] = p[:tok]
        pout[two] = p[tok:]
        out_copy(m).start()
        pl.when(m > 1)(lambda: out_copy(m - 1).start())
        return 0

    lax.fori_loop(0, nb // 2, outs, 0)
    x = after[...]
    d_mid = pmid[at.b].astype(F32)
    for m in at.peers():
        mid_copy(m).wait_recv()
        d_mid = d_mid + got_m[m].astype(F32)
    r = norm_rows(x)
    y = x * r
    gfeed[...] = jnp.sum(d_mid * y, axis=0, keepdims=True)
    dy = d_mid * gains[4:5]
    ds_ = cot_all[at.b].astype(F32) + r * (dy - y * jnp.mean(dy * y, axis=-1, keepdims=True))
    d_stream[...] = ds_
    dbr[...] = ds_.astype(BF16)
    line = SeqGather(at, dbr, dbr_out, gs, gr)
    line.start()
    own_rows = pltpu.make_async_copy(dbr, dbr_out.at[at.s], lsem.at[0])
    own_rows.start()
    halves = ns // nb
    deep, cols = share // halves, nm_all.shape[2] // ns
    flat = lambda ref: ref[...].reshape(nb * tok, -1)
    g = mm(flat(acts), flat(cot_all), TN).astype(BF16)
    for b in range(nb):
        for h in range(halves):
            for t in range(halves):
                gdown[b, h, deep * t : deep * (t + 1)] = g[
                    deep * h : deep * (h + 1), cols * (halves * b + t) : cols * (halves * b + t + 1)
                ]
    down = lambda b, h: sums.at[halves * b + h, pl.ds(2 * share, share)]
    moved = [
        send(gdown.at[at.peer(m), h], down(at.b, h), ds_s.at[m, h], dr_s.at[m, h], {"batch": at.peer(m)})
        for m in at.peers()
        for h in range(halves)
    ]
    for copy in moved:
        copy.start()
    kept = [
        pltpu.make_async_copy(gdown.at[at.b, h], down(at.b, h), lsem.at[1 + h]) for h in range(halves)
    ]
    line.forward(1)
    for k, left in enumerate((dgs, dus)):
        g = mm(flat(left), flat(nm_all), TN).astype(BF16)
        for i in range(ns):
            gbuf[k, i] = g[:, cols * i : cols * (i + 1)]
        kept.append(
            pltpu.make_async_copy(gbuf.at[k], sums.at[:, pl.ds(share * k, share)], lsem.at[1 + halves + k])
        )
        if k == 0:
            line.forward(2)
    for copy in kept:
        copy.start()
    for t in range(3, at.nz):
        line.forward(t)
    total = after[...] + pout[at.b].astype(F32)
    for m in at.peers():
        out_copy(m).wait_recv()
        total = total + got_o[m].astype(F32)
    block_out[...] = total.astype(BF16)
    line.finish()
    for copy in moved:
        copy.wait()
    for m in at.peers():
        mid_copy(m).wait_send()
        out_copy(m).wait_send()
    for copy in kept:
        copy.wait()
    own_rows.wait()


def back_kernel(
    ns, nb, rep, heads,
    len_ref, dlog_ref, dbias_ref, dbr_hbm, w_hbm, taps_hbm, hg_ref, normed_hbm, pre_hbm, gated_hbm, save_hbm,
    hid_hbm, gains, d_stream, gfeed,
    grad_in, slots, gout_sum, small_all, vec_sum,
    dbr_ref, w_ref, taps_ref, hid, save, buf, normedb, gatedb, isem, bsem,
    dbuf, dstate, small, gw, go, part, got, out, far, grads, gout, got_g, piece, got_o, got_s, got_v, vec, got_w,
    ready, ps, pr, qs, qr, gs, gr, bs, br, os_, or_, ss, sr, us, ur, vs_, vr, xs, xr,
):
    at = Place(ns, nb)
    greet(at)
    steps = at.nz
    loads = fetch([(w_hbm, w_ref), (taps_hbm, taps_ref), (hid_hbm, hid)], isem)

    def block_in(i):
        slot = lax.rem(i, 2)
        first = pl.multiple_of(i * GB, GB)
        here = pl.ds(first, GB)
        return [
            pltpu.make_async_copy(save_hbm.at[i], save.at[slot], bsem.at[slot, 0]),
            pltpu.make_async_copy(pre_hbm.at[pl.ds(first, 8 + GB)], buf.at[slot], bsem.at[slot, 1]),
            pltpu.make_async_copy(normed_hbm.at[here], normedb.at[slot], bsem.at[slot, 2]),
            pltpu.make_async_copy(gated_hbm.at[here], gatedb.at[slot], bsem.at[slot, 3]),
            pltpu.make_async_copy(dbr_hbm.at[pl.ds(2 * i, 2)], dbr_ref.at[slot], bsem.at[slot, 4]),
        ]

    for copy in block_in(steps - 1):
        copy.start()
    for copy in loads:
        copy.wait()
    head = at.s // rep
    dstate[...] = jnp.zeros_like(dstate)
    dbuf[GB : GB + 8] = jnp.zeros((8, 640), F32)
    small[...] = jnp.zeros_like(small)
    gw[...] = jnp.zeros_like(gw)
    go[...] = jnp.zeros_like(go)
    taps = head_taps(taps_ref, head, heads)
    hg = hg_ref[...].astype(F32)
    rows = SeqSum(at, part, got, out, far, (ps, pr, qs, qr))
    enter(at)
    for ds in range(1, ns):
        pl.semaphore_signal(ready, inc=1, device_id={"seq": at.seq_at(ds)}, device_id_type=MESH)

    def step(j, _):
        i = steps - 1 - j
        first = i * GB
        slot = lax.rem(i, 2)

        @pl.when(i > 0)
        def _():
            for copy in block_in(i - 1):
                copy.start()

        def kept_map(kind, s, high=128):
            row = SPAN_ROWS * s + 128 * kind
            return save[slot, row : row + high]

        def kept_rows(kind):
            row = SPAN_ROWS * GS + GB * kind
            return save[slot, row : row + GB]

        for copy in block_in(i):
            copy.wait()
        dbr = dbr_ref[slot].reshape(GB, -1)
        d_gated = mm(dbr, w_ref[:, 896:1024])
        gl, sm, o = kept_rows(0), kept_rows(1), kept_rows(2)
        sg = jax.nn.sigmoid(gl)
        rr = norm_rows(o)
        yn = o * rr
        dn = d_gated * (gl * sg)
        d_gl = d_gated * (yn * hg) * (sg * (1.0 + gl * (1.0 - sg)))
        dy = dn * hg
        d_raw = rr * (dy - yn * jnp.mean(yn * dy, axis=-1, keepdims=True))
        go[...] += mm(gatedb[slot], dbr, TN)

        mix = conv_mix(buf.at[slot], taps)
        sig = jax.nn.sigmoid(mix)
        act = mix * sig
        qn, rq = unit(act[:, 0:128])
        k0, r0 = unit(act[:, 128:256])
        k1, r1 = unit(act[:, 256:384])
        v0, v1 = act[:, 384:512], act[:, 512:640]
        q = qn * DK ** (-0.5)
        keep = (first + iota((GB, 1), 0) < len_ref[0]).astype(F32)
        sig0, sig1, al = gates(sm, dbias_ref[head])
        eg = jnp.exp(jnp.full((1, 1), dlog_ref[head], F32))
        g1 = -eg * softplus(al) * keep
        g = lane(g1)
        b0, b1 = lane(sig0 * keep), lane(sig1 * keep)
        strict, _, _ = sub_masks()
        tri = (iota((64, 64), 0) >= iota((64, 64), 1)).astype(F32)
        trit = (iota((64, 64), 0) <= iota((64, 64), 1)).astype(F32)
        causal = iota((64, 128), 0) >= (iota((64, 128), 1) & 63)
        K, Q, V, B, C, E, Kc, A1, A2, DO = [], [], [], [], [], [], [], [], [], []
        for s in range(GS):
            sl = slice(64 * s, 64 * s + 64)
            K.append(jnp.concatenate([k0[sl], k1[sl]], axis=0))
            V.append(jnp.concatenate([v0[sl], v1[sl]], axis=0))
            B.append(jnp.concatenate([b0[sl], b1[sl]], axis=0))
            Q.append(q[sl])
            c, e = span_decay(g[sl], tri)
            C.append(c)
            E.append(e)
            cc = jnp.concatenate([c, c], axis=0)
            Kc.append(jnp.exp(cc[63:64] - cc) * K[s])
            do = d_raw[sl]
            DO.append(do)
            A1.append(mm3(kept_map(5, s, HALF), do, TN))
            A2.append(mm3(jnp.exp(c) * Q[s], do, TN))
        dS = dstate[...]
        DV, DS = [None] * GS, [None] * GS
        for s in reversed(range(GS)):
            DS[s] = dS
            dvn = A1[s] + mm3(Kc[s], dS)
            DV[s] = dvn
            dS = jnp.exp(C[s][63:64]) * dS + A2[s] - mm3(kept_map(1, s), dvn, TN)
        dstate[...] = dS
        pl.when(j > 0)(lambda: rows.flush(i + 1))
        dq_l, dk0_l, dk1_l, dv0_l, dv1_l, db0_l, db1_l, dg_l = [], [], [], [], [], [], [], []
        for s in range(GS):
            vn, sst, n, p = kept_map(2, s), kept_map(4, s), kept_map(3, s), kept_map(5, s, HALF)
            vns = split(vn)
            ks = split(K[s])
            cc = jnp.concatenate([C[s], C[s]], axis=0)
            ec = jnp.exp(cc)
            ee = jnp.concatenate([E[s], E[s]], axis=0)
            dr = mm3(kept_map(0, s), DV[s], TN)
            both = split(jnp.concatenate([dr, DO[s]], axis=0))
            dd = mm3(both, vns, NT)
            dN = jnp.where(strict, -dd[:128], 0.0)
            dP = jnp.where(causal, dd[128:], 0.0)
            h = mm3(both, sst, NT)
            hk, hq = h[:128], h[128:]
            fh = dP * E[s]
            dq = ec[:64] * hq + mm3(fh, ks)
            dne = dN * ee
            dgm = dne * B[s]
            dkc = mm3(vns, DS[s], NT)
            ekc = jnp.exp(cc[63:64] - cc)
            dk = ekc * dkc - B[s] * ec * hk + mm3(fh, Q[s], TN) + mm3(dgm + jnp.transpose(dgm), ks)
            khk = jnp.sum(K[s] * hk, axis=-1, keepdims=True)
            ecl = ec[:, 0:1]
            db = (
                jnp.sum(dr * V[s], axis=-1, keepdims=True)
                - ecl * khk
                + jnp.sum(dne * mm3(ks, ks, NT), axis=-1, keepdims=True)
            )
            e1 = dN * n
            f1 = dP * p
            z = e1[:64, :64] + e1[:64, 64:] + e1[64:, :64] + e1[64:, 64:] + f1[:, :64] + f1[:, 64:]
            dc = jnp.sum(z - jnp.transpose(z), axis=-1, keepdims=True)
            dks = -B[s][:, 0:1] * ecl * khk
            hj = jnp.sum(Kc[s] * dkc, axis=-1, keepdims=True)
            dc = dc + dks[:64] + dks[64:] - hj[:64] - hj[64:]
            dc = dc + ec[:64, 0:1] * jnp.sum(Q[s] * hq, axis=-1, keepdims=True)
            dcl = jnp.sum(hj, axis=0, keepdims=True) + ec[63:64, 0:1] * jnp.sum(
                jnp.sum(sst * DS[s], axis=-1, keepdims=True), axis=0, keepdims=True
            )
            dg = mm3(trit, lane(dc)) + dcl
            dg_l.append(dg[:, 0:1])
            dq_l.append(dq)
            dk0_l.append(dk[:64])
            dk1_l.append(dk[64:])
            dv = B[s] * dr
            dv0_l.append(dv[:64])
            dv1_l.append(dv[64:])
            db0_l.append(db[:64])
            db1_l.append(db[64:])
        cat = lambda parts: jnp.concatenate(parts, axis=0)
        dq, dk0, dk1, dv0, dv1 = cat(dq_l), cat(dk0_l), cat(dk1_l), cat(dv0_l), cat(dv1_l)
        db0, db1, dg = cat(db0_l), cat(db1_l), cat(dg_l)

        def unit_back(d, n, rn):
            return rn * (d - n * jnp.sum(d * n, axis=-1, keepdims=True))

        d_act = jnp.concatenate(
            [unit_back(dq * DK ** (-0.5), qn, rq), unit_back(dk0, k0, r0), unit_back(dk1, k1, r1), dv0, dv1],
            axis=1,
        )
        d_mix = d_act * (sig * (1.0 + mix * (1.0 - sig)))
        for t in range(4):
            small[t : t + 1, 0:640] += jnp.sum(d_mix * buf[slot, 5 + t : 5 + t + GB], axis=0, keepdims=True)
        dbuf[0:GB] = d_mix
        d_pre = taps[3:4] * d_mix
        for t in range(3):
            d_pre = d_pre + taps[t : t + 1] * dbuf[3 - t : 3 - t + GB]
        dbuf[GB : GB + 8] = d_mix[0:8]
        d_al = -dg * eg * jax.nn.sigmoid(al) * keep
        d_b0 = db0 * keep * sig0 * (1.0 - sig0)
        d_b1 = db1 * keep * sig1 * (1.0 - sig1)
        lanes = iota((GB, 128), 1)
        d_sm = jnp.where(
            lanes == 0, d_b0, jnp.where(lanes == 1, d_b1, jnp.where(lanes == 2, d_al, 0.0))
        )
        small[0:1, 640:768] += jnp.sum(dn * yn, axis=0, keepdims=True)
        small[1:2, 640:768] += jnp.broadcast_to(jnp.sum(dg * g1, axis=0, keepdims=True), (1, 128))
        small[2:3, 640:768] += jnp.broadcast_to(jnp.sum(d_al, axis=0, keepdims=True), (1, 128))
        dall = jnp.concatenate([d_pre.astype(BF16), d_gl.astype(BF16), d_sm.astype(BF16)], axis=1)
        gw[...] += mm(normedb[slot], dall, TN)
        if rep > 1:
            dall = jnp.where(lax.rem(at.s, rep) == 0, dall, jnp.zeros_like(dall))
        part[i] = mm(dall, w_ref[:, 0:896], NT).astype(BF16).reshape(2, GB // 2, -1)
        rows.start(i)
        return 0

    lax.fori_loop(0, steps, step, 0)

    small[4:8] = jnp.transpose(gw[:, 768:896])[0:4]
    smalls = [send(small, got_s.at[m], ss.at[m], sr.at[m], {"batch": at.peer(m)}) for m in at.peers()]
    for copy in smalls:
        copy.start()
    nk, nq = ns // nb, slots.shape[0] // 6
    wrows = grads.shape[1]
    grads[...] = gw[:, 0:768].astype(BF16).reshape(ns, wrows, 768)
    over = []
    for k in range(nk):
        for m in at.peers():
            to = at.peer(m)
            n = k * nb + m
            over.append(send(grads.at[to + nb * k], got_g.at[n], gs.at[n], gr.at[n], {"batch": to}))
    for copy in over:
        copy.start()
    rows.flush(0)
    high, wide = gout.shape[1:]
    for b in range(nb):
        block = go[:, wide * b : wide * (b + 1)].astype(BF16)
        if rep > 1:
            block = jnp.where(lax.rem(at.s, rep) == 0, block[:high], block[high:])
        gout[b] = block
    outs = [send(gout.at[at.peer(m)], got_o.at[m], os_.at[m], or_.at[m], {"batch": at.peer(m)}) for m in at.peers()]
    for copy in outs:
        copy.start()
    total = small[...]
    for m, copy in zip(at.peers(), smalls):
        copy.wait_recv()
        total = total + got_s[m]
    small_all[at.s] = total
    heads_ = [
        send(small_all.at[at.s], small_all.at[at.s], us.at[ds], ur.at[ds], {"seq": at.seq_at(ds)})
        for ds in range(1, ns)
    ]
    for copy in heads_:
        copy.start()
    for copy in over:
        copy.wait_recv()
    pl.semaphore_wait(ready, ns - 1)
    width = slots.shape[2]
    placed = []
    for k in range(nk):
        row = at.b + nb * k
        acc = grads[row].astype(F32)
        for m in at.peers():
            acc = acc + got_g[k * nb + m].astype(F32)
        for m in range(6):
            block = acc[:, 128 * m : 128 * m + 128]
            if rep > 1:
                block = jnp.where(lax.rem(at.s, rep) == 0, block[:, :width], block[:, width:])
            piece[k * 6 + m] = block.astype(BF16)
            if m in (0, 5):
                owner, slot = at.s // nq, (0 if m == 0 else 5 * nq) + lax.rem(at.s, nq)
            else:
                unit_at = ((m - 1) % 2) * ns + at.s
                owner, slot = unit_at // (2 * nq), (nq if m < 3 else 3 * nq) + lax.rem(unit_at, 2 * nq)
            placed.append((row, owner, slot, k * 6 + m))

    def place(item):
        row, owner, slot, n = item
        src = piece.at[n]
        here = jnp.logical_and(row == at.s, owner == at.b)
        far_copy = lambda: send(src, slots.at[slot], bs.at[n], br.at[slot], {"seq": row, "batch": owner})
        near_copy = lambda: pltpu.make_async_copy(src, slots.at[slot], br.at[slot])
        return here, far_copy, near_copy

    for item in placed:
        here, far_copy, near_copy = place(item)
        pl.when(here)(lambda: near_copy().start())
        pl.when(jnp.logical_not(here))(lambda: far_copy().start())

    d_normed = rows.finish()
    x = hid[...].astype(F32)
    r = norm_rows(x)
    y = x * r
    vec[0:1] = jnp.sum(d_normed * y, axis=0, keepdims=True)
    vec[1:2] = gfeed[...]
    pairs = [send(vec, got_v.at[m], vs_.at[m], vr.at[m], {"batch": at.peer(m)}) for m in at.peers()]
    for copy in pairs:
        copy.start()
    dy = d_normed * gains[3:4]
    grad_in[...] = (d_stream[...] + r * (dy - y * jnp.mean(dy * y, axis=-1, keepdims=True))).astype(BF16)
    acc = gout[at.b].astype(F32)
    for m, copy in zip(at.peers(), outs):
        copy.wait_recv()
        acc = acc + got_o[m].astype(F32)
    gout_sum[...] = acc
    row_sum = vec[...]
    for m, copy in zip(at.peers(), pairs):
        copy.wait_recv()
        row_sum = row_sum + got_v[m]
    got_w[0] = row_sum
    spread = [send(got_w.at[0], got_w.at[ds], xs.at[ds], xr.at[ds], {"seq": at.seq_at(ds)}) for ds in range(1, ns)]
    for copy in spread:
        copy.start()
    for copy in spread + heads_:
        copy.wait_recv()
    row_sum = got_w[0]
    for ds in range(1, ns):
        row_sum = row_sum + got_w[ds]
    vec_sum[...] = row_sum
    for item in placed:
        here, far_copy, _ = place(item)
        pl.when(jnp.logical_not(here))(lambda: far_copy().wait_send())
    for slot in range(slots.shape[0]):
        pltpu.make_async_copy(piece.at[0], slots.at[slot], br.at[slot]).wait()
    for copy in smalls + over + outs + heads_ + pairs + spread:
        copy.wait_send()
    rows.drain()


def comm_call(kernel, outs, scratch, ident, name, args, specs, limit):
    return pl.pallas_call(
        kernel,
        in_specs=specs,
        out_specs=[o[1] for o in outs],
        out_shape=[o[0] for o in outs],
        scratch_shapes=scratch,
        compiler_params=pltpu.CompilerParams(
            collective_id=ident, has_side_effects=True, vmem_limit_bytes=limit * 1024 * 1024
        ),
        name=name,
    )(*args)


def dma(*shape):
    return pltpu.SemaphoreType.DMA(shape)


def on_device(
    hidden_in, cotangent, lengths, mixer_gain, query_weight, key_weight, value_weight, beta_weight, alpha_weight,
    gate_weight, out_weight, feed_gain, feed_gate, feed_up, feed_down, conv_taps, decay_log, decay_bias, head_gain,
):
    ns, nb = lax.axis_size("seq"), lax.axis_size("batch")
    heads = decay_log.shape[0]
    rep = ns // heads
    tok, width = hidden_in.shape[1:]
    assert hidden_in.shape[0] == 1 and ns == rep * heads and ns % nb == 0 and 2 * tok == GB
    rows = query_weight.shape[0]
    share = feed_gate.shape[1] // nb
    halves = ns // nb
    nz = ns // 2
    n = ns * tok
    sds = jax.ShapeDtypeStruct
    vmem, hbm = pl.BlockSpec(memory_space=pltpu.VMEM), pl.BlockSpec(memory_space=pltpu.HBM)
    smem = pl.BlockSpec(memory_space=pltpu.SMEM)
    hidden, cot = hidden_in[0], cotangent[0]
    buffer = lambda *shape: pltpu.VMEM(shape, BF16)
    block = lambda count: buffer(count, tok, width)
    wide = lambda *shape: pltpu.VMEM(shape, F32)
    vout = lambda kind, *shape: (sds(shape, kind), vmem)
    hout = lambda kind, *shape: (sds(shape, kind), hbm)
    key = heads * DK

    hid_all, wm, ff = comm_call(
        functools.partial(gather_kernel, ns, nb, rep, heads),
        [hout(BF16, ns, tok, width), hout(BF16, ns, nb, rows, 8 * DK), hout(BF16, 3, nb, rows, share)],
        [
            buffer(tok, width), buffer(rows, key), buffer(rows, 2 * key), buffer(rows, 2 * key), buffer(rows, key),
            buffer(rows, key), buffer(rows, nb * share), buffer(rows, nb * share), buffer(rows, nb * share),
            buffer(heads, rows, 8 * DK), buffer(nb, 3, rows, share), dma(9), dma(3), dma(4 * nz), dma(4 * nz), dma(ns),
            dma(ns), dma(nz, nb), dma(nz, nb), dma(nb), dma(nb),
        ],
        0, "gather",
        (
            hidden, query_weight, key_weight, value_weight, gate_weight, out_weight.T, beta_weight, alpha_weight,
            mixer_gain[None], feed_gain[None], feed_gate, feed_up, feed_down.T,
        ),
        [hbm] * 6 + [vmem] * 4 + [hbm] * 3, 62,
    )
    wm = wm.reshape(width, 8 * DK)
    ff = lax.all_gather(ff.reshape(3, nb * rows, share), "seq", axis=1, tiled=True)
    hg = head_gain[None]
    normed, pre, gated, save, gains, after, nm_all, cot_all = comm_call(
        functools.partial(front_kernel, ns, nb, rep, heads),
        [
            hout(BF16, n, width), hout(F32, n + 8, 5 * DK), hout(BF16, n, DK), hout(F32, nz, SAVE_ROWS, DK),
            vout(F32, 8, width), vout(F32, tok, width), hout(BF16, nb, tok, width), hout(BF16, nb, tok, width),
        ],
        [
            block(ns), buffer(width, 8 * DK), buffer(4, 5 * key), buffer(tok, width), buffer(tok, width),
            wide(8, 5 * DK), wide(2, SAVE_ROWS, DK), wide(2, GB, 5 * DK), buffer(2, GB, width), buffer(2, GB, DK),
            wide(8 + GB, 5 * DK), wide(DK, DK), buffer(nz, 2, tok, width), block(nz), block(nz), block(nz),
            dma(3), dma(nz), dma(3), dma(2, 4), dma(nz), dma(nz), dma(nz), dma(nz), dma(nb), dma(nb), dma(nb), dma(nb),
        ],
        1, "front",
        (lengths, decay_log, decay_bias, hid_all, wm, conv_taps, hg, cot),
        [smem] * 3 + [hbm] * 3 + [vmem, hbm], 61,
    )
    block_out, d_stream, dbr_all, gfeed, sums = comm_call(
        functools.partial(feed_kernel, ns, nb),
        [
            vout(BF16, tok, width), vout(F32, tok, width), hout(BF16, ns, tok, width), vout(F32, 1, width),
            hout(BF16, ns, 3 * share, width // ns),
        ],
        [
            block(nb), block(nb), buffer(3, width, share), buffer(nb, tok, share), buffer(nb, tok, share),
            buffer(nb, tok, share), block(nb), block(nb), block(nb), block(nb), buffer(tok, width),
            buffer(2, ns, share, width // ns), buffer(nb, halves, share, width // ns),
            dma(3), dma(3 + halves), dma(nb), dma(nb), dma(nb), dma(nb), dma(4 * nz), dma(4 * nz), dma(nb, halves),
            dma(nb, halves),
        ],
        2, "feed", (nm_all, cot_all, ff, after, gains), [hbm] * 3 + [vmem] * 2, 61,
    )
    sums = lax.psum_scatter(sums, "seq", scatter_dimension=0, tiled=False)
    g_down = jnp.swapaxes(sums[2 * share :].reshape(halves, share // halves, width // ns), 0, 1)
    g_down = g_down.reshape(share // halves, width // nb).astype(F32)

    nq = ns // nb
    nk = ns // nb
    cw = DK // rep
    wrows = width // ns
    grad_in, slots, gout_sum, small_all, vec_sum = comm_call(
        functools.partial(back_kernel, ns, nb, rep, heads),
        [
            vout(BF16, tok, width), vout(BF16, 6 * nq, wrows, cw), vout(F32, DK // rep, width // nb),
            vout(F32, ns, 8, width), vout(F32, 2, width),
        ],
        [
            buffer(2, 2, tok, width), buffer(width, 8 * DK), buffer(4, 5 * key), buffer(tok, width),
            wide(2, SAVE_ROWS, DK), wide(2, 8 + GB, 5 * DK), buffer(2, GB, width), buffer(2, GB, DK), dma(3), dma(2, 5),
            wide(GB + 8, 5 * DK), wide(DK, DK), wide(8, width), wide(width, 7 * DK),
            wide(DK, width), buffer(nz, 2, tok, width), block(nz), block(nz), block(nz),
            buffer(ns, wrows, 6 * DK), buffer(nb, DK // rep, width // nb), buffer(nk * nb, wrows, 6 * DK),
            buffer(nk * 6, wrows, cw), buffer(nb, DK // rep, width // nb), wide(nb, 8, width), wide(nb, 2, width),
            wide(2, width), wide(ns, 2, width), pltpu.SemaphoreType.REGULAR,
            dma(nz), dma(nz), dma(nz), dma(nz), dma(nk * nb), dma(nk * nb), dma(nk * 6), dma(6 * nq),
            dma(nb), dma(nb), dma(nb), dma(nb), dma(ns), dma(ns), dma(nb), dma(nb), dma(ns), dma(ns),
        ],
        3, "back",
        (
            lengths, decay_log, decay_bias, dbr_all, wm, conv_taps, hg, normed, pre, gated, save, hidden, gains,
            d_stream, gfeed,
        ),
        [smem] * 3 + [hbm] * 3 + [vmem] + [hbm] * 5 + [vmem] * 3, 61,
    )

    def owned(first, count):
        return jnp.swapaxes(slots[first : first + count], 0, 1).reshape(wrows, count * cw).astype(F32)

    small_all = small_all[::rep]
    return (
        block_out[None],
        grad_in[None],
        vec_sum[0],
        owned(0, nq),
        owned(nq, 2 * nq),
        owned(3 * nq, 2 * nq),
        jnp.transpose(small_all[:, 4:6], (2, 1, 0)).reshape(width, 2 * heads),
        small_all[:, 6].T,
        owned(5 * nq, nq),
        gout_sum,
        vec_sum[1],
        sums[:share].T.astype(F32),
        sums[share : 2 * share].T.astype(F32),
        g_down,
        jnp.transpose(small_all[:, :4, : 5 * DK].reshape(heads, 4, 5, DK), (1, 2, 0, 3)).reshape(4, -1),
        small_all[:, 1, 5 * DK],
        small_all[:, 2, 5 * DK],
        jnp.sum(small_all[:, 0, 5 * DK : 6 * DK], axis=0),
    )


def solution(mesh):
    both = ("seq", "batch")
    tokens, split_rows, grid = P("batch", "seq", None), P(both, None), P("seq", "batch")
    return jax.shard_map(
        on_device,
        mesh=mesh,
        in_specs=(
            tokens, tokens, P("batch"), P(both), split_rows, split_rows, split_rows, split_rows, split_rows,
            split_rows, P(None, both), P(both), split_rows, split_rows, P(None, both), P(), P(), P(), P(),
        ),
        out_specs=(
            tokens, tokens, P(), grid, grid, grid, P(), P(), grid, grid, P(), grid, grid, grid, P(), P(), P(), P(),
        ),
        check_vma=False,
    )
```

time: 1540 us -> 307 us (0.20)
  other arithmetic: 457 us -> 4.98 us
  waiting for transfers between devices: 407 us -> 12.5 us
  blocking collectives: 262 us -> 0 us
  Pallas kernels: 0 us -> 257 us
  matrix products: 197 us -> 0 us
  local copies, waits for them, and re-layouts: 163 us -> 15.4 us
  starting transfers between devices: 21.7 us -> 0.08 us
    another operation x9 -> x0, other arithmetic: 324 us -> none  [the longest x6 321 us: span_terms(): lax.linalg.triangular_solve(system, right_side, left_side=True, lower=Tru...]
    all_gather x16 -> x1, waiting for transfers between devices: 309 us -> 12.5 us  [on_device(): lax.all_gather(ff.reshape(3, nb * rows, share), 'seq', axis=1, tiled=True)]
    pallas_call x0 -> x4, Pallas kernels: none -> 257 us  [comm_call(): pl.pallas_call(kernel, in_specs=specs, out_specs=[o[1] for o in outs], ou...]
    dot_general x80 -> x0, matrix products: 189 us -> none  [the longest x10 29.6 us: project(): return jnp.dot(activation, weight, preferred_element_type=jnp.float32)]
    all_gather x2 -> x0, blocking collectives: 124 us -> none  [the longest x1 66.5 us: on_device(): lax.all_gather(beta_weight, ('seq', 'batch'), axis=0, tiled=True)]
    psum x1 -> x0, waiting for transfers between devices: 87.2 us -> none  [on_device(): lax.psum((grad_mixer_gain, grad_beta_weight, grad_alpha_weight, grad_feed...]
    unnamed x11 -> x0, other arithmetic: 68.7 us -> none
    all_to_all x6 -> x0, blocking collectives: 56.5 us -> none  [the longest x1 12.7 us: on_device(): lax.all_to_all(d_gate, 'batch', split_axis=2, concat_axis=0, tiled=True)]
  transfers between devices with their start and end apart: 29 -> 2, of which waited for: 11 -> 1; matrix products, arithmetic and copies ran while one was open for 40% -> 4% of each run, Pallas kernels for 0% -> 51%
where the time goes in v2:
time: 307 us; the launch traced here: 305 us
  Pallas kernels  257 us (84%)
  local copies, waits for them, and re-layouts  15.4 us (5%)
  between operations  14.8 us (5%)
  waiting for transfers between devices  12.5 us (4%)
  other arithmetic  4.98 us (2%)
    pallas_call x4, Pallas kernels, comm_call(): pl.pallas_call(kernel, in_specs=specs, out_specs=[o[1] for o in outs], ou...  257 us
    all_gather x1, waiting for transfers between devices, on_device(): lax.all_gather(ff.reshape(3, nb * rows, share), 'seq', axis=1, tiled=True)  12.5 us
    unnamed x21, local copies, waits for them, and re-layouts  9.26 us
  transfers between devices with their start and end apart: 2, of which 1 were waited for; matrix products, arithmetic and copies ran while one was open for 4% of the time, Pallas kernels for 51%

profile of v2, /device:TPU:7, one launch (start us, length us, event | category | flops | bytes accessed | tf_op | source)
XLA Modules:
  0.0 304.6 jit_solution(16690931300257279128)
XLA Ops:
  7.2 1.4 copy.54.beta
  8.6 1.4 copy.55.alpha
  10.0 41.8 %gather.1 = (bf16[8,128,1024]{2,1,0:T(8,128)(2,1)}, bf16[8,4,32,1024]{3,2,1,0:T(8,128)(2,1)}, bf16[3,4,32,704]{3,2,1,0:T(8,128)(2,1)}) custom-call(bf16[128,1024]{1,0:T(8,128)(2,1)} %bitcast.69, bf16[32,1024]{1,0:T(8,128)(2,1)} %wq.1, bf16[32,2048]{1,0:T(8,128)(2,1)} %wk.1, bf16[32,2048]{1,0:T(8,128)(2,1)} %wv.1, bf16[32,1024]{1,0:T(8,128)(2,1)} %wg.1, ...), custom_call_target="tpu_custom_call" | custom-call | tf_op jit(solution)/shard_map/gather/pallas_call | solution.py:989
  52.5 62.3 %front.1 = (bf16[1024,1024]{1,0:T(8,128)(2,1)}, f32[1032,640]{1,0:T(8,128)}, bf16[1024,128]{1,0:T(8,128)(2,1)}, f32[4,3584,128]{2,1,0:T(8,128)}, f32[8,1024]{1,0...) custom-call(s32[1]{0:T(128)S(6)} %copy.83.len_ref, f32[8]{0:T(128)} %dlog_ref.3, ...), custom_call_target="tpu_custom_call" | custom-call | tf_op jit(solution)/shard_map/front/pallas_call | solution.py:989
  114.8 12.5 %all-gather.2.cloned.1.call-done.ff_hbm = bf16[3,1024,704]{2,1,0:T(8,128)(2,1)} async-done(((bf16[3,128,704]{2,1,0:T(8,128)(2,1)}), bf16[3,1024,704]{2,1,0:T(8,128)(2,1)}) %all-gather.2.cloned.1.call-update) | async-done | bytes 4325392 | tf_op jit(solution)/shard_map/all_gather | solution.py:1048
  127.2 59.7 %feed.1 = (bf16[128,1024]{1,0:T(8,128)(2,1)}, f32[128,1024]{1,0:T(8,128)}, bf16[8,128,1024]{2,1,0:T(8,128)(2,1)}, f32[1,1024]{1,0:T(1,128)}, bf16[8,2112,128]{2,1,0:T(8,128)(2,1)}) custom-call(bf16[4,128,1024]{2,1,0:T(8,128)(2,1)} %get-tuple-element.41.nm_hbm, bf16[4,128,1024]{2,1,0:T(8,128)(2,1)} %get-tuple-element.42.cot_hbm, ...), custom_call_target="tpu_custom_call" | custom-call | tf_op jit(solution)/shard_map/feed/pallas_call | solution.py:989
  187.0 93.0 %back.1 = (bf16[128,1024]{1,0:T(8,128)(2,1)}, bf16[12,128,128]{2,1,0:T(8,128)(2,1)}, f32[128,256]{1,0:T(8,128)}, f32[8,8,1024]{2,1,0:T(8,128)}, f32[2,1024]{1,0:T(2,128)}) custom-call(s32[1]{0:T(128)S(6)} %copy.83.len_ref, f32[8]{0:T(128)} %dlog_ref.3, f32[8]{0:T(128)} %dbias_ref.3, bf16[8,128,1024]{2,1,0:T(8,128)(2,1)} %get-tuple-element.47.dbr_hbm, ...), custom_call_target="tpu_custom_call" | custom-call | tf_op jit(solution)/shard_map/back/pallas_call | solution.py:989
  280.0 1.0 slice.53
  281.1 0.9 slice.59
  282.6 1.0 slice_bitcast_fusion.2
  283.6 0.7 copy.78
  284.3 0.7 copy.76
  285.0 0.9 convert_bitcast_fusion.5
  286.0 0.8 copy.67
  286.8 0.8 copy.64
  287.8 0.8 copy.66
  288.7 0.8 copy.65
  289.6 1.3 slice_reduce_fusion
  290.9 1.5 slice_reduce_fusion.1
  293.0 2.0 fusion
  295.0 0.8 copy_bitcast_fusion
  295.7 0.7 copy.84
  296.4 0.7 copy.85
  297.2 0.7 copy.86
  (25 shorter events, 1.9 us)
Async XLA Ops:
  7.2 120.1 %all-gather.2.cloned.1.call-start = ((), (), s32[]{:S(2)}) async-start(), calls=%async_computation.1 | async-start | bytes 5308416 | tf_op jit(solution)/shard_map/all_gather | solution.py:1048
  51.8 241.2 %reduce-scatter.2.cloned.1.call-start = ((), (), s32[]{:S(2)}) async-start(), calls=%async_computation.2 | async-start | bytes 4866048 | tf_op jit(solution)/shard_map/reduce_scatter | solution.py:1081
  280.0 7.6 %copy-start = (bf16[12,128,128]{2,1,0:T(8,128)(2,1)S(1)}, bf16[12,128,128]{2,1,0:T(8,128)(2,1)}, u32[]{:S(2)}) copy-start(bf16[12,128,128]{2,1,0:T(8,128)(2,1)} %get-tuple-element.56) | copy-start | bytes 1179652
  282.6 9.8 %copy-start.4 = (f32[2,1024]{1,0:T(2,128)S(1)}, f32[2,1024]{1,0:T(2,128)}, u32[]{:S(2)}) copy-start(f32[2,1024]{1,0:T(2,128)} %get-tuple-element.55) | copy-start | bytes 24580
  286.8 8.9 %copy-start.1 = (bf16[128,1024]{1,0:T(8,128)(2,1)S(1)}, bf16[128,1024]{1,0:T(8,128)(2,1)}, u32[]{:S(2)}) copy-start(bf16[128,1024]{1,0:T(8,128)(2,1)} %get-tuple-element.46) | copy-start | bytes 786436
  287.6 8.9 %copy-start.2 = (bf16[128,1024]{1,0:T(8,128)(2,1)S(1)}, bf16[128,1024]{1,0:T(8,128)(2,1)}, u32[]{:S(2)}) copy-start(bf16[128,1024]{1,0:T(8,128)(2,1)} %get-tuple-element.54) | copy-start | bytes 786436
  287.6 9.5 %copy-start.3 = (f32[128,256]{1,0:T(8,128)S(1)}, f32[128,256]{1,0:T(8,128)}, u32[]{:S(2)}) copy-start(f32[128,256]{1,0:T(8,128)} %get-tuple-element.134) | copy-start | bytes 393220
Sparse Core Ops, SparseCore 0:
  51.9 75.2 all-gather.1
  187.1 88.3 reduce-scatter.1

commit v3 on v2

--- a/solution.py
+++ b/solution.py
@@ -268,20 +268,19 @@
     loads = fetch(
         [(hid, hv), (wq, qv), (wk, kv), (wv, vv), (wg, gv), (wo, ov), (fg, fgv), (fu, fuv), (fd, fdv)], isem
     )
-    rows = beta.shape[0]
+    rows = beta.shape[1]
     lanes = iota((rows, 128), 1)
     eye = iota((rows, rows), 0) == iota((rows, rows), 1)
-    column = lambda ref: jnp.sum(jnp.where(eye, ref[...].astype(F32), 0.0), axis=1, keepdims=True)
-    be, al = beta[...].astype(F32), alpha[...].astype(F32)
+    column = lambda ref, k=0: jnp.sum(jnp.where(eye, ref[k : k + 1].astype(F32), 0.0), axis=1, keepdims=True)
     tail = jnp.where(lanes == 3, column(gain_in), jnp.where(lanes == 4, column(gain_mid), 0.0))
     share = fbuf.shape[3]
     for copy in loads[1:6]:
         copy.wait()
     for h in range(heads):
         col = lambda j: slice(128 * (j * heads + h), 128 * (j * heads + h) + 128)
-        small = jnp.where(lanes == 0, be[:, h : h + 1], tail)
-        small = jnp.where(lanes == 1, be[:, heads + h : heads + h + 1], small)
-        small = jnp.where(lanes == 2, al[:, h : h + 1], small)
+        small = jnp.where(lanes == 0, column(beta, h), tail)
+        small = jnp.where(lanes == 1, column(beta, heads + h), small)
+        small = jnp.where(lanes == 2, column(alpha, h), small)
         parts = (
             qv[:, col(0)], kv[:, col(0)], kv[:, col(1)], vv[:, col(0)], vv[:, col(1)], gv[:, col(0)],
             small.astype(BF16), ov[:, col(0)],
@@ -297,10 +296,28 @@
     def arrives(origin):
         send(wbuf.at[0], wm_out.at[origin, at.b], ws.at[0], wr.at[origin], {"seq": at.sib}).wait_recv()
 
+    square = nb == 4
+
+    def hop(block, sem, m):
+        return lambda: send(block, block, os_.at[sem], or_.at[sem], {"batch": at.peer(m)})
+
+    def plane(zo):
+        block = wm_out.at[pl.ds(2 * zo, 2), at.b]
+        half = lambda core, m: wm_out.at[2 * zo + core, at.peer(m)]
+        if not square:
+            return [hop(block, (zo, m), m) for m in at.peers()], []
+        first = [hop(block, (zo, m), m) for m in (1, 2)]
+        return first, [hop(half(0, 1), (zo, 3), 2), hop(half(1, 2), (zo, 0), 1)]
+
     def pass_on(zo):
-        for m in at.peers():
-            both = wm_out.at[pl.ds(2 * zo, 2), at.b]
-            send(both, both, os_.at[zo, m], or_.at[zo, m], {"batch": at.peer(m)}).start()
+        for copy in plane(zo)[0]:
+            copy().start()
+
+    def follow(zo):
+        first, then = plane(zo)
+        for copy, onward in zip(first, then):
+            copy().wait_recv()
+            onward().start()
 
     def around(fn):
         for t in range(1, at.nz):
@@ -338,18 +355,29 @@
             arrives(2 * zo + core)
         pass_on(zo)
 
+    def at_distance(t, fn):
+        if t == 0:
+            fn(at.z)
+        else:
+            pl.when(at.z + t < at.nz)(lambda: fn(at.z + t))
+            pl.when(at.z - t >= 0)(lambda: fn(at.z - t))
+
     for t in range(1, at.nz):
-        pl.when(at.z + t < at.nz)(lambda: relay(at.z + t))
-        pl.when(at.z - t >= 0)(lambda: relay(at.z - t))
+        at_distance(t, relay)
         line.forward(t)
-    for copy in cols:
-        copy.start()
+        at_distance(t - 1, follow)
+        if t == 1:
+            for copy in cols:
+                copy.start()
+    at_distance(at.nz - 1, follow)
     line.finish()
 
     def settle(zo):
-        for m in at.peers():
-            both = wm_out.at[pl.ds(2 * zo, 2), at.b]
-            send(both, both, os_.at[zo, m], or_.at[zo, m], {"batch": at.peer(m)}).wait()
+        first, then = plane(zo)
+        for copy in then if square else first:
+            copy().wait_recv()
+        for copy in first + then:
+            copy().wait_send()
 
     for zo in range(at.nz):
         settle(zo)
@@ -368,10 +396,10 @@
 
 def front_kernel(
     ns, nb, rep, heads,
-    len_ref, dlog_ref, dbias_ref, hid_hbm, w_hbm, taps_hbm, hg_ref, cot_hbm,
-    normed_hbm, pre_hbm, gated_hbm, save_hbm, gains, after, nm_out, cot_out,
+    len_ref, dlog_ref, dbias_ref, hid_hbm, w_hbm, taps_hbm, hg_ref, cot_hbm, feed_hbm,
+    normed_hbm, pre_hbm, gated_hbm, save_hbm, gains, after, nm_out, cot_out, feed_out,
     hid_ref, w_ref, taps_ref, cot, nm, zero, save, preb, normedb, gatedb,
-    buf, state, part, got, out, far, isem, bsem, lsem, osem, ps, pr, qs, qr, ms, mr, cs, cr,
+    buf, state, part, got, out, far, isem, bsem, lsem, osem, ps, pr, qs, qr, ms, mr, cs, cr, fs, fr,
 ):
     at = Place(ns, nb)
     greet(at)
@@ -406,6 +434,8 @@
     hg = hg_ref[...].astype(F32)
     rows = SeqSum(at, part, got, out, far, (ps, pr, qs, qr))
     enter(at)
+    line = SeqGather(at, feed_hbm, feed_out, fs, fr)
+    line.start()
     mine = pltpu.make_async_copy(cot, cot_out.at[at.b], lsem.at[0])
     mine.start()
     edge = pltpu.make_async_copy(zero, pre_hbm.at[0:8], lsem.at[1])
@@ -487,6 +517,8 @@
             xb = [mm3(a, b) for a, b in zip(xs, bl)]
             X = [x_ - mm3(a, b) for x_, a, b in zip(X, xb, xs)]
         pl.when(i > 0)(lambda: rows.flush(i - 1))
+        for t in range(1, steps // 2):
+            pl.when(i == 2 * t)(lambda: line.forward(t))
         W, U = [], []
         for s in range(GS):
             cc = jnp.concatenate([C[s], C[s]], axis=0)
@@ -530,7 +562,10 @@
     mids.start()
     own = pltpu.make_async_copy(nm, nm_out.at[at.b], lsem.at[2])
     own.start()
+    for t in range(steps // 2, steps):
+        line.forward(t)
     rows.drain()
+    line.finish()
     for i in (steps - 2, steps - 1):
         for copy in saves(i):
             copy.wait()
@@ -543,16 +578,26 @@
 
 def feed_kernel(
     ns, nb,
-    nm_hbm, cot_hbm, ff_hbm, after, gains,
+    nm_hbm, cot_hbm, ff_hbm, mine_hbm, after, gains,
     block_out, d_stream, dbr_out, gfeed, sums,
     nm_all, cot_all, ff, acts, dgs, dus, pmid, pout, got_m, got_o, dbr, gbuf, gdown,
     isem, lsem, ms, mr, os_, or_, gs, gr, ds_s, dr_s,
 ):
     at = Place(ns, nb)
     greet(at)
-    loads = fetch([(nm_hbm, nm_all), (cot_hbm, cot_all), (ff_hbm, ff)], isem)
+    loads = fetch([(nm_hbm, nm_all), (cot_hbm, cot_all)], isem)
+    piece = mine_hbm.shape[1]
+
+    def weights(i, src):
+        return pltpu.make_async_copy(src, ff.at[:, piece * i : piece * (i + 1)], isem.at[2 + i])
+
+    for i in range(ns):
+        pl.when(i == at.s)(lambda: weights(i, mine_hbm).start())
+        pl.when(i != at.s)(lambda: weights(i, ff_hbm.at[i]).start())
     for copy in loads:
         copy.wait()
+    for i in range(ns):
+        weights(i, mine_hbm).wait()
     tok = after.shape[0]
     share = ff.shape[2]
     enter(at)
@@ -670,11 +715,12 @@
 def back_kernel(
     ns, nb, rep, heads,
     len_ref, dlog_ref, dbias_ref, dbr_hbm, w_hbm, taps_hbm, hg_ref, normed_hbm, pre_hbm, gated_hbm, save_hbm,
-    hid_hbm, gains, d_stream, gfeed,
-    grad_in, slots, gout_sum, small_all, vec_sum,
+    hid_hbm, sums, gains, d_stream, gfeed,
+    grad_in, q_slots, k_slots, gout_sum, small_all, feed_sum,
     dbr_ref, w_ref, taps_ref, hid, save, buf, normedb, gatedb, isem, bsem,
-    dbuf, dstate, small, gw, go, part, got, out, far, grads, gout, got_g, piece, got_o, got_s, got_v, vec, got_w,
-    ready, ps, pr, qs, qr, gs, gr, bs, br, os_, or_, ss, sr, us, ur, vs_, vr, xs, xr,
+    dbuf, dstate, small, gw, go, part, got, out, far, grads, gout, got_g, piece, got_o, got_s,
+    f_own, f_got, f_up, f_down,
+    ready, ps, pr, qs, qr, gs, gr, bs, br, kr, os_, or_, ss, sr, us, ur, fi, fps, fpr, fus, fur, fds, fdr,
 ):
     at = Place(ns, nb)
     greet(at)
@@ -706,9 +752,19 @@
     taps = head_taps(taps_ref, head, heads)
     hg = hg_ref[...].astype(F32)
     rows = SeqSum(at, part, got, out, far, (ps, pr, qs, qr))
+    feed = LineSum(at, sums, f_own, f_got, f_up, f_down, (fi, fps, fpr, fus, fur, fds, fdr))
+    feed.load()
     enter(at)
+    feed.start()
     for ds in range(1, ns):
         pl.semaphore_signal(ready, inc=1, device_id={"seq": at.seq_at(ds)}, device_id_type=MESH)
+
+    when = {f: f + (2 if f == 1 else 3) for f in range(1, feed.turns() + 1)}
+
+    def turn(j, half):
+        for f, h in when.items():
+            if h < 2 * steps and h % 2 == half:
+                pl.when(j == h // 2)(lambda: feed.relay(f))
 
     def step(j, _):
         i = steps - 1 - j
@@ -785,6 +841,9 @@
             dS = jnp.exp(C[s][63:64]) * dS + A2[s] - mm3(kept_map(1, s), dvn, TN)
         dstate[...] = dS
         pl.when(j > 0)(lambda: rows.flush(i + 1))
+
+        pl.when(j == 0)(feed.begin)
+        turn(j, 0)
         dq_l, dk0_l, dk1_l, dv0_l, dv1_l, db0_l, db1_l, dg_l = [], [], [], [], [], [], [], []
         for s in range(GS):
             vn, sst, n, p = kept_map(2, s), kept_map(4, s), kept_map(3, s), kept_map(5, s, HALF)
@@ -835,6 +894,7 @@
             dv1_l.append(dv[64:])
             db0_l.append(db[:64])
             db1_l.append(db[64:])
+        turn(j, 1)
         cat = lambda parts: jnp.concatenate(parts, axis=0)
         dq, dk0, dk1, dv0, dv1 = cat(dq_l), cat(dk0_l), cat(dk1_l), cat(dv0_l), cat(dv1_l)
         db0, db1, dg = cat(db0_l), cat(db1_l), cat(dg_l)
@@ -868,28 +928,34 @@
         gw[...] += mm(normedb[slot], dall, TN)
         if rep > 1:
             dall = jnp.where(lax.rem(at.s, rep) == 0, dall, jnp.zeros_like(dall))
-        part[i] = mm(dall, w_ref[:, 0:896], NT).astype(BF16).reshape(2, GB // 2, -1)
+        d_normed = mm(dall, w_ref[:, 0:896], NT)
+        part[i] = d_normed.astype(BF16).reshape(2, GB // 2, -1)
         rows.start(i)
+        small[7:8] += jnp.sum(d_normed * normedb[slot].astype(F32), axis=0, keepdims=True)
         return 0
 
     lax.fori_loop(0, steps, step, 0)
 
-    small[4:8] = jnp.transpose(gw[:, 768:896])[0:4]
+    small[4:7] = jnp.transpose(gw[:, 768:896])[0:3]
+    small[7:8] = small[7:8] / gains[3:4]
+    fourth = small.shape[1] // 4
+    for k in range(4):
+        small[k : k + 1, 3 * fourth :] = gfeed[:, fourth * k : fourth * (k + 1)]
     smalls = [send(small, got_s.at[m], ss.at[m], sr.at[m], {"batch": at.peer(m)}) for m in at.peers()]
     for copy in smalls:
         copy.start()
-    nk, nq = ns // nb, slots.shape[0] // 6
-    wrows = grads.shape[1]
-    grads[...] = gw[:, 0:768].astype(BF16).reshape(ns, wrows, 768)
-    over = []
-    for k in range(nk):
-        for m in at.peers():
-            to = at.peer(m)
-            n = k * nb + m
-            over.append(send(grads.at[to + nb * k], got_g.at[n], gs.at[n], gr.at[n], {"batch": to}))
+    nq = q_slots.shape[0]
+    part_rows, width = grads.shape[2], q_slots.shape[4]
+    grads[...] = gw[:, 0:768].astype(BF16).reshape(ns, nb, part_rows, 768)
+    over = [
+        send(grads.at[:, at.peer(m)], got_g.at[m], gs.at[m], gr.at[m], {"batch": at.peer(m)}) for m in at.peers()
+    ]
     for copy in over:
         copy.start()
     rows.flush(0)
+    for f, h in when.items():
+        if h >= 2 * steps:
+            feed.relay(f)
     high, wide = gout.shape[1:]
     for b in range(nb):
         block = go[:, wide * b : wide * (b + 1)].astype(BF16)
@@ -913,31 +979,29 @@
     for copy in over:
         copy.wait_recv()
     pl.semaphore_wait(ready, ns - 1)
-    width = slots.shape[2]
+    acc = grads[:, at.b].astype(F32)
+    for m in at.peers():
+        acc = acc + got_g[m].astype(F32)
+    for g, mats in enumerate(((0, 5), (1, 3), (2, 4))):
+        for n, m in enumerate(mats):
+            block = acc[:, :, 128 * m : 128 * m + 128]
+            if rep > 1:
+                block = jnp.where(lax.rem(at.s, rep) == 0, block[:, :, :width], block[:, :, width:])
+            piece[g, :, n] = block.astype(BF16)
     placed = []
-    for k in range(nk):
-        row = at.b + nb * k
-        acc = grads[row].astype(F32)
-        for m in at.peers():
-            acc = acc + got_g[k * nb + m].astype(F32)
-        for m in range(6):
-            block = acc[:, 128 * m : 128 * m + 128]
-            if rep > 1:
-                block = jnp.where(lax.rem(at.s, rep) == 0, block[:, :width], block[:, width:])
-            piece[k * 6 + m] = block.astype(BF16)
-            if m in (0, 5):
-                owner, slot = at.s // nq, (0 if m == 0 else 5 * nq) + lax.rem(at.s, nq)
-            else:
-                unit_at = ((m - 1) % 2) * ns + at.s
-                owner, slot = unit_at // (2 * nq), (nq if m < 3 else 3 * nq) + lax.rem(unit_at, 2 * nq)
-            placed.append((row, owner, slot, k * 6 + m))
+    for g in range(3):
+        unit_at = at.s if g < 2 else ns + at.s
+        dst, count, dst_sem = (q_slots, nq, br) if g == 0 else (k_slots, 2 * nq, kr)
+        owner, slot = unit_at // count, lax.rem(unit_at, count)
+        for row in range(ns):
+            placed.append((g, row, owner, dst.at[slot, :, at.b], dst_sem.at[slot, at.b]))
 
     def place(item):
-        row, owner, slot, n = item
-        src = piece.at[n]
+        g, row, owner, dst, sem = item
+        src = piece.at[g, row]
         here = jnp.logical_and(row == at.s, owner == at.b)
-        far_copy = lambda: send(src, slots.at[slot], bs.at[n], br.at[slot], {"seq": row, "batch": owner})
-        near_copy = lambda: pltpu.make_async_copy(src, slots.at[slot], br.at[slot])
+        far_copy = lambda: send(src, dst, bs.at[g, row], sem, {"seq": row, "batch": owner})
+        near_copy = lambda: pltpu.make_async_copy(src, dst, sem)
         return here, far_copy, near_copy
 
     for item in placed:
@@ -949,11 +1013,6 @@
     x = hid[...].astype(F32)
     r = norm_rows(x)
     y = x * r
-    vec[0:1] = jnp.sum(d_normed * y, axis=0, keepdims=True)
-    vec[1:2] = gfeed[...]
-    pairs = [send(vec, got_v.at[m], vs_.at[m], vr.at[m], {"batch": at.peer(m)}) for m in at.peers()]
-    for copy in pairs:
-        copy.start()
     dy = d_normed * gains[3:4]
     grad_in[...] = (d_stream[...] + r * (dy - y * jnp.mean(dy * y, axis=-1, keepdims=True))).astype(BF16)
     acc = gout[at.b].astype(F32)
@@ -961,28 +1020,171 @@
         copy.wait_recv()
         acc = acc + got_o[m].astype(F32)
     gout_sum[...] = acc
-    row_sum = vec[...]
-    for m, copy in zip(at.peers(), pairs):
+    for copy in heads_:
         copy.wait_recv()
-        row_sum = row_sum + got_v[m]
-    got_w[0] = row_sum
-    spread = [send(got_w.at[0], got_w.at[ds], xs.at[ds], xr.at[ds], {"seq": at.seq_at(ds)}) for ds in range(1, ns)]
-    for copy in spread:
-        copy.start()
-    for copy in spread + heads_:
-        copy.wait_recv()
-    row_sum = got_w[0]
-    for ds in range(1, ns):
-        row_sum = row_sum + got_w[ds]
-    vec_sum[...] = row_sum
     for item in placed:
         here, far_copy, _ = place(item)
         pl.when(jnp.logical_not(here))(lambda: far_copy().wait_send())
-    for slot in range(slots.shape[0]):
-        pltpu.make_async_copy(piece.at[0], slots.at[slot], br.at[slot]).wait()
-    for copy in smalls + over + outs + heads_ + pairs + spread:
+    for dst, sem in ((q_slots, br), (k_slots, kr)):
+        for slot in range(dst.shape[0]):
+            for b in range(nb):
+                pltpu.make_async_copy(piece.at[0, 0], dst.at[slot, :, b], sem.at[slot, b]).wait()
+    for copy in smalls + over + outs + heads_:
         copy.wait_send()
+    feed.finish(feed_sum)
+    feed.drain()
     rows.drain()
+
+
+class LineSum:
+    def __init__(self, at, part, own, got, ups, downs, sems):
+        self.at, self.part, self.own, self.got = at, part, own, got
+        self.line = (ups, downs)
+        self.isem, self.pair_s, self.pair_r, self.sems = sems[0], sems[1], sems[2], sems[3:]
+
+    def mine(self, i):
+        return pltpu.make_async_copy(self.part.at[i, self.at.c], self.own.at[i], self.isem.at[i])
+
+    def pair(self, i):
+        at = self.at
+        return send(self.part.at[i, 1 - at.c], self.got.at[i], self.pair_s.at[i], self.pair_r.at[i], {"seq": at.sib})
+
+    def hop(self, i, up, src=None):
+        buf, k = self.line[0 if up else 1], 0 if up else 2
+        return send(
+            buf.at[i] if src is None else src, buf.at[i], self.sems[k].at[i], self.sems[k + 1].at[i],
+            {"seq": self.at.s + 2 if up else self.at.s - 2},
+        )
+
+    def load(self):
+        for i in range(self.at.nz):
+            self.mine(i).start()
+
+    def start(self):
+        for i in range(self.at.nz):
+            self.pair(i).start()
+
+    def begin(self):
+        at, nz = self.at, self.at.nz
+        for i in range(nz):
+            self.mine(i).wait()
+            self.pair(i).wait_recv()
+            self.own[i] = (self.own[i].astype(F32) + self.got[i].astype(F32)).astype(BF16)
+        for k in range(nz - 1):
+            pl.when(at.z == 0)(lambda: self.hop(nz - 1 - k, True, self.own.at[nz - 1 - k]).start())
+            pl.when(at.z == nz - 1)(lambda: self.hop(k, False, self.own.at[k]).start())
+
+    def relay(self, f):
+        at, nz = self.at, self.at.nz
+        for a in range(1, nz - 1):
+            k = f - (2 * a - 1)
+            if not 0 <= k < nz - 1 - a:
+                continue
+
+            @pl.when(at.z == a)
+            def _():
+                self.pass_on(nz - 1 - k, True)
+
+            @pl.when(at.z == nz - 1 - a)
+            def _():
+                self.pass_on(k, False)
+
+    def turns(self):
+        nz = self.at.nz
+        return max(2 * a - 1 + nz - 2 - a for a in range(1, nz - 1)) if nz > 2 else 0
+
+    def pass_on(self, i, up):
+        buf = self.line[0 if up else 1]
+        self.hop(i, up).wait_recv()
+        buf[i] = (buf[i].astype(F32) + self.own[i].astype(F32)).astype(BF16)
+        self.hop(i, up).start()
+
+    def finish(self, out):
+        at = self.at
+        out[...] = self.own[at.z].astype(F32)
+        for up in (True, False):
+
+            @pl.when(at.z > 0 if up else at.z < at.nz - 1)
+            def _():
+                self.hop(at.z, up).wait_recv()
+                out[...] += self.line[0 if up else 1][at.z].astype(F32)
+
+    def drain(self):
+        at, nz = self.at, self.at.nz
+        for i in range(nz):
+            self.pair(i).wait_send()
+            pl.when(i > at.z)(lambda: self.hop(i, True).wait_send())
+            pl.when(i < at.z)(lambda: self.hop(i, False).wait_send())
+
+
+def finish_kernel(
+    rep, heads, share, halves,
+    block_in, grad_in_, q_in, k_in, gout_in, small_in, feed_in,
+    o_block, o_grad, o_gain, o_q, o_k, o_v, o_beta, o_alpha, o_gate, o_out, o_mid, o_fg, o_fu, o_fd, o_taps, o_log,
+    o_bias, o_hg,
+    block, grad, q_slots, k_slots, gout, small, feed, gq, gk, gv, gg, fd, taps, vec_a, vec_b, dlog, dbias,
+    hgain, stack, isem, osem,
+):
+    loads = fetch(
+        [
+            (q_in, q_slots), (feed_in, feed), (small_in, small), (block_in, block), (grad_in_, grad),
+            (gout_in, gout), (k_in, k_slots),
+        ],
+        isem,
+    )
+    outs = []
+
+    def put(src, dst):
+        copy = pltpu.make_async_copy(src, dst, osem.at[len(outs)])
+        copy.start()
+        outs.append(copy)
+
+    loads[0].wait()
+    loads[6].wait()
+    cw = q_slots.shape[4]
+    for ref, slots, n in ((gq, q_slots, 0), (gg, q_slots, 1), (gk, k_slots, 0), (gv, k_slots, 1)):
+        for k in range(slots.shape[0]):
+            ref[:, cw * k : cw * (k + 1)] = slots[k, n].astype(F32).reshape(ref.shape[0], cw)
+    for src, dst in ((gq, o_q), (gk, o_k), (gv, o_v), (gg, o_gate)):
+        put(src, dst)
+    loads[1].wait()
+    deep, cols = share // halves, feed.shape[1]
+    for t in range(halves):
+        fd[:, cols * t : cols * (t + 1)] = feed[2 * share + deep * t : 2 * share + deep * (t + 1)]
+    for src, dst in ((feed.at[0:share], o_fg), (feed.at[share : 2 * share], o_fu), (fd, o_fd)):
+        put(src, dst)
+    loads[2].wait()
+    lanes = iota((1, heads), 1)
+    log_row, bias_row, gain_row = jnp.zeros((1, heads), F32), jnp.zeros((1, heads), F32), jnp.zeros((1, DK), F32)
+    for h in range(heads):
+        at = small.at[rep * h]
+        for j in range(3):
+            stack[j * heads + h : j * heads + h + 1] = at[4 + j : 5 + j]
+        for g in range(5):
+            col = DK * (heads * g + h)
+            taps[:, col : col + DK] = at[0:4, DK * g : DK * (g + 1)]
+        gain_row = gain_row + at[0:1, 5 * DK : 6 * DK]
+        log_row = jnp.where(lanes == h, at[1:2, 5 * DK : 5 * DK + 1], log_row)
+        bias_row = jnp.where(lanes == h, at[2:3, 5 * DK : 5 * DK + 1], bias_row)
+    hgain[...] = gain_row
+    dlog[...] = log_row
+    dbias[...] = bias_row
+    for src, dst in ((stack.at[: 2 * heads], o_beta), (stack.at[2 * heads :], o_alpha), (taps, o_taps), (hgain, o_hg), (dlog, o_log), (dbias, o_bias)):
+        put(src, dst)
+    every = small[0]
+    for k in range(1, small.shape[0]):
+        every = every + small[k]
+    vec_a[...] = every[7:8]
+    fourth = every.shape[1] // 4
+    for k in range(4):
+        vec_b[:, fourth * k : fourth * (k + 1)] = every[k : k + 1, 3 * fourth :]
+    put(vec_a, o_gain)
+    put(vec_b, o_mid)
+    for copy, src, dst in ((loads[3], block, o_block), (loads[4], grad, o_grad), (loads[5], gout, o_out)):
+        copy.wait()
+        put(src, dst)
+    for copy in outs:
+        copy.wait()
 
 
 def comm_call(kernel, outs, scratch, ident, name, args, specs, limit):
@@ -1039,29 +1241,31 @@
         ],
         0, "gather",
         (
-            hidden, query_weight, key_weight, value_weight, gate_weight, out_weight.T, beta_weight, alpha_weight,
+            hidden, query_weight, key_weight, value_weight, gate_weight, out_weight.T, beta_weight.T, alpha_weight.T,
             mixer_gain[None], feed_gain[None], feed_gate, feed_up, feed_down.T,
         ),
         [hbm] * 6 + [vmem] * 4 + [hbm] * 3, 62,
     )
     wm = wm.reshape(width, 8 * DK)
-    ff = lax.all_gather(ff.reshape(3, nb * rows, share), "seq", axis=1, tiled=True)
+    ff = ff.reshape(3, nb * rows, share)
     hg = head_gain[None]
-    normed, pre, gated, save, gains, after, nm_all, cot_all = comm_call(
+    normed, pre, gated, save, gains, after, nm_all, cot_all, ff_all = comm_call(
         functools.partial(front_kernel, ns, nb, rep, heads),
         [
             hout(BF16, n, width), hout(F32, n + 8, 5 * DK), hout(BF16, n, DK), hout(F32, nz, SAVE_ROWS, DK),
             vout(F32, 8, width), vout(F32, tok, width), hout(BF16, nb, tok, width), hout(BF16, nb, tok, width),
+            hout(BF16, ns, 3, nb * rows, share),
         ],
         [
             block(ns), buffer(width, 8 * DK), buffer(4, 5 * key), buffer(tok, width), buffer(tok, width),
             wide(8, 5 * DK), wide(2, SAVE_ROWS, DK), wide(2, GB, 5 * DK), buffer(2, GB, width), buffer(2, GB, DK),
             wide(8 + GB, 5 * DK), wide(DK, DK), buffer(nz, 2, tok, width), block(nz), block(nz), block(nz),
             dma(3), dma(nz), dma(3), dma(2, 4), dma(nz), dma(nz), dma(nz), dma(nz), dma(nb), dma(nb), dma(nb), dma(nb),
+            dma(4 * nz), dma(4 * nz),
         ],
         1, "front",
-        (lengths, decay_log, decay_bias, hid_all, wm, conv_taps, hg, cot),
-        [smem] * 3 + [hbm] * 3 + [vmem, hbm], 61,
+        (lengths, decay_log, decay_bias, hid_all, wm, conv_taps, hg, cot, ff),
+        [smem] * 3 + [hbm] * 3 + [vmem, hbm, hbm], 61,
     )
     block_out, d_stream, dbr_all, gfeed, sums = comm_call(
         functools.partial(feed_kernel, ns, nb),
@@ -1073,68 +1277,70 @@
             block(nb), block(nb), buffer(3, width, share), buffer(nb, tok, share), buffer(nb, tok, share),
             buffer(nb, tok, share), block(nb), block(nb), block(nb), block(nb), buffer(tok, width),
             buffer(2, ns, share, width // ns), buffer(nb, halves, share, width // ns),
-            dma(3), dma(3 + halves), dma(nb), dma(nb), dma(nb), dma(nb), dma(4 * nz), dma(4 * nz), dma(nb, halves),
+            dma(2 + ns), dma(3 + halves), dma(nb), dma(nb), dma(nb), dma(nb), dma(4 * nz), dma(4 * nz), dma(nb, halves),
             dma(nb, halves),
         ],
-        2, "feed", (nm_all, cot_all, ff, after, gains), [hbm] * 3 + [vmem] * 2, 61,
+        2, "feed", (nm_all, cot_all, ff_all, ff, after, gains), [hbm] * 4 + [vmem] * 2, 61,
     )
-    sums = lax.psum_scatter(sums, "seq", scatter_dimension=0, tiled=False)
-    g_down = jnp.swapaxes(sums[2 * share :].reshape(halves, share // halves, width // ns), 0, 1)
-    g_down = g_down.reshape(share // halves, width // nb).astype(F32)
-
     nq = ns // nb
-    nk = ns // nb
     cw = DK // rep
     wrows = width // ns
-    grad_in, slots, gout_sum, small_all, vec_sum = comm_call(
+    deep = 3 * share
+    feed_buffers = [buffer(nz, deep, width // ns)] * 4
+    quarter = wrows // nb
+    grad_in, q_slots, k_slots, gout_sum, small_all, feed_sum = comm_call(
         functools.partial(back_kernel, ns, nb, rep, heads),
         [
-            vout(BF16, tok, width), vout(BF16, 6 * nq, wrows, cw), vout(F32, DK // rep, width // nb),
-            vout(F32, ns, 8, width), vout(F32, 2, width),
+            vout(BF16, tok, width), vout(BF16, nq, 2, nb, quarter, cw), vout(BF16, 2 * nq, 2, nb, quarter, cw),
+            vout(F32, DK // rep, width // nb),
+            vout(F32, ns, 8, width), vout(F32, deep, width // ns),
         ],
         [
             buffer(2, 2, tok, width), buffer(width, 8 * DK), buffer(4, 5 * key), buffer(tok, width),
             wide(2, SAVE_ROWS, DK), wide(2, 8 + GB, 5 * DK), buffer(2, GB, width), buffer(2, GB, DK), dma(3), dma(2, 5),
             wide(GB + 8, 5 * DK), wide(DK, DK), wide(8, width), wide(width, 7 * DK),
             wide(DK, width), buffer(nz, 2, tok, width), block(nz), block(nz), block(nz),
-            buffer(ns, wrows, 6 * DK), buffer(nb, DK // rep, width // nb), buffer(nk * nb, wrows, 6 * DK),
-            buffer(nk * 6, wrows, cw), buffer(nb, DK // rep, width // nb), wide(nb, 8, width), wide(nb, 2, width),
-            wide(2, width), wide(ns, 2, width), pltpu.SemaphoreType.REGULAR,
-            dma(nz), dma(nz), dma(nz), dma(nz), dma(nk * nb), dma(nk * nb), dma(nk * 6), dma(6 * nq),
-            dma(nb), dma(nb), dma(nb), dma(nb), dma(ns), dma(ns), dma(nb), dma(nb), dma(ns), dma(ns),
+            buffer(ns, nb, quarter, 6 * DK), buffer(nb, DK // rep, width // nb), buffer(nb, ns, quarter, 6 * DK),
+            buffer(3, ns, 2, quarter, cw), buffer(nb, DK // rep, width // nb), wide(nb, 8, width),
+            *feed_buffers, pltpu.SemaphoreType.REGULAR,
+            dma(nz), dma(nz), dma(nz), dma(nz), dma(nb), dma(nb), dma(3, ns), dma(nq, nb), dma(2 * nq, nb),
+            dma(nb), dma(nb), dma(nb), dma(nb), dma(ns), dma(ns),
+            *[dma(nz)] * 7,
         ],
         3, "back",
         (
-            lengths, decay_log, decay_bias, dbr_all, wm, conv_taps, hg, normed, pre, gated, save, hidden, gains,
-            d_stream, gfeed,
+            lengths, decay_log, decay_bias, dbr_all, wm, conv_taps, hg, normed, pre, gated, save, hidden,
+            sums.reshape(nz, 2, deep, width // ns), gains, d_stream, gfeed,
         ),
-        [smem] * 3 + [hbm] * 3 + [vmem] + [hbm] * 5 + [vmem] * 3, 61,
+        [smem] * 3 + [hbm] * 3 + [vmem] + [hbm] * 6 + [vmem] * 3, 61,
     )
 
-    def owned(first, count):
-        return jnp.swapaxes(slots[first : first + count], 0, 1).reshape(wrows, count * cw).astype(F32)
-
-    small_all = small_all[::rep]
-    return (
-        block_out[None],
-        grad_in[None],
-        vec_sum[0],
-        owned(0, nq),
-        owned(nq, 2 * nq),
-        owned(3 * nq, 2 * nq),
-        jnp.transpose(small_all[:, 4:6], (2, 1, 0)).reshape(width, 2 * heads),
-        small_all[:, 6].T,
-        owned(5 * nq, nq),
-        gout_sum,
-        vec_sum[1],
-        sums[:share].T.astype(F32),
-        sums[share : 2 * share].T.astype(F32),
-        g_down,
-        jnp.transpose(small_all[:, :4, : 5 * DK].reshape(heads, 4, 5, DK), (1, 2, 0, 3)).reshape(4, -1),
-        small_all[:, 1, 5 * DK],
-        small_all[:, 2, 5 * DK],
-        jnp.sum(small_all[:, 0, 5 * DK : 6 * DK], axis=0),
-    )
+    shapes = [
+        sds((tok, width), BF16), sds((tok, width), BF16), sds((1, width), F32), sds((wrows, nq * cw), F32),
+        sds((wrows, 2 * nq * cw), F32), sds((wrows, 2 * nq * cw), F32), sds((2 * heads, width), F32),
+        sds((heads, width), F32), sds((wrows, nq * cw), F32), sds((DK // rep, width // nb), F32), sds((1, width), F32),
+        sds((share, wrows), F32), sds((share, wrows), F32), sds((share // halves, width // nb), F32),
+        sds((4, 5 * key), F32), sds((1, heads), F32), sds((1, heads), F32), sds((1, DK), F32),
+    ]
+    like = lambda *which: [pltpu.VMEM(shapes[k].shape, shapes[k].dtype) for k in which]
+    outs = list(pl.pallas_call(
+        functools.partial(finish_kernel, rep, heads, share, halves),
+        in_specs=[hbm] * 7,
+        out_specs=[hbm] * len(shapes),
+        out_shape=shapes,
+        scratch_shapes=like(0, 1) + [buffer(nq, 2, nb, quarter, cw), buffer(2 * nq, 2, nb, quarter, cw)] + like(9) + [wide(ns, 8, width)]
+        + [wide(deep, width // ns)] + like(3, 4, 5, 8, 13, 14, 2, 10, 15, 16, 17)
+        + [wide(3 * heads, width), dma(7), dma(len(shapes))],
+        compiler_params=pltpu.CompilerParams(vmem_limit_bytes=61 * 1024 * 1024),
+        name="finish",
+    )(block_out, grad_in, q_slots, k_slots, gout_sum, small_all, feed_sum))
+    for k in (0, 1):
+        outs[k] = outs[k][None]
+    for k in (6, 7, 11, 12):
+        outs[k] = outs[k].T
+    for k in (2, 10, 15, 16, 17):
+        outs[k] = outs[k][0]
+    return tuple(outs)
 
 
 def solution(mesh):

time: 307 us -> 255 us (0.83)
  local copies, waits for them, and re-layouts: 15.4 us -> 0 us
  between operations: 14.8 us -> 1.52 us
  waiting for transfers between devices: 12.5 us -> 0 us
  other arithmetic: 4.98 us -> 0 us
    all_gather x1 -> x0, waiting for transfers between devices: 12.5 us -> none  [on_device(): lax.all_gather(ff.reshape(3, nb * rows, share), 'seq', axis=1, tiled=True)]
    unnamed x21 -> x0, local copies, waits for them, and re-layouts: 9.26 us -> none
    pallas_call x4, Pallas kernels: 257 us -> 250 us  [comm_call(): pl.pallas_call(kernel, in_specs=specs, out_specs=[o[1] for o in outs], ou...]
    slice x5 -> x0, local copies, waits for them, and re-layouts: 4.06 us -> none  [the longest x1 1.49 us: on_device(): small_all[:, 2, 5 * DK]]
    pallas_call x0 -> x1, Pallas kernels: none -> 3.38 us  [on_device(): pl.pallas_call(functools.partial(finish_kernel, rep, heads, share, halves...]
  transfers between devices with their start and end apart: 2 -> 0, of which waited for: 1 -> 0; matrix products, arithmetic and copies ran while one was open for 4% -> 0% of each run, Pallas kernels for 51% -> 0%
where the time goes in v3:
time: 255 us
  Pallas kernels  254 us (100%)
    pallas_call x4, Pallas kernels, comm_call(): pl.pallas_call(kernel, in_specs=specs, out_specs=[o[1] for o in outs], ou...  250 us

profile of v3, /device:TPU:7, one launch (start us, length us, event | category | flops | bytes accessed | tf_op | source)
XLA Modules:
  0.0 255.1 jit_solution(13811425794776291747)
XLA Ops:
  1.3 39.4 %gather.1 = (bf16[8,128,1024]{2,1,0:T(8,128)(2,1)}, bf16[8,4,32,1024]{3,2,1,0:T(8,128)(2,1)}, bf16[3,4,32,704]{3,2,1,0:T(8,128)(2,1)}) custom-call(bf16[128,1024]{1,0:T(8,128)(2,1)} %bitcast.28, bf16[32,1024]{1,0:T(8,128)(2,1)} %wq.1, bf16[32,2048]{1,0:T(8,128)(2,1)} %wk.1, bf16[32,2048]{1,0:T(8,128)(2,1)} %wv.1, bf16[32,1024]{1,0:T(8,128)(2,1)} %wg.1, ...), custom_call_target="tpu_custom_call" | custom-call | tf_op jit(solution)/shard_map/gather/pallas_call | solution.py:1191
  40.7 71.6 %front.1 = (bf16[1024,1024]{1,0:T(8,128)(2,1)}, f32[1032,640]{1,0:T(8,128)}, bf16[1024,128]{1,0:T(8,128)(2,1)}, f32[4,3584,128]{2,1,0:T(8,128)}, f32[8,1024]{1,0...) custom-call(s32[1]{0:T(128)S(6)} %copy.37.len_ref, ...), custom_call_target="tpu_custom_call" | custom-call | tf_op jit(solution)/shard_map/front/pallas_call | solution.py:1191
  112.3 49.8 %feed.1 = (bf16[128,1024]{1,0:T(8,128)(2,1)}, f32[128,1024]{1,0:T(8,128)}, bf16[8,128,1024]{2,1,0:T(8,128)(2,1)}, f32[1,1024]{1,0:T(1,128)}, bf16[8,2112,128]{2,1,0:T(8,128)(2,1)}) custom-call(bf16[4,128,1024]{2,1,0:T(8,128)(2,1)} %get-tuple-element.62.nm_hbm, bf16[4,128,1024]{2,1,0:T(8,128)(2,1)} %get-tuple-element.63.cot_hbm, ...), custom_call_target="tpu_custom_call" | custom-call | tf_op jit(solution)/shard_map/feed/pallas_call | solution.py:1191
  162.2 89.4 %back.1 = (bf16[128,1024]{1,0:T(8,128)(2,1)}, bf16[2,2,4,32,128]{4,3,2,1,0:T(8,128)(2,1)}, bf16[4,2,4,32,128]{4,3,2,1,0:T(8,128)(2,1)}, f32[128,256]{1,0:T(8,128...) custom-call(s32[1]{0:T(128)S(6)} %copy.37.len_ref, f32[8]{0:T(128)} %dlog_ref.3, f32[8]{0:T(128)} %dbias_ref.3, ...), custom_call_target="tpu_custom_call" | custom-call | tf_op jit(solution)/shard_map/back/pallas_call | solution.py:1191
  251.5 3.4 %finish.1 = (bf16[128,1024]{1,0:T(8,128)(2,1)}, bf16[128,1024]{1,0:T(8,128)(2,1)}, f32[1,1024]{1,0:T(1,128)}, f32[128,256]{1,0:T(8,128)}, f32[128,512]{1,0:T(8,1...) custom-call(bf16[128,1024]{1,0:T(8,128)(2,1)} %get-tuple-element.67., ...), custom_call_target="tpu_custom_call" | custom-call | tf_op jit(solution)/shard_map/finish/pallas_call | solution.py:1326

commit v4 on v3

--- a/solution.py
+++ b/solution.py
@@ -257,13 +257,13 @@
     return lax.rsqrt(jnp.mean(x * x, axis=-1, keepdims=True) + EPS)
 
 
-def gather_kernel(
-    ns, nb, rep, heads,
+def collect(
+    at, rep, heads,
     hid, wq, wk, wv, wg, wo, beta, alpha, gain_in, gain_mid, fg, fu, fd,
     hid_out, wm_out, ff_out,
     hv, qv, kv, vv, gv, ov, fgv, fuv, fdv, wbuf, fbuf, isem, lsem, hs, hr, ws, wr, os_, or_, fs, fr,
 ):
-    at = Place(ns, nb)
+    ns, nb = at.ns, at.nb
     greet(at)
     loads = fetch(
         [(hid, hv), (wq, qv), (wk, kv), (wv, vv), (wg, gv), (wo, ov), (fg, fgv), (fu, fuv), (fd, fdv)], isem
@@ -396,21 +396,23 @@
 
 def front_kernel(
     ns, nb, rep, heads,
-    len_ref, dlog_ref, dbias_ref, hid_hbm, w_hbm, taps_hbm, hg_ref, cot_hbm, feed_hbm,
-    normed_hbm, pre_hbm, gated_hbm, save_hbm, gains, after, nm_out, cot_out, feed_out,
-    hid_ref, w_ref, taps_ref, cot, nm, zero, save, preb, normedb, gatedb,
+    len_ref, dlog_ref, dbias_ref, taps_hbm, hg_ref, cot_hbm,
+    hid, wq, wk, wv, wg, wo, beta, alpha, gain_in, gain_mid, fg, fu, fd,
+    w_hbm, feed_hbm, normed_hbm, pre_hbm, gated_hbm, save_hbm, gains, after, nm_out, cot_out, feed_out,
+    hv, qv, kv, vv, gv, ov, fgv, fuv, fdv, wbuf, fbuf, gisem, glsem, hs, hr, ws, wr, gs, gr, gfs, gfr,
+    hid_ref, w4, taps_ref, cot, nm, zero, save, preb, normedb, gatedb,
     buf, state, part, got, out, far, isem, bsem, lsem, osem, ps, pr, qs, qr, ms, mr, cs, cr, fs, fr,
 ):
     at = Place(ns, nb)
-    greet(at)
     steps = at.nz
-    loads = fetch([(w_hbm, w_ref), (taps_hbm, taps_ref), (cot_hbm, cot)], isem)
-
-    def block_in(i):
-        return pltpu.make_async_copy(hid_hbm.at[pl.ds(2 * i, 2)], hid_ref.at[pl.ds(2 * i, 2)], bsem.at[i])
-
-    for i in range(steps):
-        block_in(i).start()
+    loads = fetch([(taps_hbm, taps_ref), (cot_hbm, cot)], isem)
+    collect(
+        at, rep, heads, hid, wq, wk, wv, wg, wo, beta, alpha, gain_in, gain_mid, fg, fu, fd, hid_ref, w4, feed_hbm,
+        hv, qv, kv, vv, gv, ov, fgv, fuv, fdv, wbuf, fbuf, gisem, glsem, hs, hr, ws, wr, gs, gr, gfs, gfr,
+    )
+    weights_out = pltpu.make_async_copy(w4, w_hbm, bsem.at[0])
+    weights_out.start()
+    columns = lambda a, b: w4[:, :, :, a:b].reshape(-1, b - a)
     zero[...] = jnp.zeros_like(zero)
     for copy in loads:
         copy.wait()
@@ -429,11 +431,10 @@
     head = at.s // rep
     state[...] = jnp.zeros_like(state)
     buf[0:8] = jnp.zeros((8, 640), F32)
-    gains[...] = jnp.transpose(w_ref[:, 768:896].astype(F32))[0:8]
+    gains[...] = jnp.transpose(columns(768, 896).astype(F32))[0:8]
     taps = head_taps(taps_ref, head, heads)
     hg = hg_ref[...].astype(F32)
     rows = SeqSum(at, part, got, out, far, (ps, pr, qs, qr))
-    enter(at)
     line = SeqGather(at, feed_hbm, feed_out, fs, fr)
     line.start()
     mine = pltpu.make_async_copy(cot, cot_out.at[at.b], lsem.at[0])
@@ -460,11 +461,10 @@
             row = SPAN_ROWS * GS + GB * kind
             save[slot, row : row + GB] = value
 
-        block_in(i).wait()
         x = hid_ref[pl.ds(2 * i, 2)].reshape(GB, -1).astype(F32)
         normed = (x * norm_rows(x) * gains[3:4]).astype(BF16)
         normedb[slot] = normed
-        proj = mm(normed, w_ref[:, 0:896])
+        proj = mm(normed, columns(0, 896))
         pre = proj[:, 0:640].astype(BF16).astype(F32)
         preb[slot] = pre
         gl, sm = proj[:, 640:768], proj[:, 768:896]
@@ -549,7 +549,7 @@
             copy.start()
         if rep > 1:
             gated = jnp.where(lax.rem(at.s, rep) == 0, gated, jnp.zeros_like(gated))
-        part[i] = mm(gated, w_ref[:, 896:1024], NT).astype(BF16).reshape(2, GB // 2, -1)
+        part[i] = mm(gated, columns(896, 1024), NT).astype(BF16).reshape(2, GB // 2, -1)
         rows.start(i)
         return 0
 
@@ -573,18 +573,18 @@
     mids.finish()
     mine.wait()
     edge.wait()
+    weights_out.wait()
     own.wait()
 
 
-def feed_kernel(
-    ns, nb,
+def feed_part(
+    at,
     nm_hbm, cot_hbm, ff_hbm, mine_hbm, after, gains,
     block_out, d_stream, dbr_out, gfeed, sums,
-    nm_all, cot_all, ff, acts, dgs, dus, pmid, pout, got_m, got_o, dbr, gbuf, gdown,
-    isem, lsem, ms, mr, os_, or_, gs, gr, ds_s, dr_s,
+    nm_all, cot_all, ff, acts, dgs, dus, pmid, pout, got_m, got_o, gbuf, gdown,
+    isem, lsem, ms, mr, os_, or_, gs, gr, ds_s, dr_s, then=lambda: None,
 ):
-    at = Place(ns, nb)
-    greet(at)
+    ns, nb = at.ns, at.nb
     loads = fetch([(nm_hbm, nm_all), (cot_hbm, cot_all)], isem)
     piece = mine_hbm.shape[1]
 
@@ -656,11 +656,9 @@
     dy = d_mid * gains[4:5]
     ds_ = cot_all[at.b].astype(F32) + r * (dy - y * jnp.mean(dy * y, axis=-1, keepdims=True))
     d_stream[...] = ds_
-    dbr[...] = ds_.astype(BF16)
-    line = SeqGather(at, dbr, dbr_out, gs, gr)
+    dbr_out[at.s] = ds_.astype(BF16)
+    line = SeqGather(at, dbr_out.at[at.s], dbr_out, gs, gr)
     line.start()
-    own_rows = pltpu.make_async_copy(dbr, dbr_out.at[at.s], lsem.at[0])
-    own_rows.start()
     halves = ns // nb
     deep, cols = share // halves, nm_all.shape[2] // ns
     flat = lambda ref: ref[...].reshape(nb * tok, -1)
@@ -694,6 +692,9 @@
             line.forward(2)
     for copy in kept:
         copy.start()
+    for copy in moved + kept:
+        copy.wait()
+    then()
     for t in range(3, at.nz):
         line.forward(t)
     total = after[...] + pout[at.b].astype(F32)
@@ -702,28 +703,42 @@
         total = total + got_o[m].astype(F32)
     block_out[...] = total.astype(BF16)
     line.finish()
-    for copy in moved:
-        copy.wait()
     for m in at.peers():
         mid_copy(m).wait_send()
         out_copy(m).wait_send()
-    for copy in kept:
-        copy.wait()
-    own_rows.wait()
+
+
+def feed_kernel(ns, nb, *refs):
+    at = Place(ns, nb)
+    greet(at)
+    feed_part(at, *refs)
+
+
+FEED_SCRATCH = 24
 
 
 def back_kernel(
-    ns, nb, rep, heads,
-    len_ref, dlog_ref, dbias_ref, dbr_hbm, w_hbm, taps_hbm, hg_ref, normed_hbm, pre_hbm, gated_hbm, save_hbm,
-    hid_hbm, sums, gains, d_stream, gfeed,
-    grad_in, q_slots, k_slots, gout_sum, small_all, feed_sum,
-    dbr_ref, w_ref, taps_ref, hid, save, buf, normedb, gatedb, isem, bsem,
-    dbuf, dstate, small, gw, go, part, got, out, far, grads, gout, got_g, piece, got_o, got_s,
-    f_own, f_got, f_up, f_down,
-    ready, ps, pr, qs, qr, gs, gr, bs, br, kr, os_, or_, ss, sr, us, ur, fi, fps, fpr, fus, fur, fds, fdr,
+    ns, nb, rep, heads, merged,
+    len_ref, dlog_ref, dbias_ref, w_hbm, taps_hbm, hg_ref, normed_hbm, pre_hbm, gated_hbm, save_hbm,
+    hid_hbm, gains, *refs,
 ):
     at = Place(ns, nb)
     greet(at)
+    if merged:
+        nm_hbm, cot_hbm, ff_hbm, mine_hbm, after, block_out, sums, *refs = refs
+        outs, refs = refs[:6], refs[6:]
+        *feed_refs, d_stream, gfeed = refs[:FEED_SCRATCH]
+        refs = refs[FEED_SCRATCH:]
+    else:
+        dbr_hbm, sums, d_stream, gfeed, *refs = refs
+        outs, refs = refs[:6], refs[6:]
+    grad_in, q_slots, k_slots, gout_sum, small_all, feed_sum = outs
+    (
+        dbr_ref, w_ref, taps_ref, hid, save, buf, normedb, gatedb, isem, bsem,
+        dbuf, dstate, small, gw, go, part, got, out, far, grads, gout, got_g, piece, got_o, got_s,
+        f_own, f_got, f_up, f_down,
+        ready, ps, pr, qs, qr, gs, gr, bs, br, kr, os_, or_, ss, sr, us, ur, fi, fps, fpr, fus, fur, fds, fdr,
+    ) = refs
     steps = at.nz
     loads = fetch([(w_hbm, w_ref), (taps_hbm, taps_ref), (hid_hbm, hid)], isem)
 
@@ -736,7 +751,6 @@
             pltpu.make_async_copy(pre_hbm.at[pl.ds(first, 8 + GB)], buf.at[slot], bsem.at[slot, 1]),
             pltpu.make_async_copy(normed_hbm.at[here], normedb.at[slot], bsem.at[slot, 2]),
             pltpu.make_async_copy(gated_hbm.at[here], gatedb.at[slot], bsem.at[slot, 3]),
-            pltpu.make_async_copy(dbr_hbm.at[pl.ds(2 * i, 2)], dbr_ref.at[slot], bsem.at[slot, 4]),
         ]
 
     for copy in block_in(steps - 1):
@@ -753,9 +767,23 @@
     hg = hg_ref[...].astype(F32)
     rows = SeqSum(at, part, got, out, far, (ps, pr, qs, qr))
     feed = LineSum(at, sums, f_own, f_got, f_up, f_down, (fi, fps, fpr, fus, fur, fds, fdr))
-    feed.load()
-    enter(at)
-    feed.start()
+
+    def begin_sums():
+        feed.load()
+        feed.start()
+
+    if merged:
+        feed_part(
+            at, nm_hbm, cot_hbm, ff_hbm, mine_hbm, after, gains, block_out, d_stream, dbr_ref, gfeed, sums,
+            *feed_refs, begin_sums,
+        )
+    else:
+        rows_in = pltpu.make_async_copy(dbr_hbm, dbr_ref, isem.at[3])
+        rows_in.start()
+        enter(at)
+        begin_sums()
+        rows_in.wait()
+    feed.begin()
     for ds in range(1, ns):
         pl.semaphore_signal(ready, inc=1, device_id={"seq": at.seq_at(ds)}, device_id_type=MESH)
 
@@ -786,7 +814,7 @@
 
         for copy in block_in(i):
             copy.wait()
-        dbr = dbr_ref[slot].reshape(GB, -1)
+        dbr = dbr_ref[pl.ds(2 * i, 2)].reshape(GB, -1)
         d_gated = mm(dbr, w_ref[:, 896:1024])
         gl, sm, o = kept_rows(0), kept_rows(1), kept_rows(2)
         sg = jax.nn.sigmoid(gl)
@@ -842,7 +870,6 @@
         dstate[...] = dS
         pl.when(j > 0)(lambda: rows.flush(i + 1))
 
-        pl.when(j == 0)(feed.begin)
         turn(j, 0)
         dq_l, dk0_l, dk1_l, dv0_l, dv1_l, db0_l, db1_l, dg_l = [], [], [], [], [], [], [], []
         for s in range(GS):
@@ -1043,11 +1070,11 @@
         self.isem, self.pair_s, self.pair_r, self.sems = sems[0], sems[1], sems[2], sems[3:]
 
     def mine(self, i):
-        return pltpu.make_async_copy(self.part.at[i, self.at.c], self.own.at[i], self.isem.at[i])
+        return pltpu.make_async_copy(self.part.at[2 * i + self.at.c], self.own.at[i], self.isem.at[i])
 
     def pair(self, i):
         at = self.at
-        return send(self.part.at[i, 1 - at.c], self.got.at[i], self.pair_s.at[i], self.pair_r.at[i], {"seq": at.sib})
+        return send(self.part.at[2 * i + 1 - at.c], self.got.at[i], self.pair_s.at[i], self.pair_r.at[i], {"seq": at.sib})
 
     def hop(self, i, up, src=None):
         buf, k = self.line[0 if up else 1], 0 if up else 2
@@ -1230,91 +1257,95 @@
     hout = lambda kind, *shape: (sds(shape, kind), hbm)
     key = heads * DK
 
-    hid_all, wm, ff = comm_call(
-        functools.partial(gather_kernel, ns, nb, rep, heads),
-        [hout(BF16, ns, tok, width), hout(BF16, ns, nb, rows, 8 * DK), hout(BF16, 3, nb, rows, share)],
+    hg = head_gain[None]
+    wm, ff, normed, pre, gated, save, gains, after, nm_all, cot_all, ff_all = comm_call(
+        functools.partial(front_kernel, ns, nb, rep, heads),
+        [
+            hout(BF16, ns, nb, rows, 8 * DK), hout(BF16, 3, nb, rows, share),
+            hout(BF16, n, width), hout(F32, n + 8, 5 * DK), hout(BF16, n, DK), hout(F32, nz, SAVE_ROWS, DK),
+            vout(F32, 8, width), vout(F32, tok, width), hout(BF16, nb, tok, width), hout(BF16, nb, tok, width),
+            hout(BF16, ns, 3, nb, rows, share),
+        ],
         [
             buffer(tok, width), buffer(rows, key), buffer(rows, 2 * key), buffer(rows, 2 * key), buffer(rows, key),
             buffer(rows, key), buffer(rows, nb * share), buffer(rows, nb * share), buffer(rows, nb * share),
             buffer(heads, rows, 8 * DK), buffer(nb, 3, rows, share), dma(9), dma(3), dma(4 * nz), dma(4 * nz), dma(ns),
             dma(ns), dma(nz, nb), dma(nz, nb), dma(nb), dma(nb),
+            block(ns), buffer(ns, nb, rows, 8 * DK), buffer(4, 5 * key), buffer(tok, width), buffer(tok, width),
+            wide(8, 5 * DK), wide(2, SAVE_ROWS, DK), wide(2, GB, 5 * DK), buffer(2, GB, width), buffer(2, GB, DK),
+            wide(8 + GB, 5 * DK), wide(DK, DK), buffer(nz, 2, tok, width), block(nz), block(nz), block(nz),
+            dma(2), dma(1), dma(3), dma(2, 4), dma(nz), dma(nz), dma(nz), dma(nz), dma(nb), dma(nb), dma(nb), dma(nb),
+            dma(4 * nz), dma(4 * nz),
         ],
-        0, "gather",
+        1, "front",
         (
+            lengths, decay_log, decay_bias, conv_taps, hg, cot,
             hidden, query_weight, key_weight, value_weight, gate_weight, out_weight.T, beta_weight.T, alpha_weight.T,
             mixer_gain[None], feed_gain[None], feed_gate, feed_up, feed_down.T,
         ),
-        [hbm] * 6 + [vmem] * 4 + [hbm] * 3, 62,
+        [smem] * 3 + [hbm, vmem, hbm] + [hbm] * 6 + [vmem] * 4 + [hbm] * 3, 61,
     )
     wm = wm.reshape(width, 8 * DK)
     ff = ff.reshape(3, nb * rows, share)
-    hg = head_gain[None]
-    normed, pre, gated, save, gains, after, nm_all, cot_all, ff_all = comm_call(
-        functools.partial(front_kernel, ns, nb, rep, heads),
-        [
-            hout(BF16, n, width), hout(F32, n + 8, 5 * DK), hout(BF16, n, DK), hout(F32, nz, SAVE_ROWS, DK),
-            vout(F32, 8, width), vout(F32, tok, width), hout(BF16, nb, tok, width), hout(BF16, nb, tok, width),
-            hout(BF16, ns, 3, nb * rows, share),
-        ],
-        [
-            block(ns), buffer(width, 8 * DK), buffer(4, 5 * key), buffer(tok, width), buffer(tok, width),
-            wide(8, 5 * DK), wide(2, SAVE_ROWS, DK), wide(2, GB, 5 * DK), buffer(2, GB, width), buffer(2, GB, DK),
-            wide(8 + GB, 5 * DK), wide(DK, DK), buffer(nz, 2, tok, width), block(nz), block(nz), block(nz),
-            dma(3), dma(nz), dma(3), dma(2, 4), dma(nz), dma(nz), dma(nz), dma(nz), dma(nb), dma(nb), dma(nb), dma(nb),
-            dma(4 * nz), dma(4 * nz),
-        ],
-        1, "front",
-        (lengths, decay_log, decay_bias, hid_all, wm, conv_taps, hg, cot, ff),
-        [smem] * 3 + [hbm] * 3 + [vmem, hbm, hbm], 61,
-    )
-    block_out, d_stream, dbr_all, gfeed, sums = comm_call(
-        functools.partial(feed_kernel, ns, nb),
-        [
-            vout(BF16, tok, width), vout(F32, tok, width), hout(BF16, ns, tok, width), vout(F32, 1, width),
-            hout(BF16, ns, 3 * share, width // ns),
-        ],
-        [
-            block(nb), block(nb), buffer(3, width, share), buffer(nb, tok, share), buffer(nb, tok, share),
-            buffer(nb, tok, share), block(nb), block(nb), block(nb), block(nb), buffer(tok, width),
-            buffer(2, ns, share, width // ns), buffer(nb, halves, share, width // ns),
-            dma(2 + ns), dma(3 + halves), dma(nb), dma(nb), dma(nb), dma(nb), dma(4 * nz), dma(4 * nz), dma(nb, halves),
-            dma(nb, halves),
-        ],
-        2, "feed", (nm_all, cot_all, ff_all, ff, after, gains), [hbm] * 4 + [vmem] * 2, 61,
-    )
+    ff_all = ff_all.reshape(ns, 3, nb * rows, share)
     nq = ns // nb
     cw = DK // rep
     wrows = width // ns
     deep = 3 * share
-    feed_buffers = [buffer(nz, deep, width // ns)] * 4
     quarter = wrows // nb
-    grad_in, q_slots, k_slots, gout_sum, small_all, feed_sum = comm_call(
-        functools.partial(back_kernel, ns, nb, rep, heads),
-        [
-            vout(BF16, tok, width), vout(BF16, nq, 2, nb, quarter, cw), vout(BF16, 2 * nq, 2, nb, quarter, cw),
-            vout(F32, DK // rep, width // nb),
-            vout(F32, ns, 8, width), vout(F32, deep, width // ns),
-        ],
-        [
-            buffer(2, 2, tok, width), buffer(width, 8 * DK), buffer(4, 5 * key), buffer(tok, width),
-            wide(2, SAVE_ROWS, DK), wide(2, 8 + GB, 5 * DK), buffer(2, GB, width), buffer(2, GB, DK), dma(3), dma(2, 5),
+    merged = nb <= 4
+    feed_scratch = [
+        block(nb), block(nb), buffer(3, width, share), buffer(nb, tok, share), buffer(nb, tok, share),
+        buffer(nb, tok, share), block(nb), block(nb), block(nb), block(nb),
+        buffer(2, ns, share, width // ns), buffer(nb, halves, share, width // ns),
+        dma(2 + ns), dma(3 + halves), dma(nb), dma(nb), dma(nb), dma(nb), dma(4 * nz), dma(4 * nz), dma(nb, halves),
+        dma(nb, halves),
+    ]
+    sums_out = hout(BF16, ns, deep, width // ns)
+    back_in = [lengths, decay_log, decay_bias, wm, conv_taps, hg, normed, pre, gated, save, hidden, gains]
+    back_specs = [smem] * 3 + [hbm] * 2 + [vmem] + [hbm] * 5 + [vmem]
+    back_outs = [
+        vout(BF16, tok, width), vout(BF16, nq, 2, nb, quarter, cw), vout(BF16, 2 * nq, 2, nb, quarter, cw),
+        vout(F32, DK // rep, width // nb), vout(F32, ns, 8, width), vout(F32, deep, width // ns),
+    ]
+    if merged:
+        back_in += [nm_all, cot_all, ff_all, ff, after]
+        back_specs += [hbm] * 4 + [vmem]
+        back_outs = [vout(BF16, tok, width), sums_out] + back_outs
+        extra = feed_scratch + [wide(tok, width), wide(1, width)]
+        assert len(extra) == FEED_SCRATCH
+    else:
+        block_out, d_stream, dbr_all, gfeed, sums = comm_call(
+            functools.partial(feed_kernel, ns, nb),
+            [
+                vout(BF16, tok, width), vout(F32, tok, width), vout(BF16, ns, tok, width), vout(F32, 1, width),
+                sums_out,
+            ],
+            feed_scratch, 2, "feed", (nm_all, cot_all, ff_all, ff, after, gains), [hbm] * 4 + [vmem] * 2, 55,
+        )
+        back_in += [dbr_all, sums, d_stream, gfeed]
+        back_specs += [hbm] * 2 + [vmem] * 2
+        extra = []
+    outs = comm_call(
+        functools.partial(back_kernel, ns, nb, rep, heads, merged),
+        back_outs,
+        extra + [
+            block(ns), buffer(width, 8 * DK), buffer(4, 5 * key), buffer(tok, width),
+            wide(2, SAVE_ROWS, DK), wide(2, 8 + GB, 5 * DK), buffer(2, GB, width), buffer(2, GB, DK), dma(4), dma(2, 4),
             wide(GB + 8, 5 * DK), wide(DK, DK), wide(8, width), wide(width, 7 * DK),
             wide(DK, width), buffer(nz, 2, tok, width), block(nz), block(nz), block(nz),
             buffer(ns, nb, quarter, 6 * DK), buffer(nb, DK // rep, width // nb), buffer(nb, ns, quarter, 6 * DK),
             buffer(3, ns, 2, quarter, cw), buffer(nb, DK // rep, width // nb), wide(nb, 8, width),
-            *feed_buffers, pltpu.SemaphoreType.REGULAR,
+            *[buffer(nz, deep, width // ns)] * 4, pltpu.SemaphoreType.REGULAR,
             dma(nz), dma(nz), dma(nz), dma(nz), dma(nb), dma(nb), dma(3, ns), dma(nq, nb), dma(2 * nq, nb),
             dma(nb), dma(nb), dma(nb), dma(nb), dma(ns), dma(ns),
             *[dma(nz)] * 7,
         ],
-        3, "back",
-        (
-            lengths, decay_log, decay_bias, dbr_all, wm, conv_taps, hg, normed, pre, gated, save, hidden,
-            sums.reshape(nz, 2, deep, width // ns), gains, d_stream, gfeed,
-        ),
-        [smem] * 3 + [hbm] * 3 + [vmem] + [hbm] * 6 + [vmem] * 3, 61,
+        3, "back", back_in, back_specs, 61,
     )
-
+    if merged:
+        block_out, _, *outs = outs
+    grad_in, q_slots, k_slots, gout_sum, small_all, feed_sum = outs
     shapes = [
         sds((tok, width), BF16), sds((tok, width), BF16), sds((1, width), F32), sds((wrows, nq * cw), F32),
         sds((wrows, 2 * nq * cw), F32), sds((wrows, 2 * nq * cw), F32), sds((2 * heads, width), F32),

time: 255 us -> 249 us (0.976)
  Pallas kernels: 254 us -> 247 us
    pallas_call x4 -> x2, Pallas kernels: 250 us -> 244 us  [comm_call(): pl.pallas_call(kernel, in_specs=specs, out_specs=[o[1] for o in outs], ou...]
where the time goes in v4:
time: 249 us
  Pallas kernels  247 us (99%)
    pallas_call x2, Pallas kernels, comm_call(): pl.pallas_call(kernel, in_specs=specs, out_specs=[o[1] for o in outs], ou...  244 us

profile of v4, /device:TPU:7, one launch (start us, length us, event | category | flops | bytes accessed | tf_op | source)
XLA Modules:
  0.0 248.6 jit_solution(17369684266425048752)
XLA Ops:
  1.3 105.2 %front.1 = (bf16[8,4,32,1024]{3,2,1,0:T(8,128)(2,1)}, bf16[3,4,32,704]{3,2,1,0:T(8,128)(2,1)}, bf16[1024,1024]{1,0:T(8,128)(2,1)}, f32[1032,640]{1,0:T(8,128)}, ...) custom-call(s32[1]{0:T(128)S(6)} %copy.37.len_ref, ...), custom_call_target="tpu_custom_call" | custom-call | tf_op jit(solution)/shard_map/front/pallas_call | solution.py:1218
  106.5 138.5 %back.1 = (bf16[128,1024]{1,0:T(8,128)(2,1)}, bf16[8,2112,128]{2,1,0:T(8,128)(2,1)}, bf16[128,1024]{1,0:T(8,128)(2,1)}, bf16[2,2,4,32,128]{4,3,2,1,0:T(8,128)(2,...) custom-call(s32[1]{0:T(128)S(6)} %copy.37.len_ref, ...), custom_call_target="tpu_custom_call" | custom-call | tf_op jit(solution)/shard_map/back/pallas_call | solution.py:1218
  245.1 3.4 %finish.1 = (bf16[128,1024]{1,0:T(8,128)(2,1)}, bf16[128,1024]{1,0:T(8,128)(2,1)}, f32[1,1024]{1,0:T(1,128)}, f32[128,256]{1,0:T(8,128)}, f32[128,512]{1,0:T(8,1...) custom-call(bf16[128,1024]{1,0:T(8,128)(2,1)} %get-tuple-element.65., ...), custom_call_target="tpu_custom_call" | custom-call | tf_op jit(solution)/shard_map/finish/pallas_call | solution.py:1357
